TPU v7x, 32 devices: a whole 2x2x4 slice. The times are simulated.
32 devices in a mesh: rep: 2 (over x), slab: 8 (over z, y), pix: 2 (over core).
Axes of the slice: x: 2, y: 2, z: 4, core: 2. Of those that a mesh axis runs over, the one named last changes fastest.
Arguments:
- projections: bfloat16 [16, 256, 512], P(('rep', 'pix'), 'slab'), may hold values from -6 to 6
- ctf_weight: bfloat16 [16, 256, 256], P(('rep', 'pix'), 'slab'), may hold values from 0.099609375 to 4
- orient: int32 [16], P(('rep', 'pix')), may hold values from 0 to 63
- angle_table: int32 [64, 4, 256], replicated, may hold values from 0 to 255, as said below
Outputs:
- density: float32 [256, 256, 512], P(('rep', 'pix'), 'slab')
Inputs may be any that keep to these rules, and one draw needn't show every extreme that they name: `angle_table`: for every entry and column, the lower indices lie between 3 and 253, and the fractions between 0 and 255.
All inputs are finite; a program needn't handle non-finite values.
Results may differ from a plain program's by a relative error of at most 0.0022.
Values may be sent and summed in bfloat16 or wider, within the bound.
No kernel may reach another device: no remote copies, remote signals or barrier semaphores. Data moves between devices by JAX's collectives and lax.ppermute only.
A program may use at most 128 MiB of HBM per device.

v0:
```python
import jax
import jax.numpy as jnp
import numpy as np
from jax import lax
from jax.experimental import pallas as pl
from jax.experimental.pallas import tpu as pltpu
from jax.sharding import PartitionSpec as P


BATCH_AXES = ("rep", "pix")
GROUP = 16
TILE = 256
LANES = 128


class Ports:
    def __init__(self, mesh):
        self.rep, self.slab, self.pix = (mesh.shape[a] for a in ("rep", "slab", "pix"))
        self.ids = np.arange(self.rep * self.slab * self.pix).reshape(self.rep, self.slab, self.pix)

    def fits(self):
        return (self.rep, self.slab, self.pix) == (2, 8, 2)

    def target(self, port, rep, slab, pix):
        if port == "x|y":
            port = "y" if pix else "x"
        if port in ("x", "xy"):
            rep = 1 - rep
        if port in ("y", "xy"):
            slab = slab ^ 1
        if port == "z":
            slab = (slab + 2) % self.slab
        if port == "back":
            slab = (slab - 2) % self.slab
        if port == "core":
            pix = 1 - pix
        return self.ids[rep, slab, pix]

    def pairs(self, port):
        return [(int(self.ids[at]), int(self.target(port, *at))) for at in np.ndindex(self.ids.shape)]

    def move(self, owner, port):
        moved = np.empty_like(owner)
        for source, target in self.pairs(port):
            moved.flat[target] = owner.flat[source]
        return moved

    def send(self, held, port):
        value, owners = held
        value = lax.ppermute(value, ("rep", "slab", "pix"), self.pairs(port))
        return value, [self.move(owner, port) for owner in owners]

    def both(self, held):
        other = self.send(held, "core")
        return other, (jnp.concatenate([held[0], other[0]], axis=0), held[1] + other[1])


def gather_pieces(samples, orient, ports):
    own = (samples, [ports.ids])
    core_own, chip_own = ports.both(own)
    up1 = ports.send(own, "z")
    side0 = ports.send(chip_own, "x|y")
    down = ports.send(own, "back")
    across = ports.send(own, "xy")
    orient = (orient, [ports.ids])
    orient_x = ports.send(orient, "x")
    core_up1, chip_up1 = ports.both(up1)
    up2 = ports.send(up1, "z")
    side1 = ports.send(chip_up1, "x|y")
    orient = (jnp.concatenate([orient[0], orient_x[0]]), orient[1] + orient_x[1])
    orient_core = ports.send(orient, "core")
    orient = (jnp.concatenate([orient[0], orient_core[0]]), orient[1] + orient_core[1])
    core_down, chip_down = ports.both(down)
    across1 = ports.send(across, "z")
    side3 = ports.send(chip_down, "x|y")
    across3 = ports.send(across, "back")
    core_up2, chip_up2 = ports.both(up2)
    side2 = ports.send(chip_up2, "x|y")
    across2 = ports.send(across1, "z")
    pieces = [own, core_own, up1, core_up1, up2, core_up2, down, core_down]
    late = (across, side0, side1, across1, side3, across3, side2, across2)
    for held in late:
        pieces += [held, ports.send(held, "core")]
    owners = np.stack([owner for _, owned in pieces for owner in owned], axis=-1)
    assert (np.sort(owners, -1) == np.arange(ports.ids.size)).all()
    return [value for value, _ in pieces], owners, orient[0], np.stack(orient[1], axis=-1)


def lookup(orient, angle_table):
    choose = (orient[:, None] == lax.iota(jnp.int32, angle_table.shape[0])[None, :]).astype(jnp.int32)
    return jnp.sum(choose[:, :, None, None] * angle_table[None], axis=1)


def corner(indices, lower, fraction):
    return jnp.where(indices == lower, 1.0 - fraction, 0.0) + jnp.where(indices == lower + 1, fraction, 0.0)


def shift_of(size):
    assert size & (size - 1) == 0
    return size.bit_length() - 1


def make_plan(orient, place, table, pieces_n, sizes):
    batch, planes, columns, count_x, row_block, batches = sizes
    items = batch * planes // GROUP
    segments = pieces_n * items
    steps, lane_groups = count_x // row_block, LANES // GROUP
    bits_at = 2 * segments
    info_size = segments + segments * GROUP // TILE + 1
    total_n = batch * batches

    def kernel(orient_ref, place_ref, table_ref, info_ref, where_ref, raw, geometry, found, found_s, listed, sems):
        me = (lax.axis_index("rep") * lax.axis_size("slab") + lax.axis_index("slab")) * lax.axis_size("pix")
        me += lax.axis_index("pix")
        rep, pix = lax.axis_index("rep"), lax.axis_index("pix")
        first_x = (rep * lax.axis_size("pix") + pix) * count_x
        first_z = lax.axis_index("slab") * planes
        copies = [
            pltpu.make_async_copy(table_ref.at[orient_ref[n]], raw.at[place_ref[me, n]], sems.at[n])
            for n in range(total_n)
        ]
        for copy in copies:
            copy.start()
        for copy in copies:
            copy.wait()
        unit = lax.broadcasted_iota(jnp.int32, (1, 4, columns), 1) & 1
        geometry[:, 0:4, :] = raw[...].astype(jnp.float32) * jnp.where(unit == 1, 1.0 / 256.0, 1.0)
        near_x = geometry[:, 0, :] - first_x.astype(jnp.float32)
        near_z = geometry[:, 2, :] - first_z.astype(jnp.float32)
        hit_z = (near_z >= -1.0) & (near_z < planes)
        hits = [
            jnp.where(hit_z & (near_x >= s * row_block - 1.0) & (near_x < (s + 1) * row_block), 1.0, 0.0)
            for s in range(steps)
        ]
        hits = jnp.concatenate(hits, axis=0).astype(jnp.bfloat16)
        lane = lax.broadcasted_iota(jnp.int32, (columns, LANES), 0)
        group = lax.broadcasted_iota(jnp.int32, (columns, LANES), 1)
        member = (lane // GROUP == group).astype(jnp.bfloat16)
        counted = jnp.dot(hits, member, preferred_element_type=jnp.float32)
        bits = jnp.zeros((total_n, LANES), jnp.float32)
        for s in range(steps):
            bits += jnp.where(counted[s * total_n : (s + 1) * total_n] > 0.0, float(2**s), 0.0)
        any_hit = jnp.where(bits > 0.0, 1.0, 0.0).astype(jnp.bfloat16)
        row = lax.broadcasted_iota(jnp.int32, (total_n, total_n), 0)
        col = lax.broadcasted_iota(jnp.int32, (total_n, total_n), 1)
        above = jnp.dot((col < row).astype(jnp.bfloat16), any_hit, preferred_element_type=jnp.float32)
        whole = jnp.dot(jnp.ones((total_n, total_n), jnp.bfloat16), any_hit, preferred_element_type=jnp.float32)
        row = lax.broadcasted_iota(jnp.int32, (LANES, LANES), 0)
        col = lax.broadcasted_iota(jnp.int32, (LANES, LANES), 1)
        before = jnp.dot(
            whole.astype(jnp.bfloat16), (row < col).astype(jnp.bfloat16), preferred_element_type=jnp.float32
        )
        code = jnp.where(bits > 0.0, bits * bits_at + above + before, 0.0)
        found[...] = code.astype(jnp.int32)
        to_scalar = pltpu.make_async_copy(found, found_s, sems.at[0])
        to_scalar.start()
        to_scalar.wait()

        for tile in range(segments, info_size):
            info_ref[tile] = 0

        count = jnp.int32(0)
        for piece in range(pieces_n):
            first_n = place_ref[me, total_n + 2 * piece]
            first_g = place_ref[me, total_n + 2 * piece + 1]
            for item in range(items):
                n, g = first_n + item // (items // batch), first_g + item % (items // batch)
                code = found_s[n, g]
                hit = code > 0
                listed[jnp.where(hit, code & (bits_at - 1), segments)] = n * LANES + g
                info_ref[piece * items + item] = jnp.where(hit, code & (bits_at - 1), segments)
                count += hit.astype(jnp.int32)
        info_ref[info_size - 1] = count
        tiles = (count + TILE // GROUP - 1) >> shift_of(TILE // GROUP)
        lane_group = lax.broadcasted_iota(jnp.int32, (8, LANES), 1) >> shift_of(GROUP)

        def order(block, carry):
            gathered = jnp.full((8, LANES), -4.0, jnp.float32)
            tile_bits = jnp.int32(0)
            for slot in range(lane_groups):
                index = block * lane_groups + slot
                valid = index < count
                name = listed[jnp.minimum(index, count - 1)]
                n, g = name >> shift_of(LANES), name & (LANES - 1)
                tile_bits |= found_s[n, g] >> shift_of(bits_at)
                lanes = pl.ds(pl.multiple_of((g >> shift_of(lane_groups)) * LANES, LANES), LANES)
                shift = ((slot - g) & (lane_groups - 1)) * GROUP
                rolled = pltpu.roll(geometry[n, :, lanes], shift, 1)
                gathered = jnp.where((lane_group == slot) & valid, rolled, gathered)
            where_ref[:, pl.ds(pl.multiple_of(block * LANES, LANES), LANES)] = gathered
            tile = segments + (block >> shift_of(TILE // LANES))
            info_ref[tile] = info_ref[tile] | tile_bits
            return carry

        lax.fori_loop(0, tiles * (TILE // LANES), order, 0)

    smem, vmem = pl.BlockSpec(memory_space=pltpu.SMEM), pl.BlockSpec(memory_space=pltpu.VMEM)
    return pl.pallas_call(
        kernel,
        out_shape=[
            jax.ShapeDtypeStruct((info_size,), jnp.int32),
            jax.ShapeDtypeStruct((8, segments * GROUP), jnp.float32),
        ],
        in_specs=[smem, smem, pl.BlockSpec(memory_space=pl.ANY)],
        out_specs=[smem, vmem],
        scratch_shapes=[
            pltpu.VMEM((total_n, 4, columns), jnp.int32),
            pltpu.VMEM((total_n, 8, columns), jnp.float32),
            pltpu.VMEM((total_n, LANES), jnp.int32),
            pltpu.SMEM((total_n, LANES), jnp.int32),
            pltpu.SMEM((segments + 1,), jnp.int32),
            pltpu.SemaphoreType.DMA((total_n,)),
        ],
        compiler_params=pltpu.CompilerParams(vmem_limit_bytes=4 << 20),
        name="plan",
    )(orient, place, table)


def spread(pieces, info, where, sizes):
    batch, planes, columns, count_x, row_block, _ = sizes
    pieces_n = len(pieces)
    segments = sum(piece.shape[0] for piece in pieces) // GROUP
    steps = count_x // row_block
    channels = 3 * columns

    def kernel(*refs):
        info_ref, where_ref = refs[:2]
        piece_refs = refs[2 : 2 + pieces_n]
        out_ref = refs[2 + pieces_n]
        compact, total, staged, sems = refs[3 + pieces_n :]
        first_x = (lax.axis_index("rep") * lax.axis_size("pix") + lax.axis_index("pix")) * count_x
        first_z = lax.axis_index("slab") * planes
        count = info_ref[segments + segments * GROUP // TILE]
        tiles = (count + TILE // GROUP - 1) >> shift_of(TILE // GROUP)

        first = 0
        for piece in piece_refs:
            items = batch * planes // GROUP
            for start in range(0, piece.shape[0] // GROUP, items):
                targets = [info_ref[first + item] for item in range(items)]
                least = targets[0]
                for target in targets[1:]:
                    least = jnp.minimum(least, target)

                @pl.when(least < segments)
                def _(targets=targets, piece=piece, start=start):
                    for item, target in enumerate(targets):
                        rows = pl.ds(pl.multiple_of(target * GROUP, GROUP), GROUP)
                        source = (start + item) * GROUP
                        compact[rows, :] = piece[source : source + GROUP, :]

                first += items

        def clear(item, carry):
            target = pl.ds(pl.multiple_of(item * GROUP, GROUP), GROUP)
            compact[target, :] = jnp.zeros((GROUP, channels), jnp.bfloat16)
            return carry

        lax.fori_loop(count, tiles * (TILE // GROUP), clear, 0)

        def out_copy(step, slot):
            rows = pl.ds(step * row_block, row_block)
            return pltpu.make_async_copy(staged.at[slot], out_ref.at[rows], sems.at[slot])

        for step in range(steps):
            slot = step % 2

            def product(tile, step=step):
                lanes = pl.ds(pl.multiple_of(tile * TILE, TILE), TILE)
                lower_x, part_x = where_ref[0:1, lanes], where_ref[1:2, lanes]
                lower_z, part_z = where_ref[2:3, lanes], where_ref[3:4, lanes]
                at_x = first_x + step * row_block + lax.broadcasted_iota(jnp.int32, (row_block, TILE), 0)
                at_z = first_z + lax.broadcasted_iota(jnp.int32, (planes, TILE), 0)
                weight_x = corner(at_x.astype(jnp.float32), lower_x, part_x)
                weight_z = corner(at_z.astype(jnp.float32), lower_z, part_z)
                matrix = (weight_x[:, None, :] * weight_z[None, :, :]).astype(jnp.bfloat16)
                matrix = matrix.reshape(row_block * planes, TILE)
                return jnp.dot(matrix, compact[lanes, :], preferred_element_type=jnp.float32)

            def add(tile, seen, step=step, product=product):
                hit = (info_ref[segments + tile] >> step) & 1

                @pl.when((hit > 0) & (seen == 0))
                def _():
                    total[...] = product(tile)

                @pl.when((hit > 0) & (seen > 0))
                def _():
                    total[...] += product(tile)

                return seen + hit

            seen = lax.fori_loop(0, tiles, add, jnp.int32(0))
            if step >= 2:
                out_copy(step - 2, slot).wait()
            shape = (row_block, planes, columns)

            @pl.when(seen > 0)
            def _(slot=slot):
                scale = 1.0 / (total[:, 2 * columns :] + 1.0)
                staged[slot, :, :, :columns] = (total[:, :columns] * scale).reshape(shape)
                staged[slot, :, :, columns:] = (total[:, columns : 2 * columns] * scale).reshape(shape)

            @pl.when(seen == 0)
            def _(slot=slot):
                staged[slot] = jnp.zeros((row_block, planes, 2 * columns), jnp.float32)

            out_copy(step, slot).start()
        for step in range(max(steps - 2, 0), steps):
            out_copy(step, step % 2).wait()

    smem, vmem = pl.BlockSpec(memory_space=pltpu.SMEM), pl.BlockSpec(memory_space=pltpu.VMEM)
    return pl.pallas_call(
        kernel,
        out_shape=jax.ShapeDtypeStruct((count_x, planes, 2 * columns), jnp.float32),
        in_specs=[smem, vmem] + [vmem] * pieces_n,
        out_specs=pl.BlockSpec(memory_space=pl.ANY),
        scratch_shapes=[
            pltpu.VMEM((segments * GROUP + GROUP, channels), jnp.bfloat16),
            pltpu.VMEM((row_block * planes, channels), jnp.float32),
            pltpu.VMEM((2, row_block, planes, 2 * columns), jnp.float32),
            pltpu.SemaphoreType.DMA((2,)),
        ],
        compiler_params=pltpu.CompilerParams(vmem_limit_bytes=14 << 20),
        name="spread",
    )(info, where, *pieces)


def make_body(ports):
    def body(projections, ctf_weight, orient, angle_table):
        batch, planes = projections.shape[:2]
        columns = projections.shape[2] // 2
        count_x = columns // (ports.rep * ports.pix)
        row_block = TILE // planes
        sizes = (batch, planes, columns, count_x, row_block, ports.rep * ports.pix)
        samples = jnp.concatenate([projections, ctf_weight], axis=2).reshape(batch * planes, 3 * columns)
        pieces, owners, orient, orient_owners = gather_pieces(samples, orient, ports)
        place = []
        for owner in (orient_owners, owners):
            rep, slab, pix = np.unravel_index(owner, ports.ids.shape)
            place.append(((rep * ports.pix + pix) * batch, slab * (planes // GROUP)))
        (order, _), (first_n, first_g) = place
        order = order[..., None] + np.arange(batch)
        place = [order.reshape(ports.ids.size, -1), np.stack([first_n, first_g], -1).reshape(ports.ids.size, -1)]
        place = jnp.asarray(np.concatenate(place, axis=1), jnp.int32)
        info, where = make_plan(orient, place, angle_table, owners.shape[-1], sizes)
        return spread(pieces, info, where, sizes)

    return body


def plain_body(projections, ctf_weight, orient, angle_table):
    planes = projections.shape[1]
    columns = projections.shape[2] // 2
    owned_rows = columns // (lax.axis_size("rep") * lax.axis_size("pix"))
    first_z = lax.axis_index("slab") * planes
    first_x = (lax.axis_index("rep") * lax.axis_size("pix") + lax.axis_index("pix")) * owned_rows
    samples = jnp.concatenate([projections, ctf_weight], axis=2)
    samples = lax.all_gather(samples, "slab", axis=1, tiled=True)
    samples = lax.all_gather(samples, BATCH_AXES, axis=0, tiled=True)
    geometry = lookup(lax.all_gather(orient, BATCH_AXES, axis=0, tiled=True), angle_table)
    geometry = geometry.astype(jnp.float32)
    at_x = (first_x + lax.iota(jnp.int32, owned_rows)).astype(jnp.float32)[:, None, None]
    at_z = (first_z + lax.iota(jnp.int32, planes)).astype(jnp.float32)[:, None, None]
    weight_x = corner(at_x, geometry[None, :, 0], geometry[None, :, 1] / 256.0)
    weight_z = corner(at_z, geometry[None, :, 2], geometry[None, :, 3] / 256.0)
    matrix = (weight_x[:, None] * weight_z[None]).astype(jnp.bfloat16).reshape(owned_rows * planes, -1)
    volume = jnp.dot(matrix, samples.reshape(-1, 3 * columns), preferred_element_type=jnp.float32)
    values = volume[:, : 2 * columns].reshape(-1, 2, columns) / (volume[:, None, 2 * columns :] + 1.0)
    return values.reshape(owned_rows, planes, 2 * columns)


def solution(mesh):
    placed = (
        P(BATCH_AXES, "slab", None),
        P(BATCH_AXES, "slab", None),
        P(BATCH_AXES),
        P(),
    )
    ports = Ports(mesh)

    def shard(body):
        return jax.shard_map(
            body, mesh=mesh, in_specs=placed, out_specs=P(BATCH_AXES, "slab", None), check_vma=False
        )

    if not ports.fits():
        return shard(plain_body)
    return shard(make_body(ports))
```

profile of v0, /device:TPU:18, one launch (start us, length us, event | category | flops | bytes accessed | tf_op | source)
XLA Modules:
  0.0 57.7 jit_solution(5957760416137527421)
XLA Ops:
  0.0 1.0 %pad_maximum_fusion.4 = bf16[4,32,768]{2,1,0:T(8,128)(2,1)S(1)} fusion(bf16[4,32,256]{2,1,0:T(8,128)(2,1)} %param.6, bf16[4,32,512]{2,1,0:T(8,128)(2,1)} %param.5), kind=kLoop, calls=%fused_computation.4 | loop fusion | flops 393216 | bytes 393216 | tf_op jit(solution)/shard_map/concatenate | solution.py:336
  1.0 1.6 %collective-permute-start.3 = (bf16[128,768]{1,0:T(8,128)(2,1)S(1)}, bf16[128,768]{1,0:T(8,128)(2,1)S(1)}, u32[]{:S(2)}, u32[]{:S(2)}) collective-permute-start(bf16[128,768]{1,0:T(8,128)(2,1)S(1)} %bitcast.1), channel_id=1, source_target_pairs={{0,4},{1,5},{2,6},{3,7},{4,8},{5,9},{6,10},{7,11},{8,12},{9,13},{1... | collective-permute-start | bytes 589832 | tf_op jit(solution)/shard_map/ppermute | solution.py:50
  2.6 1.5 %collective-permute-start.9 = (bf16[128,768]{1,0:T(8,128)(2,1)S(1)}, bf16[128,768]{1,0:T(8,128)(2,1)S(1)}, u32[]{:S(2)}, u32[]{:S(2)}) collective-permute-start(bf16[128,768]{1,0:T(8,128)(2,1)S(1)} %bitcast.2), channel_id=1, source_target_pairs={{0,18},{1,19},{2,16},{3,17},{4,22},{5,23},{6,20},{7,21},{8,26},{9,... | collective-permute-start | bytes 589832 | tf_op jit(solution)/shard_map/ppermute | solution.py:50
  4.1 0.4 collective-permute-start.7
  4.5 0.0 collective-permute-start.2
  4.5 1.5 %collective-permute-start = (s32[4]{0:T(128)}, s32[4]{0:T(128)S(1)}, u32[]{:S(2)}, u32[]{:S(2)}) collective-permute-start(s32[4]{0:T(128)} %param.7), channel_id=1, source_target_pairs={{0,16},{1,17},{2,18},{3,19},{4,20},{5,21},{6,22},{7,23},{8,24},{9,... | collective-permute-start | bytes 56 | tf_op jit(solution)/shard_map/ppermute | solution.py:50
  6.0 5.0 %collective-permute-done.3.refs_4_ = bf16[128,768]{1,0:T(8,128)(2,1)S(1)} collective-permute-done((bf16[128,768]{1,0:T(8,128)(2,1)S(1)}, bf16[128,768]{1,0:T(8,128)(2,1)S(1)}, u32[]{:S(2)}, u32[]{:S(2)}) %collective-permute-start.3) | collective-permute-done | bytes 196640 | tf_op jit(solution)/shard_map/ppermute | solution.py:50
  11.1 1.9 %collective-permute-start.5 = (bf16[128,768]{1,0:T(8,128)(2,1)S(1)}, bf16[128,768]{1,0:T(8,128)(2,1)S(1)}, u32[]{:S(2)}, u32[]{:S(2)}) collective-permute-start(bf16[128,768]{1,0:T(8,128)(2,1)S(1)} %collective-permute-done.3.refs_4_), channel_id=1, source_target_pairs={{0,4},{1,5},{2,6},{3,7},{4,8},{5,9},{6,10},{7,11},{8,12},{9,13},{1... | collective-permute-start | bytes 589832 | tf_op jit(solution)/shard_map/ppermute | solution.py:50
  13.0 0.7 %pad_add_fusion = s32[8]{0:T(128)S(1)} fusion(s32[4]{0:T(128)S(1)} %collective-permute-done, s32[4]{0:T(128)} %param.7), kind=kLoop, calls=%fused_computation.5 | loop fusion | flops 8 | bytes 64 | tf_op jit(solution)/shard_map/concatenate | solution.py:70
  13.7 0.0 collective-permute-done.9.refs_10_
  13.7 0.5 collective-permute-start.1
  14.2 0.1 collective-permute-start.19
  14.3 0.0 collective-permute-start.8
  14.4 2.3 %collective-permute-done.5.refs_6_ = bf16[128,768]{1,0:T(8,128)(2,1)S(1)} collective-permute-done((bf16[128,768]{1,0:T(8,128)(2,1)S(1)}, bf16[128,768]{1,0:T(8,128)(2,1)S(1)}, u32[]{:S(2)}, u32[]{:S(2)}) %collective-permute-start.5) | collective-permute-done | bytes 196640 | tf_op jit(solution)/shard_map/ppermute | solution.py:50
  16.7 1.9 %collective-permute-start.15 = (bf16[128,768]{1,0:T(8,128)(2,1)S(1)}, bf16[128,768]{1,0:T(8,128)(2,1)S(1)}, u32[]{:S(2)}, u32[]{:S(2)}) collective-permute-start(bf16[128,768]{1,0:T(8,128)(2,1)S(1)} %collective-permute-done.9.refs_10_), channel_id=1, source_target_pairs={{0,4},{1,5},{2,6},{3,7},{4,8},{5,9},{6,10},{7,11},{8,12},{9,13},{1... | collective-permute-start | bytes 589832 | tf_op jit(solution)/shard_map/ppermute | solution.py:50
  18.7 0.6 collective-permute-start.10
  19.3 2.7 %collective-permute-done.19.refs_20_ = bf16[128,768]{1,0:T(8,128)(2,1)S(1)} collective-permute-done((bf16[128,768]{1,0:T(8,128)(2,1)S(1)}, bf16[128,768]{1,0:T(8,128)(2,1)S(1)}, u32[]{:S(2)}, u32[]{:S(2)}) %collective-permute-start.19) | collective-permute-done | bytes 196640 | tf_op jit(solution)/shard_map/ppermute | solution.py:50
  22.1 2.1 %collective-permute-start.17 = (bf16[256,768]{1,0:T(8,128)(2,1)S(1)}, bf16[256,768]{1,0:T(8,128)(2,1)S(1)}, u32[]{:S(2)}, u32[]{:S(2)}) collective-permute-start(bf16[256,768]{1,0:T(8,128)(2,1)S(1)} %pad_maximum_fusion.2), channel_id=1, source_target_pairs={{0,16},{1,3},{2,18},{3,1},{4,20},{5,7},{6,22},{7,5},{8,24},{9,11},... | collective-permute-start | bytes 1179656 | tf_op jit(solution)/shard_map/ppermute | solution.py:50
  24.1 1.5 %collective-permute-done.15.refs_16_ = bf16[128,768]{1,0:T(8,128)(2,1)S(1)} collective-permute-done((bf16[128,768]{1,0:T(8,128)(2,1)S(1)}, bf16[128,768]{1,0:T(8,128)(2,1)S(1)}, u32[]{:S(2)}, u32[]{:S(2)}) %collective-permute-start.15) | collective-permute-done | bytes 196640 | tf_op jit(solution)/shard_map/ppermute | solution.py:50
  25.7 2.0 %collective-permute-start.21 = (bf16[256,768]{1,0:T(8,128)(2,1)S(1)}, bf16[256,768]{1,0:T(8,128)(2,1)S(1)}, u32[]{:S(2)}, u32[]{:S(2)}) collective-permute-start(bf16[256,768]{1,0:T(8,128)(2,1)S(1)} %pad_maximum_fusion.3), channel_id=1, source_target_pairs={{0,16},{1,3},{2,18},{3,1},{4,20},{5,7},{6,22},{7,5},{8,24},{9,11},... | collective-permute-start | bytes 1179656 | tf_op jit(solution)/shard_map/ppermute | solution.py:50
  27.7 1.5 %collective-permute-start.23 = (bf16[128,768]{1,0:T(8,128)(2,1)S(1)}, bf16[128,768]{1,0:T(8,128)(2,1)S(1)}, u32[]{:S(2)}, u32[]{:S(2)}) collective-permute-start(bf16[128,768]{1,0:T(8,128)(2,1)S(1)} %collective-permute-done.15.refs_16_), channel_id=1, source_target_pairs={{0,4},{1,5},{2,6},{3,7},{4,8},{5,9},{6,10},{7,11},{8,12},{9,13},{1... | collective-permute-start | bytes 589832 | tf_op jit(solution)/shard_map/ppermute | solution.py:50
  29.2 4.8 %collective-permute-done.23.refs_24_ = bf16[128,768]{1,0:T(8,128)(2,1)S(1)} collective-permute-done((bf16[128,768]{1,0:T(8,128)(2,1)S(1)}, bf16[128,768]{1,0:T(8,128)(2,1)S(1)}, u32[]{:S(2)}, u32[]{:S(2)}) %collective-permute-start.23) | collective-permute-done | bytes 196640 | tf_op jit(solution)/shard_map/ppermute | solution.py:50
  34.0 0.5 collective-permute-start.12
  34.5 0.1 collective-permute-start.18
  34.5 3.7 %collective-permute-done.13.refs_14_ = bf16[256,768]{1,0:T(8,128)(2,1)S(1)} collective-permute-done((bf16[256,768]{1,0:T(8,128)(2,1)S(1)}, bf16[256,768]{1,0:T(8,128)(2,1)S(1)}, u32[]{:S(2)}, u32[]{:S(2)}) %collective-permute-start.13) | collective-permute-done | bytes 393248 | tf_op jit(solution)/shard_map/ppermute | solution.py:50
  38.2 4.2 %collective-permute-done.21.refs_22_ = bf16[256,768]{1,0:T(8,128)(2,1)S(1)} collective-permute-done((bf16[256,768]{1,0:T(8,128)(2,1)S(1)}, bf16[256,768]{1,0:T(8,128)(2,1)S(1)}, u32[]{:S(2)}, u32[]{:S(2)}) %collective-permute-start.21) | collective-permute-done | bytes 393248 | tf_op jit(solution)/shard_map/ppermute | solution.py:50
  42.4 0.5 collective-permute-start.24
  42.9 0.7 %pad_add_fusion.1.orient_ref = s32[16]{0:T(128)S(1)} fusion(s32[8]{0:T(128)S(1)} %collective-permute-done.1, s32[4]{0:T(128)S(1)} %collective-permute-done, s32[4]{0:T(128)} %param.7), kind=kLoop, calls=%fused_computation.6 | loop fusion | flops 32 | bytes 128 | tf_op jit(solution)/shard_map/concatenate | solution.py:72
  43.7 0.9 %copy-done = s32[64,4,256]{2,1,0:T(4,128)S(1)} copy-done((s32[64,4,256]{2,1,0:T(4,128)S(1)}, s32[64,4,256]{2,1,0:T(4,128)}, u32[]{:S(2)}) %copy-start) | copy-done | bytes 262168
  44.6 0.7 %copy-done.1 = s32[32,80]{1,0:T(8,128)S(1)} copy-done((s32[32,80]{1,0:T(8,128)S(1)}, s32[32,80]{1,0:T(8,128)}, u32[]{:S(2)}) %copy-start.1) | copy-done | bytes 10264
  45.3 4.9 %plan.1 = (s32[273]{0:T(512)S(1)}, f32[8,4096]{1,0:T(8,128)S(1)}) custom-call(s32[16]{0:T(128)S(1)} %pad_add_fusion.1.orient_ref, s32[32,80]{1,0:T(8,128)S(1)} %copy-done.1, s32[64,4,256]{2,1,0:T(4,128)S(1)} %copy-done), custom_call_target="tpu_custom_call" | custom-call | tf_op jit(solution)/shard_map/plan/pallas_call | solution.py:198
  50.3 7.4 %spread.1 = f32[64,32,512]{2,1,0:T(8,128)} custom-call(s32[273]{0:T(512)S(1)} %get-tuple-element.7.refs_0_, f32[8,4096]{1,0:T(8,128)S(1)} %get-tuple-element.8.refs_1_, bf16[128,768]{1,0:T(8,128)(2,1)S(1)} %bitcast.6, bf16[128,768]{1,0:T(8,128)(2,1)S(1)} %collective-permute-done.2.refs_3_, bf16[128,768]{1,0:T(8,128)(2,1)S(1)} %collective-permute-done.3.refs_4_, ...), custom_call_target="tpu_custom_call" | custom-call | tf_op jit(solution)/shard_map/spread/pallas_call | solution.py:313
  (31 shorter events, 0.2 us)
Async XLA Ops:
  1.0 10.1 %collective-permute-start.3 = (bf16[128,768]{1,0:T(8,128)(2,1)S(1)}, bf16[128,768]{1,0:T(8,128)(2,1)S(1)}, u32[]{:S(2)}, u32[]{:S(2)}) collective-permute-start(bf16[128,768]{1,0:T(8,128)(2,1)S(1)} %bitcast.1), channel_id=1, source_target_pairs={{0,4},{1,5},{2,6},{3,7},{4,8},{5,9},{6,10},{7,11},{8,12},{9,13},{1... | collective-permute-start | bytes 589832 | tf_op jit(solution)/shard_map/ppermute | solution.py:50
  2.6 11.1 %collective-permute-start.9 = (bf16[128,768]{1,0:T(8,128)(2,1)S(1)}, bf16[128,768]{1,0:T(8,128)(2,1)S(1)}, u32[]{:S(2)}, u32[]{:S(2)}) collective-permute-start(bf16[128,768]{1,0:T(8,128)(2,1)S(1)} %bitcast.2), channel_id=1, source_target_pairs={{0,18},{1,19},{2,16},{3,17},{4,22},{5,23},{6,20},{7,21},{8,26},{9,... | collective-permute-start | bytes 589832 | tf_op jit(solution)/shard_map/ppermute | solution.py:50
  4.1 10.1 %collective-permute-start.7 = (bf16[128,768]{1,0:T(8,128)(2,1)S(1)}, bf16[128,768]{1,0:T(8,128)(2,1)S(1)}, u32[]{:S(2)}, u32[]{:S(2)}) collective-permute-start(bf16[128,768]{1,0:T(8,128)(2,1)S(1)} %bitcast.3), channel_id=1, source_target_pairs={{0,12},{1,13},{2,14},{3,15},{4,0},{5,1},{6,2},{7,3},{8,4},{9,5},{1... | collective-permute-start | bytes 589832 | tf_op jit(solution)/shard_map/ppermute | solution.py:50
  4.5 9.8 %collective-permute-start.2 = (bf16[128,768]{1,0:T(8,128)(2,1)S(1)}, bf16[128,768]{1,0:T(8,128)(2,1)S(1)}, u32[]{:S(2)}, u32[]{:S(2)}) collective-permute-start(bf16[128,768]{1,0:T(8,128)(2,1)S(1)} %bitcast.4), channel_id=1, source_target_pairs={{0,1},{1,0},{2,3},{3,2},{4,5},{5,4},{6,7},{7,6},{8,9},{9,8},{10,11... | collective-permute-start | bytes 589832 | tf_op jit(solution)/shard_map/ppermute | solution.py:50
  4.5 8.4 %collective-permute-start = (s32[4]{0:T(128)}, s32[4]{0:T(128)S(1)}, u32[]{:S(2)}, u32[]{:S(2)}) collective-permute-start(s32[4]{0:T(128)} %param.7), channel_id=1, source_target_pairs={{0,16},{1,17},{2,18},{3,19},{4,20},{5,21},{6,22},{7,23},{8,24},{9,... | collective-permute-start | bytes 56 | tf_op jit(solution)/shard_map/ppermute | solution.py:50
  11.1 5.7 %collective-permute-start.5 = (bf16[128,768]{1,0:T(8,128)(2,1)S(1)}, bf16[128,768]{1,0:T(8,128)(2,1)S(1)}, u32[]{:S(2)}, u32[]{:S(2)}) collective-permute-start(bf16[128,768]{1,0:T(8,128)(2,1)S(1)} %collective-permute-done.3.refs_4_), channel_id=1, source_target_pairs={{0,4},{1,5},{2,6},{3,7},{4,8},{5,9},{6,10},{7,11},{8,12},{9,13},{1... | collective-permute-start | bytes 589832 | tf_op jit(solution)/shard_map/ppermute | solution.py:50
  13.0 5.7 %collective-permute-start.4 = (bf16[128,768]{1,0:T(8,128)(2,1)S(1)}, bf16[128,768]{1,0:T(8,128)(2,1)S(1)}, u32[]{:S(2)}, u32[]{:S(2)}) collective-permute-start(bf16[128,768]{1,0:T(8,128)(2,1)S(1)} %collective-permute-done.3.refs_4_), channel_id=1, source_target_pairs={{0,1},{1,0},{2,3},{3,2},{4,5},{5,4},{6,7},{7,6},{8,9},{9,8},{10,11... | collective-permute-start | bytes 589832 | tf_op jit(solution)/shard_map/ppermute | solution.py:50
  13.7 8.3 %collective-permute-start.1 = (s32[8]{0:T(128)S(1)}, s32[8]{0:T(128)S(1)}, u32[]{:S(2)}, u32[]{:S(2)}) collective-permute-start(s32[8]{0:T(128)S(1)} %pad_add_fusion), channel_id=1, source_target_pairs={{0,1},{1,0},{2,3},{3,2},{4,5},{5,4},{6,7},{7,6},{8,9},{9,8},{10,11... | collective-permute-start | bytes 104 | tf_op jit(solution)/shard_map/ppermute | solution.py:50
  14.2 7.8 %collective-permute-start.19 = (bf16[128,768]{1,0:T(8,128)(2,1)S(1)}, bf16[128,768]{1,0:T(8,128)(2,1)S(1)}, u32[]{:S(2)}, u32[]{:S(2)}) collective-permute-start(bf16[128,768]{1,0:T(8,128)(2,1)S(1)} %collective-permute-done.9.refs_10_), channel_id=1, source_target_pairs={{0,12},{1,13},{2,14},{3,15},{4,0},{5,1},{6,2},{7,3},{8,4},{9,5},{1... | collective-permute-start | bytes 589832 | tf_op jit(solution)/shard_map/ppermute | solution.py:50
  14.3 4.3 %collective-permute-start.8 = (bf16[128,768]{1,0:T(8,128)(2,1)S(1)}, bf16[128,768]{1,0:T(8,128)(2,1)S(1)}, u32[]{:S(2)}, u32[]{:S(2)}) collective-permute-start(bf16[128,768]{1,0:T(8,128)(2,1)S(1)} %collective-permute-done.7.refs_8_), channel_id=1, source_target_pairs={{0,1},{1,0},{2,3},{3,2},{4,5},{5,4},{6,7},{7,6},{8,9},{9,8},{10,11... | collective-permute-start | bytes 589832 | tf_op jit(solution)/shard_map/ppermute | solution.py:50
  16.7 8.9 %collective-permute-start.15 = (bf16[128,768]{1,0:T(8,128)(2,1)S(1)}, bf16[128,768]{1,0:T(8,128)(2,1)S(1)}, u32[]{:S(2)}, u32[]{:S(2)}) collective-permute-start(bf16[128,768]{1,0:T(8,128)(2,1)S(1)} %collective-permute-done.9.refs_10_), channel_id=1, source_target_pairs={{0,4},{1,5},{2,6},{3,7},{4,8},{5,9},{6,10},{7,11},{8,12},{9,13},{1... | collective-permute-start | bytes 589832 | tf_op jit(solution)/shard_map/ppermute | solution.py:50
  18.6 3.4 %collective-permute-start.6 = (bf16[128,768]{1,0:T(8,128)(2,1)S(1)}, bf16[128,768]{1,0:T(8,128)(2,1)S(1)}, u32[]{:S(2)}, u32[]{:S(2)}) collective-permute-start(bf16[128,768]{1,0:T(8,128)(2,1)S(1)} %collective-permute-done.5.refs_6_), channel_id=1, source_target_pairs={{0,1},{1,0},{2,3},{3,2},{4,5},{5,4},{6,7},{7,6},{8,9},{9,8},{10,11... | collective-permute-start | bytes 589832 | tf_op jit(solution)/shard_map/ppermute | solution.py:50
  18.7 7.0 %collective-permute-start.10 = (bf16[128,768]{1,0:T(8,128)(2,1)S(1)}, bf16[128,768]{1,0:T(8,128)(2,1)S(1)}, u32[]{:S(2)}, u32[]{:S(2)}) collective-permute-start(bf16[128,768]{1,0:T(8,128)(2,1)S(1)} %collective-permute-done.9.refs_10_), channel_id=1, source_target_pairs={{0,1},{1,0},{2,3},{3,2},{4,5},{5,4},{6,7},{7,6},{8,9},{9,8},{10,11... | collective-permute-start | bytes 589832 | tf_op jit(solution)/shard_map/ppermute | solution.py:50
  22.0 12.0 %collective-permute-start.11 = (bf16[256,768]{1,0:T(8,128)(2,1)S(1)}, bf16[256,768]{1,0:T(8,128)(2,1)S(1)}, u32[]{:S(2)}, u32[]{:S(2)}) collective-permute-start(bf16[256,768]{1,0:T(8,128)(2,1)S(1)} %pad_maximum_fusion), channel_id=1, source_target_pairs={{0,16},{1,3},{2,18},{3,1},{4,20},{5,7},{6,22},{7,5},{8,24},{9,11},... | collective-permute-start | bytes 1179656 | tf_op jit(solution)/shard_map/ppermute | solution.py:50
  22.0 5.7 %collective-permute-start.20 = (bf16[128,768]{1,0:T(8,128)(2,1)S(1)}, bf16[128,768]{1,0:T(8,128)(2,1)S(1)}, u32[]{:S(2)}, u32[]{:S(2)}) collective-permute-start(bf16[128,768]{1,0:T(8,128)(2,1)S(1)} %collective-permute-done.19.refs_20_), channel_id=1, source_target_pairs={{0,1},{1,0},{2,3},{3,2},{4,5},{5,4},{6,7},{7,6},{8,9},{9,8},{10,11... | collective-permute-start | bytes 589832 | tf_op jit(solution)/shard_map/ppermute | solution.py:50
  22.1 12.4 %collective-permute-start.17 = (bf16[256,768]{1,0:T(8,128)(2,1)S(1)}, bf16[256,768]{1,0:T(8,128)(2,1)S(1)}, u32[]{:S(2)}, u32[]{:S(2)}) collective-permute-start(bf16[256,768]{1,0:T(8,128)(2,1)S(1)} %pad_maximum_fusion.2), channel_id=1, source_target_pairs={{0,16},{1,3},{2,18},{3,1},{4,20},{5,7},{6,22},{7,5},{8,24},{9,11},... | collective-permute-start | bytes 1179656 | tf_op jit(solution)/shard_map/ppermute | solution.py:50
  25.6 12.5 %collective-permute-start.13 = (bf16[256,768]{1,0:T(8,128)(2,1)S(1)}, bf16[256,768]{1,0:T(8,128)(2,1)S(1)}, u32[]{:S(2)}, u32[]{:S(2)}) collective-permute-start(bf16[256,768]{1,0:T(8,128)(2,1)S(1)} %pad_maximum_fusion.1), channel_id=1, source_target_pairs={{0,16},{1,3},{2,18},{3,1},{4,20},{5,7},{6,22},{7,5},{8,24},{9,11},... | collective-permute-start | bytes 1179656 | tf_op jit(solution)/shard_map/ppermute | solution.py:50
  25.7 16.8 %collective-permute-start.21 = (bf16[256,768]{1,0:T(8,128)(2,1)S(1)}, bf16[256,768]{1,0:T(8,128)(2,1)S(1)}, u32[]{:S(2)}, u32[]{:S(2)}) collective-permute-start(bf16[256,768]{1,0:T(8,128)(2,1)S(1)} %pad_maximum_fusion.3), channel_id=1, source_target_pairs={{0,16},{1,3},{2,18},{3,1},{4,20},{5,7},{6,22},{7,5},{8,24},{9,11},... | collective-permute-start | bytes 1179656 | tf_op jit(solution)/shard_map/ppermute | solution.py:50
  27.7 6.3 %collective-permute-start.23 = (bf16[128,768]{1,0:T(8,128)(2,1)S(1)}, bf16[128,768]{1,0:T(8,128)(2,1)S(1)}, u32[]{:S(2)}, u32[]{:S(2)}) collective-permute-start(bf16[128,768]{1,0:T(8,128)(2,1)S(1)} %collective-permute-done.15.refs_16_), channel_id=1, source_target_pairs={{0,4},{1,5},{2,6},{3,7},{4,8},{5,9},{6,10},{7,11},{8,12},{9,13},{1... | collective-permute-start | bytes 589832 | tf_op jit(solution)/shard_map/ppermute | solution.py:50
  33.9 8.5 %collective-permute-start.16 = (bf16[128,768]{1,0:T(8,128)(2,1)S(1)}, bf16[128,768]{1,0:T(8,128)(2,1)S(1)}, u32[]{:S(2)}, u32[]{:S(2)}) collective-permute-start(bf16[128,768]{1,0:T(8,128)(2,1)S(1)} %collective-permute-done.15.refs_16_), channel_id=1, source_target_pairs={{0,1},{1,0},{2,3},{3,2},{4,5},{5,4},{6,7},{7,6},{8,9},{9,8},{10,11... | collective-permute-start | bytes 589832 | tf_op jit(solution)/shard_map/ppermute | solution.py:50
  34.0 16.3 %collective-permute-start.12 = (bf16[256,768]{1,0:T(8,128)(2,1)S(1)}, bf16[256,768]{1,0:T(8,128)(2,1)S(1)}, u32[]{:S(2)}, u32[]{:S(2)}) collective-permute-start(bf16[256,768]{1,0:T(8,128)(2,1)S(1)} %collective-permute-done.11.refs_12_), channel_id=1, source_target_pairs={{0,1},{1,0},{2,3},{3,2},{4,5},{5,4},{6,7},{7,6},{8,9},{9,8},{10,11... | collective-permute-start | bytes 1179656 | tf_op jit(solution)/shard_map/ppermute | solution.py:50
  34.5 15.8 %collective-permute-start.18 = (bf16[256,768]{1,0:T(8,128)(2,1)S(1)}, bf16[256,768]{1,0:T(8,128)(2,1)S(1)}, u32[]{:S(2)}, u32[]{:S(2)}) collective-permute-start(bf16[256,768]{1,0:T(8,128)(2,1)S(1)} %collective-permute-done.17.refs_18_), channel_id=1, source_target_pairs={{0,1},{1,0},{2,3},{3,2},{4,5},{5,4},{6,7},{7,6},{8,9},{9,8},{10,11... | collective-permute-start | bytes 1179656 | tf_op jit(solution)/shard_map/ppermute | solution.py:50
  38.2 12.1 %collective-permute-start.14 = (bf16[256,768]{1,0:T(8,128)(2,1)S(1)}, bf16[256,768]{1,0:T(8,128)(2,1)S(1)}, u32[]{:S(2)}, u32[]{:S(2)}) collective-permute-start(bf16[256,768]{1,0:T(8,128)(2,1)S(1)} %collective-permute-done.13.refs_14_), channel_id=1, source_target_pairs={{0,1},{1,0},{2,3},{3,2},{4,5},{5,4},{6,7},{7,6},{8,9},{9,8},{10,11... | collective-permute-start | bytes 1179656 | tf_op jit(solution)/shard_map/ppermute | solution.py:50
  42.4 7.9 %collective-permute-start.22 = (bf16[256,768]{1,0:T(8,128)(2,1)S(1)}, bf16[256,768]{1,0:T(8,128)(2,1)S(1)}, u32[]{:S(2)}, u32[]{:S(2)}) collective-permute-start(bf16[256,768]{1,0:T(8,128)(2,1)S(1)} %collective-permute-done.21.refs_22_), channel_id=1, source_target_pairs={{0,1},{1,0},{2,3},{3,2},{4,5},{5,4},{6,7},{7,6},{8,9},{9,8},{10,11... | collective-permute-start | bytes 1179656 | tf_op jit(solution)/shard_map/ppermute | solution.py:50
  42.4 7.8 %collective-permute-start.24 = (bf16[128,768]{1,0:T(8,128)(2,1)S(1)}, bf16[128,768]{1,0:T(8,128)(2,1)S(1)}, u32[]{:S(2)}, u32[]{:S(2)}) collective-permute-start(bf16[128,768]{1,0:T(8,128)(2,1)S(1)} %collective-permute-done.23.refs_24_), channel_id=1, source_target_pairs={{0,1},{1,0},{2,3},{3,2},{4,5},{5,4},{6,7},{7,6},{8,9},{9,8},{10,11... | collective-permute-start | bytes 589832 | tf_op jit(solution)/shard_map/ppermute | solution.py:50
  43.6 1.0 %copy-start = (s32[64,4,256]{2,1,0:T(4,128)S(1)}, s32[64,4,256]{2,1,0:T(4,128)}, u32[]{:S(2)}) copy-start(s32[64,4,256]{2,1,0:T(4,128)} %table_ref.1) | copy-start | bytes 786436
  44.6 0.7 %copy-start.1 = (s32[32,80]{1,0:T(8,128)S(1)}, s32[32,80]{1,0:T(8,128)}, u32[]{:S(2)}) copy-start(s32[32,80]{1,0:T(8,128)} %constant.2.clone.place_ref) | copy-start | bytes 30724
where the time goes:
time: 58.1 us; the launch traced here: 57.7 us
  waiting for transfers between devices  24.2 us (42%)
  starting transfers between devices  16.8 us (29%)
  Pallas kernels  12.3 us (21%)
  other arithmetic  2.52 us (4%)
  local copies, waits for them, and re-layouts  1.67 us (3%)
    ppermute x25, waiting for transfers between devices, send(): value = lax.ppermute(value, ('rep', 'slab', 'pix'), self.pairs(port))  24.2 us
    ppermute x25, starting transfers between devices, send(): value = lax.ppermute(value, ('rep', 'slab', 'pix'), self.pairs(port))  16.8 us
    pallas_call x1, Pallas kernels, spread(): pl.pallas_call(kernel, out_shape=jax.ShapeDtypeStruct((count_x, planes, 2...  7.43 us
    pallas_call x1, Pallas kernels, make_plan(): pl.pallas_call(kernel, out_shape=[jax.ShapeDtypeStruct((info_size,), jnp....  4.89 us
    unnamed x4, local copies, waits for them, and re-layouts  1.67 us
  transfers between devices with their start and end apart: 25, of which 7 were waited for; matrix products, arithmetic and copies ran while one was open for 3% of the time, Pallas kernels for 8%

commit v1 on v0

--- a/solution.py
+++ b/solution.py
@@ -62,14 +62,12 @@
     side0 = ports.send(chip_own, "x|y")
     down = ports.send(own, "back")
     across = ports.send(own, "xy")
-    orient = (orient, [ports.ids])
-    orient_x = ports.send(orient, "x")
+    orients = [(orient, [ports.ids])]
+    orients.append(ports.send(orients[0], "core"))
+    orients += [ports.send(orients[0], "x"), ports.send(orients[1], "x")]
     core_up1, chip_up1 = ports.both(up1)
     up2 = ports.send(up1, "z")
     side1 = ports.send(chip_up1, "x|y")
-    orient = (jnp.concatenate([orient[0], orient_x[0]]), orient[1] + orient_x[1])
-    orient_core = ports.send(orient, "core")
-    orient = (jnp.concatenate([orient[0], orient_core[0]]), orient[1] + orient_core[1])
     core_down, chip_down = ports.both(down)
     across1 = ports.send(across, "z")
     side3 = ports.send(chip_down, "x|y")
@@ -83,7 +81,8 @@
         pieces += [held, ports.send(held, "core")]
     owners = np.stack([owner for _, owned in pieces for owner in owned], axis=-1)
     assert (np.sort(owners, -1) == np.arange(ports.ids.size)).all()
-    return [value for value, _ in pieces], owners, orient[0], np.stack(orient[1], axis=-1)
+    orient_owners = np.stack([owner for _, owned in orients for owner in owned], axis=-1)
+    return [value for value, _ in pieces], owners, [value for value, _ in orients], orient_owners
 
 
 def lookup(orient, angle_table):
@@ -100,8 +99,9 @@
     return size.bit_length() - 1
 
 
-def make_plan(orient, place, table, pieces_n, sizes):
+def make_plan(orients, place, table, pieces_n, sizes):
     batch, planes, columns, count_x, row_block, batches = sizes
+    parts = len(orients)
     items = batch * planes // GROUP
     segments = pieces_n * items
     steps, lane_groups = count_x // row_block, LANES // GROUP
@@ -109,22 +109,31 @@
     info_size = segments + segments * GROUP // TILE + 1
     total_n = batch * batches
 
-    def kernel(orient_ref, place_ref, table_ref, info_ref, where_ref, raw, geometry, found, found_s, listed, sems):
+    def kernel(*refs):
+        orient_refs = refs[:parts]
+        place_all, table_ref, info_ref, where_ref, place_ref, raw, geometry, found, found_s, listed, sems = refs[parts:]
         me = (lax.axis_index("rep") * lax.axis_size("slab") + lax.axis_index("slab")) * lax.axis_size("pix")
         me += lax.axis_index("pix")
         rep, pix = lax.axis_index("rep"), lax.axis_index("pix")
         first_x = (rep * lax.axis_size("pix") + pix) * count_x
         first_z = lax.axis_index("slab") * planes
+        placing = pltpu.make_async_copy(place_all.at[me, 0], place_ref, sems.at[total_n])
+        placing.start()
         copies = [
-            pltpu.make_async_copy(table_ref.at[orient_ref[n]], raw.at[place_ref[me, n]], sems.at[n])
+            pltpu.make_async_copy(
+                table_ref.at[orient_refs[n // batch][n % batch]], raw.at[n], sems.at[n]
+            )
             for n in range(total_n)
         ]
         for copy in copies:
             copy.start()
+        placing.wait()
         for copy in copies:
             copy.wait()
         unit = lax.broadcasted_iota(jnp.int32, (1, 4, columns), 1) & 1
-        geometry[:, 0:4, :] = raw[...].astype(jnp.float32) * jnp.where(unit == 1, 1.0 / 256.0, 1.0)
+        unit = jnp.where(unit[0] == 1, 1.0 / 256.0, 1.0)
+        for n in range(total_n):
+            geometry[place_ref[n], 0:4, :] = raw[n].astype(jnp.float32) * unit
         near_x = geometry[:, 0, :] - first_x.astype(jnp.float32)
         near_z = geometry[:, 2, :] - first_z.astype(jnp.float32)
         hit_z = (near_z >= -1.0) & (near_z < planes)
@@ -161,8 +170,8 @@
 
         count = jnp.int32(0)
         for piece in range(pieces_n):
-            first_n = place_ref[me, total_n + 2 * piece]
-            first_g = place_ref[me, total_n + 2 * piece + 1]
+            first_n = place_ref[total_n + 2 * piece]
+            first_g = place_ref[total_n + 2 * piece + 1]
             for item in range(items):
                 n, g = first_n + item // (items // batch), first_g + item % (items // batch)
                 code = found_s[n, g]
@@ -201,19 +210,20 @@
             jax.ShapeDtypeStruct((info_size,), jnp.int32),
             jax.ShapeDtypeStruct((8, segments * GROUP), jnp.float32),
         ],
-        in_specs=[smem, smem, pl.BlockSpec(memory_space=pl.ANY)],
+        in_specs=[smem] * parts + [pl.BlockSpec(memory_space=pltpu.HBM)] * 2,
         out_specs=[smem, vmem],
         scratch_shapes=[
+            pltpu.SMEM(place.shape[2:], jnp.int32),
             pltpu.VMEM((total_n, 4, columns), jnp.int32),
             pltpu.VMEM((total_n, 8, columns), jnp.float32),
             pltpu.VMEM((total_n, LANES), jnp.int32),
             pltpu.SMEM((total_n, LANES), jnp.int32),
             pltpu.SMEM((segments + 1,), jnp.int32),
-            pltpu.SemaphoreType.DMA((total_n,)),
+            pltpu.SemaphoreType.DMA((total_n + 1,)),
         ],
         compiler_params=pltpu.CompilerParams(vmem_limit_bytes=4 << 20),
         name="plan",
-    )(orient, place, table)
+    )(*orients, place, table)
 
 
 def spread(pieces, info, where, sizes):
@@ -334,7 +344,7 @@
         row_block = TILE // planes
         sizes = (batch, planes, columns, count_x, row_block, ports.rep * ports.pix)
         samples = jnp.concatenate([projections, ctf_weight], axis=2).reshape(batch * planes, 3 * columns)
-        pieces, owners, orient, orient_owners = gather_pieces(samples, orient, ports)
+        pieces, owners, orients, orient_owners = gather_pieces(samples, orient, ports)
         place = []
         for owner in (orient_owners, owners):
             rep, slab, pix = np.unravel_index(owner, ports.ids.shape)
@@ -342,8 +352,9 @@
         (order, _), (first_n, first_g) = place
         order = order[..., None] + np.arange(batch)
         place = [order.reshape(ports.ids.size, -1), np.stack([first_n, first_g], -1).reshape(ports.ids.size, -1)]
-        place = jnp.asarray(np.concatenate(place, axis=1), jnp.int32)
-        info, where = make_plan(orient, place, angle_table, owners.shape[-1], sizes)
+        place = np.concatenate(place, axis=1)
+        place = np.pad(place, ((0, 0), (0, -place.shape[1] % LANES)))[:, None]
+        info, where = make_plan(orients, jnp.asarray(place, jnp.int32), angle_table, owners.shape[-1], sizes)
         return spread(pieces, info, where, sizes)
 
     return body

time: 58.1 us -> 63.6 us (1.095)
  waiting for transfers between devices: 24.2 us -> 30.3 us
  other arithmetic: 2.52 us -> 1.06 us
  local copies, waits for them, and re-layouts: 1.67 us -> 2.32 us
    ppermute x25 -> x26, waiting for transfers between devices: 24.2 us -> 30.3 us  [send(): value = lax.ppermute(value, ('rep', 'slab', 'pix'), self.pairs(port))]
    concatenate x2 -> x0, other arithmetic: 1.46 us -> none  [the longest x1 0.73 us: gather_pieces(): jnp.concatenate([orient[0], orient_x[0]])]
    unnamed x4 -> x6, local copies, waits for them, and re-layouts: 1.67 us -> 2.32 us
    ppermute x25 -> x26, starting transfers between devices: 16.8 us -> 17.1 us  [send(): value = lax.ppermute(value, ('rep', 'slab', 'pix'), self.pairs(port))]
  transfers between devices with their start and end apart: 25 -> 26, of which waited for: 7 -> 8; matrix products, arithmetic and copies ran while one was open for 3% -> 0% of each run, Pallas kernels for 8% -> 8%
where the time goes in v1:
time: 63.6 us; the launch traced here: 63.4 us
  waiting for transfers between devices  30.3 us (48%)
  starting transfers between devices  17.1 us (27%)
  Pallas kernels  12.5 us (20%)
  local copies, waits for them, and re-layouts  2.32 us (4%)
  other arithmetic  1.06 us (2%)
    ppermute x26, waiting for transfers between devices, send(): value = lax.ppermute(value, ('rep', 'slab', 'pix'), self.pairs(port))  30.3 us
    ppermute x26, starting transfers between devices, send(): value = lax.ppermute(value, ('rep', 'slab', 'pix'), self.pairs(port))  17.1 us
    pallas_call x1, Pallas kernels, spread(): pl.pallas_call(kernel, out_shape=jax.ShapeDtypeStruct((count_x, planes, 2...  7.43 us
    pallas_call x1, Pallas kernels, make_plan(): pl.pallas_call(kernel, out_shape=[jax.ShapeDtypeStruct((info_size,), jnp....  5.07 us
    unnamed x6, local copies, waits for them, and re-layouts  2.32 us
  transfers between devices with their start and end apart: 26, of which 8 were waited for; matrix products, arithmetic and copies ran while one was open for 0% of the time, Pallas kernels for 8%

profile of v1, /device:TPU:18, one launch (start us, length us, event | category | flops | bytes accessed | tf_op | source)
XLA Modules:
  0.0 63.4 jit_solution(8757521434655774563)
XLA Ops:
  0.0 1.0 %pad_maximum_fusion.4 = bf16[4,32,768]{2,1,0:T(8,128)(2,1)S(1)} fusion(bf16[4,32,256]{2,1,0:T(8,128)(2,1)} %param.6, bf16[4,32,512]{2,1,0:T(8,128)(2,1)} %param.5), kind=kLoop, calls=%fused_computation.4 | loop fusion | flops 393216 | bytes 393216 | tf_op jit(solution)/shard_map/concatenate | solution.py:346
  1.0 1.6 %collective-permute-start.4 = (bf16[128,768]{1,0:T(8,128)(2,1)S(1)}, bf16[128,768]{1,0:T(8,128)(2,1)S(1)}, u32[]{:S(2)}, u32[]{:S(2)}) collective-permute-start(bf16[128,768]{1,0:T(8,128)(2,1)S(1)} %bitcast.1), channel_id=1, source_target_pairs={{0,4},{1,5},{2,6},{3,7},{4,8},{5,9},{6,10},{7,11},{8,12},{9,13},{1... | collective-permute-start | bytes 589832 | tf_op jit(solution)/shard_map/ppermute | solution.py:50
  2.6 1.5 %collective-permute-start.10 = (bf16[128,768]{1,0:T(8,128)(2,1)S(1)}, bf16[128,768]{1,0:T(8,128)(2,1)S(1)}, u32[]{:S(2)}, u32[]{:S(2)}) collective-permute-start(bf16[128,768]{1,0:T(8,128)(2,1)S(1)} %bitcast.2), channel_id=1, source_target_pairs={{0,18},{1,19},{2,16},{3,17},{4,22},{5,23},{6,20},{7,21},{8,26},{9,... | collective-permute-start | bytes 589832 | tf_op jit(solution)/shard_map/ppermute | solution.py:50
  4.1 0.4 collective-permute-start.8
  4.5 0.0 collective-permute-start.3
  4.5 6.5 %collective-permute-done.4.refs_4_ = bf16[128,768]{1,0:T(8,128)(2,1)S(1)} collective-permute-done((bf16[128,768]{1,0:T(8,128)(2,1)S(1)}, bf16[128,768]{1,0:T(8,128)(2,1)S(1)}, u32[]{:S(2)}, u32[]{:S(2)}) %collective-permute-start.4) | collective-permute-done | bytes 196640 | tf_op jit(solution)/shard_map/ppermute | solution.py:50
  11.1 1.9 %collective-permute-start.6 = (bf16[128,768]{1,0:T(8,128)(2,1)S(1)}, bf16[128,768]{1,0:T(8,128)(2,1)S(1)}, u32[]{:S(2)}, u32[]{:S(2)}) collective-permute-start(bf16[128,768]{1,0:T(8,128)(2,1)S(1)} %collective-permute-done.4.refs_4_), channel_id=1, source_target_pairs={{0,4},{1,5},{2,6},{3,7},{4,8},{5,9},{6,10},{7,11},{8,12},{9,13},{1... | collective-permute-start | bytes 589832 | tf_op jit(solution)/shard_map/ppermute | solution.py:50
  13.0 0.5 collective-permute-start
  13.5 0.5 collective-permute-start.20
  14.0 6.2 %collective-permute-done.6.refs_6_ = bf16[128,768]{1,0:T(8,128)(2,1)S(1)} collective-permute-done((bf16[128,768]{1,0:T(8,128)(2,1)S(1)}, bf16[128,768]{1,0:T(8,128)(2,1)S(1)}, u32[]{:S(2)}, u32[]{:S(2)}) %collective-permute-start.6) | collective-permute-done | bytes 196640 | tf_op jit(solution)/shard_map/ppermute | solution.py:50
  20.1 3.0 %collective-permute-start.16 = (bf16[128,768]{1,0:T(8,128)(2,1)S(1)}, bf16[128,768]{1,0:T(8,128)(2,1)S(1)}, u32[]{:S(2)}, u32[]{:S(2)}) collective-permute-start(bf16[128,768]{1,0:T(8,128)(2,1)S(1)} %collective-permute-done.10.refs_10_), channel_id=1, source_target_pairs={{0,4},{1,5},{2,6},{3,7},{4,8},{5,9},{6,10},{7,11},{8,12},{9,13},{1... | collective-permute-start | bytes 589832 | tf_op jit(solution)/shard_map/ppermute | solution.py:50
  23.2 0.6 collective-permute-start.11
  23.8 0.1 collective-permute-start.1
  23.9 2.0 %collective-permute-start.2 = (s32[4]{0:T(128)S(1)}, s32[4]{0:T(128)S(1)}, u32[]{:S(2)}, u32[]{:S(2)}) collective-permute-start(s32[4]{0:T(128)S(1)} %collective-permute-done.refs_1_), channel_id=1, source_target_pairs={{0,16},{1,17},{2,18},{3,19},{4,20},{5,21},{6,22},{7,23},{8,24},{9,... | collective-permute-start | bytes 56 | tf_op jit(solution)/shard_map/ppermute | solution.py:50
  25.9 1.6 %collective-permute-done.1.refs_2_ = s32[4]{0:T(128)S(1)} collective-permute-done((s32[4]{0:T(128)}, s32[4]{0:T(128)S(1)}, u32[]{:S(2)}, u32[]{:S(2)}) %collective-permute-start.1) | collective-permute-done | bytes 48 | tf_op jit(solution)/shard_map/ppermute | solution.py:50
  27.5 0.0 collective-permute-start.12
  27.5 0.1 collective-permute-done.2.refs_3_
  27.6 1.9 %collective-permute-start.18 = (bf16[256,768]{1,0:T(8,128)(2,1)S(1)}, bf16[256,768]{1,0:T(8,128)(2,1)S(1)}, u32[]{:S(2)}, u32[]{:S(2)}) collective-permute-start(bf16[256,768]{1,0:T(8,128)(2,1)S(1)} %pad_maximum_fusion.2), channel_id=1, source_target_pairs={{0,16},{1,3},{2,18},{3,1},{4,20},{5,7},{6,22},{7,5},{8,24},{9,11},... | collective-permute-start | bytes 1179656 | tf_op jit(solution)/shard_map/ppermute | solution.py:50
  29.6 0.1 collective-permute-start.14
  29.7 1.9 %collective-permute-start.22 = (bf16[256,768]{1,0:T(8,128)(2,1)S(1)}, bf16[256,768]{1,0:T(8,128)(2,1)S(1)}, u32[]{:S(2)}, u32[]{:S(2)}) collective-permute-start(bf16[256,768]{1,0:T(8,128)(2,1)S(1)} %pad_maximum_fusion.3), channel_id=1, source_target_pairs={{0,16},{1,3},{2,18},{3,1},{4,20},{5,7},{6,22},{7,5},{8,24},{9,11},... | collective-permute-start | bytes 1179656 | tf_op jit(solution)/shard_map/ppermute | solution.py:50
  31.6 0.0 collective-permute-start.24
  31.6 5.7 %collective-permute-done.24.refs_24_ = bf16[128,768]{1,0:T(8,128)(2,1)S(1)} collective-permute-done((bf16[128,768]{1,0:T(8,128)(2,1)S(1)}, bf16[128,768]{1,0:T(8,128)(2,1)S(1)}, u32[]{:S(2)}, u32[]{:S(2)}) %collective-permute-start.24) | collective-permute-done | bytes 196640 | tf_op jit(solution)/shard_map/ppermute | solution.py:50
  37.3 0.5 collective-permute-start.13
  37.8 1.7 %collective-permute-done.18.refs_18_ = bf16[256,768]{1,0:T(8,128)(2,1)S(1)} collective-permute-done((bf16[256,768]{1,0:T(8,128)(2,1)S(1)}, bf16[256,768]{1,0:T(8,128)(2,1)S(1)}, u32[]{:S(2)}, u32[]{:S(2)}) %collective-permute-start.18) | collective-permute-done | bytes 393248 | tf_op jit(solution)/shard_map/ppermute | solution.py:50
  39.5 4.2 %collective-permute-done.14.refs_14_ = bf16[256,768]{1,0:T(8,128)(2,1)S(1)} collective-permute-done((bf16[256,768]{1,0:T(8,128)(2,1)S(1)}, bf16[256,768]{1,0:T(8,128)(2,1)S(1)}, u32[]{:S(2)}, u32[]{:S(2)}) %collective-permute-start.14) | collective-permute-done | bytes 393248 | tf_op jit(solution)/shard_map/ppermute | solution.py:50
  43.7 4.2 %collective-permute-done.22.refs_22_ = bf16[256,768]{1,0:T(8,128)(2,1)S(1)} collective-permute-done((bf16[256,768]{1,0:T(8,128)(2,1)S(1)}, bf16[256,768]{1,0:T(8,128)(2,1)S(1)}, u32[]{:S(2)}, u32[]{:S(2)}) %collective-permute-start.22) | collective-permute-done | bytes 393248 | tf_op jit(solution)/shard_map/ppermute | solution.py:50
  48.0 0.5 collective-permute-start.25
  48.5 0.9 %copy-done = s32[64,4,256]{2,1,0:T(4,128)S(1)} copy-done((s32[64,4,256]{2,1,0:T(4,128)S(1)}, s32[64,4,256]{2,1,0:T(4,128)}, u32[]{:S(2)}) %copy-start) | copy-done | bytes 262168
  49.4 0.7 %copy-done.1 = s32[32,1,128]{2,1,0:T(1,128)S(1)} copy-done((s32[32,1,128]{2,1,0:T(1,128)S(1)}, s32[32,1,128]{2,1,0:T(1,128)}, u32[]{:S(2)}) %copy-start.1) | copy-done | bytes 16408
  50.1 0.7 %copy-done.2 = s32[4]{0:T(128)S(1)} copy-done((s32[4]{0:T(128)S(1)}, s32[4]{0:T(128)}, u32[]{:S(2)}) %copy-start.2) | copy-done | bytes 40
  50.8 5.1 %plan.1 = (s32[273]{0:T(512)S(1)}, f32[8,4096]{1,0:T(8,128)S(1)}) custom-call(s32[4]{0:T(128)S(1)} %copy-done.2, s32[4]{0:T(128)S(1)} %collective-permute-done.refs_1_, s32[4]{0:T(128)S(1)} %collective-permute-done.1.refs_2_, s32[4]{0:T(128)S(1)} %collective-permute-done.2.refs_3_, s32[32,1,128]{2,1,0:T(1,128)S(1)} %copy-done.1, s32[64,4,256]{2,1,0:T(4,128)S(1)} %copy-done), custom_call_target="tpu_custom_call" | custom-call | tf_op jit(solution)/shard_map/plan/pallas_call | solution.py:207
  55.9 7.4 %spread.1 = f32[64,32,512]{2,1,0:T(8,128)} custom-call(s32[273]{0:T(512)S(1)} %get-tuple-element.7.refs_0_, f32[8,4096]{1,0:T(8,128)S(1)} %get-tuple-element.8.refs_1_, bf16[128,768]{1,0:T(8,128)(2,1)S(1)} %bitcast.6, bf16[128,768]{1,0:T(8,128)(2,1)S(1)} %collective-permute-done.3.refs_3_, bf16[128,768]{1,0:T(8,128)(2,1)S(1)} %collective-permute-done.4.refs_4_, ...), custom_call_target="tpu_custom_call" | custom-call | tf_op jit(solution)/shard_map/spread/pallas_call | solution.py:323
  (33 shorter events, 0.2 us)
Async XLA Ops:
  1.0 10.1 %collective-permute-start.4 = (bf16[128,768]{1,0:T(8,128)(2,1)S(1)}, bf16[128,768]{1,0:T(8,128)(2,1)S(1)}, u32[]{:S(2)}, u32[]{:S(2)}) collective-permute-start(bf16[128,768]{1,0:T(8,128)(2,1)S(1)} %bitcast.1), channel_id=1, source_target_pairs={{0,4},{1,5},{2,6},{3,7},{4,8},{5,9},{6,10},{7,11},{8,12},{9,13},{1... | collective-permute-start | bytes 589832 | tf_op jit(solution)/shard_map/ppermute | solution.py:50
  2.6 10.4 %collective-permute-start.10 = (bf16[128,768]{1,0:T(8,128)(2,1)S(1)}, bf16[128,768]{1,0:T(8,128)(2,1)S(1)}, u32[]{:S(2)}, u32[]{:S(2)}) collective-permute-start(bf16[128,768]{1,0:T(8,128)(2,1)S(1)} %bitcast.2), channel_id=1, source_target_pairs={{0,18},{1,19},{2,16},{3,17},{4,22},{5,23},{6,20},{7,21},{8,26},{9,... | collective-permute-start | bytes 589832 | tf_op jit(solution)/shard_map/ppermute | solution.py:50
  4.1 9.4 %collective-permute-start.8 = (bf16[128,768]{1,0:T(8,128)(2,1)S(1)}, bf16[128,768]{1,0:T(8,128)(2,1)S(1)}, u32[]{:S(2)}, u32[]{:S(2)}) collective-permute-start(bf16[128,768]{1,0:T(8,128)(2,1)S(1)} %bitcast.3), channel_id=1, source_target_pairs={{0,12},{1,13},{2,14},{3,15},{4,0},{5,1},{6,2},{7,3},{8,4},{9,5},{1... | collective-permute-start | bytes 589832 | tf_op jit(solution)/shard_map/ppermute | solution.py:50
  4.5 9.4 %collective-permute-start.3 = (bf16[128,768]{1,0:T(8,128)(2,1)S(1)}, bf16[128,768]{1,0:T(8,128)(2,1)S(1)}, u32[]{:S(2)}, u32[]{:S(2)}) collective-permute-start(bf16[128,768]{1,0:T(8,128)(2,1)S(1)} %bitcast.4), channel_id=1, source_target_pairs={{0,1},{1,0},{2,3},{3,2},{4,5},{5,4},{6,7},{7,6},{8,9},{9,8},{10,11... | collective-permute-start | bytes 589832 | tf_op jit(solution)/shard_map/ppermute | solution.py:50
  11.1 9.1 %collective-permute-start.6 = (bf16[128,768]{1,0:T(8,128)(2,1)S(1)}, bf16[128,768]{1,0:T(8,128)(2,1)S(1)}, u32[]{:S(2)}, u32[]{:S(2)}) collective-permute-start(bf16[128,768]{1,0:T(8,128)(2,1)S(1)} %collective-permute-done.4.refs_4_), channel_id=1, source_target_pairs={{0,4},{1,5},{2,6},{3,7},{4,8},{5,9},{6,10},{7,11},{8,12},{9,13},{1... | collective-permute-start | bytes 589832 | tf_op jit(solution)/shard_map/ppermute | solution.py:50
  13.0 10.2 %collective-permute-start.5 = (bf16[128,768]{1,0:T(8,128)(2,1)S(1)}, bf16[128,768]{1,0:T(8,128)(2,1)S(1)}, u32[]{:S(2)}, u32[]{:S(2)}) collective-permute-start(bf16[128,768]{1,0:T(8,128)(2,1)S(1)} %collective-permute-done.4.refs_4_), channel_id=1, source_target_pairs={{0,1},{1,0},{2,3},{3,2},{4,5},{5,4},{6,7},{7,6},{8,9},{9,8},{10,11... | collective-permute-start | bytes 589832 | tf_op jit(solution)/shard_map/ppermute | solution.py:50
  13.0 10.8 %collective-permute-start = (s32[4]{0:T(128)}, s32[4]{0:T(128)S(1)}, u32[]{:S(2)}, u32[]{:S(2)}) collective-permute-start(s32[4]{0:T(128)} %refs_0_.1), channel_id=1, source_target_pairs={{0,1},{1,0},{2,3},{3,2},{4,5},{5,4},{6,7},{7,6},{8,9},{9,8},{10,11... | collective-permute-start | bytes 56 | tf_op jit(solution)/shard_map/ppermute | solution.py:50
  13.5 10.4 %collective-permute-start.20 = (bf16[128,768]{1,0:T(8,128)(2,1)S(1)}, bf16[128,768]{1,0:T(8,128)(2,1)S(1)}, u32[]{:S(2)}, u32[]{:S(2)}) collective-permute-start(bf16[128,768]{1,0:T(8,128)(2,1)S(1)} %collective-permute-done.10.refs_10_), channel_id=1, source_target_pairs={{0,12},{1,13},{2,14},{3,15},{4,0},{5,1},{6,2},{7,3},{8,4},{9,5},{1... | collective-permute-start | bytes 589832 | tf_op jit(solution)/shard_map/ppermute | solution.py:50
  13.9 9.2 %collective-permute-start.9 = (bf16[128,768]{1,0:T(8,128)(2,1)S(1)}, bf16[128,768]{1,0:T(8,128)(2,1)S(1)}, u32[]{:S(2)}, u32[]{:S(2)}) collective-permute-start(bf16[128,768]{1,0:T(8,128)(2,1)S(1)} %collective-permute-done.8.refs_8_), channel_id=1, source_target_pairs={{0,1},{1,0},{2,3},{3,2},{4,5},{5,4},{6,7},{7,6},{8,9},{9,8},{10,11... | collective-permute-start | bytes 589832 | tf_op jit(solution)/shard_map/ppermute | solution.py:50
  20.1 9.4 %collective-permute-start.16 = (bf16[128,768]{1,0:T(8,128)(2,1)S(1)}, bf16[128,768]{1,0:T(8,128)(2,1)S(1)}, u32[]{:S(2)}, u32[]{:S(2)}) collective-permute-start(bf16[128,768]{1,0:T(8,128)(2,1)S(1)} %collective-permute-done.10.refs_10_), channel_id=1, source_target_pairs={{0,4},{1,5},{2,6},{3,7},{4,8},{5,9},{6,10},{7,11},{8,12},{9,13},{1... | collective-permute-start | bytes 589832 | tf_op jit(solution)/shard_map/ppermute | solution.py:50
  23.1 2.8 %collective-permute-start.7 = (bf16[128,768]{1,0:T(8,128)(2,1)S(1)}, bf16[128,768]{1,0:T(8,128)(2,1)S(1)}, u32[]{:S(2)}, u32[]{:S(2)}) collective-permute-start(bf16[128,768]{1,0:T(8,128)(2,1)S(1)} %collective-permute-done.6.refs_6_), channel_id=1, source_target_pairs={{0,1},{1,0},{2,3},{3,2},{4,5},{5,4},{6,7},{7,6},{8,9},{9,8},{10,11... | collective-permute-start | bytes 589832 | tf_op jit(solution)/shard_map/ppermute | solution.py:50
  23.2 6.5 %collective-permute-start.11 = (bf16[128,768]{1,0:T(8,128)(2,1)S(1)}, bf16[128,768]{1,0:T(8,128)(2,1)S(1)}, u32[]{:S(2)}, u32[]{:S(2)}) collective-permute-start(bf16[128,768]{1,0:T(8,128)(2,1)S(1)} %collective-permute-done.10.refs_10_), channel_id=1, source_target_pairs={{0,1},{1,0},{2,3},{3,2},{4,5},{5,4},{6,7},{7,6},{8,9},{9,8},{10,11... | collective-permute-start | bytes 589832 | tf_op jit(solution)/shard_map/ppermute | solution.py:50
  23.8 3.8 %collective-permute-start.1 = (s32[4]{0:T(128)}, s32[4]{0:T(128)S(1)}, u32[]{:S(2)}, u32[]{:S(2)}) collective-permute-start(s32[4]{0:T(128)} %refs_0_.1), channel_id=1, source_target_pairs={{0,16},{1,17},{2,18},{3,19},{4,20},{5,21},{6,22},{7,23},{8,24},{9,... | collective-permute-start | bytes 56 | tf_op jit(solution)/shard_map/ppermute | solution.py:50
  23.9 3.8 %collective-permute-start.2 = (s32[4]{0:T(128)S(1)}, s32[4]{0:T(128)S(1)}, u32[]{:S(2)}, u32[]{:S(2)}) collective-permute-start(s32[4]{0:T(128)S(1)} %collective-permute-done.refs_1_), channel_id=1, source_target_pairs={{0,16},{1,17},{2,18},{3,19},{4,20},{5,21},{6,22},{7,23},{8,24},{9,... | collective-permute-start | bytes 56 | tf_op jit(solution)/shard_map/ppermute | solution.py:50
  25.9 5.7 %collective-permute-start.21 = (bf16[128,768]{1,0:T(8,128)(2,1)S(1)}, bf16[128,768]{1,0:T(8,128)(2,1)S(1)}, u32[]{:S(2)}, u32[]{:S(2)}) collective-permute-start(bf16[128,768]{1,0:T(8,128)(2,1)S(1)} %collective-permute-done.20.refs_20_), channel_id=1, source_target_pairs={{0,1},{1,0},{2,3},{3,2},{4,5},{5,4},{6,7},{7,6},{8,9},{9,8},{10,11... | collective-permute-start | bytes 589832 | tf_op jit(solution)/shard_map/ppermute | solution.py:50
  27.5 9.7 %collective-permute-start.12 = (bf16[256,768]{1,0:T(8,128)(2,1)S(1)}, bf16[256,768]{1,0:T(8,128)(2,1)S(1)}, u32[]{:S(2)}, u32[]{:S(2)}) collective-permute-start(bf16[256,768]{1,0:T(8,128)(2,1)S(1)} %pad_maximum_fusion), channel_id=1, source_target_pairs={{0,16},{1,3},{2,18},{3,1},{4,20},{5,7},{6,22},{7,5},{8,24},{9,11},... | collective-permute-start | bytes 1179656 | tf_op jit(solution)/shard_map/ppermute | solution.py:50
  27.6 11.9 %collective-permute-start.18 = (bf16[256,768]{1,0:T(8,128)(2,1)S(1)}, bf16[256,768]{1,0:T(8,128)(2,1)S(1)}, u32[]{:S(2)}, u32[]{:S(2)}) collective-permute-start(bf16[256,768]{1,0:T(8,128)(2,1)S(1)} %pad_maximum_fusion.2), channel_id=1, source_target_pairs={{0,16},{1,3},{2,18},{3,1},{4,20},{5,7},{6,22},{7,5},{8,24},{9,11},... | collective-permute-start | bytes 1179656 | tf_op jit(solution)/shard_map/ppermute | solution.py:50
  29.6 14.2 %collective-permute-start.14 = (bf16[256,768]{1,0:T(8,128)(2,1)S(1)}, bf16[256,768]{1,0:T(8,128)(2,1)S(1)}, u32[]{:S(2)}, u32[]{:S(2)}) collective-permute-start(bf16[256,768]{1,0:T(8,128)(2,1)S(1)} %pad_maximum_fusion.1), channel_id=1, source_target_pairs={{0,16},{1,3},{2,18},{3,1},{4,20},{5,7},{6,22},{7,5},{8,24},{9,11},... | collective-permute-start | bytes 1179656 | tf_op jit(solution)/shard_map/ppermute | solution.py:50
  29.7 18.3 %collective-permute-start.22 = (bf16[256,768]{1,0:T(8,128)(2,1)S(1)}, bf16[256,768]{1,0:T(8,128)(2,1)S(1)}, u32[]{:S(2)}, u32[]{:S(2)}) collective-permute-start(bf16[256,768]{1,0:T(8,128)(2,1)S(1)} %pad_maximum_fusion.3), channel_id=1, source_target_pairs={{0,16},{1,3},{2,18},{3,1},{4,20},{5,7},{6,22},{7,5},{8,24},{9,11},... | collective-permute-start | bytes 1179656 | tf_op jit(solution)/shard_map/ppermute | solution.py:50
  31.6 5.7 %collective-permute-start.24 = (bf16[128,768]{1,0:T(8,128)(2,1)S(1)}, bf16[128,768]{1,0:T(8,128)(2,1)S(1)}, u32[]{:S(2)}, u32[]{:S(2)}) collective-permute-start(bf16[128,768]{1,0:T(8,128)(2,1)S(1)} %collective-permute-done.16.refs_16_), channel_id=1, source_target_pairs={{0,4},{1,5},{2,6},{3,7},{4,8},{5,9},{6,10},{7,11},{8,12},{9,13},{1... | collective-permute-start | bytes 589832 | tf_op jit(solution)/shard_map/ppermute | solution.py:50
  37.3 10.7 %collective-permute-start.17 = (bf16[128,768]{1,0:T(8,128)(2,1)S(1)}, bf16[128,768]{1,0:T(8,128)(2,1)S(1)}, u32[]{:S(2)}, u32[]{:S(2)}) collective-permute-start(bf16[128,768]{1,0:T(8,128)(2,1)S(1)} %collective-permute-done.16.refs_16_), channel_id=1, source_target_pairs={{0,1},{1,0},{2,3},{3,2},{4,5},{5,4},{6,7},{7,6},{8,9},{9,8},{10,11... | collective-permute-start | bytes 589832 | tf_op jit(solution)/shard_map/ppermute | solution.py:50
  37.3 18.6 %collective-permute-start.13 = (bf16[256,768]{1,0:T(8,128)(2,1)S(1)}, bf16[256,768]{1,0:T(8,128)(2,1)S(1)}, u32[]{:S(2)}, u32[]{:S(2)}) collective-permute-start(bf16[256,768]{1,0:T(8,128)(2,1)S(1)} %collective-permute-done.12.refs_12_), channel_id=1, source_target_pairs={{0,1},{1,0},{2,3},{3,2},{4,5},{5,4},{6,7},{7,6},{8,9},{9,8},{10,11... | collective-permute-start | bytes 1179656 | tf_op jit(solution)/shard_map/ppermute | solution.py:50
  39.5 16.4 %collective-permute-start.19 = (bf16[256,768]{1,0:T(8,128)(2,1)S(1)}, bf16[256,768]{1,0:T(8,128)(2,1)S(1)}, u32[]{:S(2)}, u32[]{:S(2)}) collective-permute-start(bf16[256,768]{1,0:T(8,128)(2,1)S(1)} %collective-permute-done.18.refs_18_), channel_id=1, source_target_pairs={{0,1},{1,0},{2,3},{3,2},{4,5},{5,4},{6,7},{7,6},{8,9},{9,8},{10,11... | collective-permute-start | bytes 1179656 | tf_op jit(solution)/shard_map/ppermute | solution.py:50
  43.7 12.2 %collective-permute-start.15 = (bf16[256,768]{1,0:T(8,128)(2,1)S(1)}, bf16[256,768]{1,0:T(8,128)(2,1)S(1)}, u32[]{:S(2)}, u32[]{:S(2)}) collective-permute-start(bf16[256,768]{1,0:T(8,128)(2,1)S(1)} %collective-permute-done.14.refs_14_), channel_id=1, source_target_pairs={{0,1},{1,0},{2,3},{3,2},{4,5},{5,4},{6,7},{7,6},{8,9},{9,8},{10,11... | collective-permute-start | bytes 1179656 | tf_op jit(solution)/shard_map/ppermute | solution.py:50
  48.0 8.0 %collective-permute-start.23 = (bf16[256,768]{1,0:T(8,128)(2,1)S(1)}, bf16[256,768]{1,0:T(8,128)(2,1)S(1)}, u32[]{:S(2)}, u32[]{:S(2)}) collective-permute-start(bf16[256,768]{1,0:T(8,128)(2,1)S(1)} %collective-permute-done.22.refs_22_), channel_id=1, source_target_pairs={{0,1},{1,0},{2,3},{3,2},{4,5},{5,4},{6,7},{7,6},{8,9},{9,8},{10,11... | collective-permute-start | bytes 1179656 | tf_op jit(solution)/shard_map/ppermute | solution.py:50
  48.0 7.9 %collective-permute-start.25 = (bf16[128,768]{1,0:T(8,128)(2,1)S(1)}, bf16[128,768]{1,0:T(8,128)(2,1)S(1)}, u32[]{:S(2)}, u32[]{:S(2)}) collective-permute-start(bf16[128,768]{1,0:T(8,128)(2,1)S(1)} %collective-permute-done.24.refs_24_), channel_id=1, source_target_pairs={{0,1},{1,0},{2,3},{3,2},{4,5},{5,4},{6,7},{7,6},{8,9},{9,8},{10,11... | collective-permute-start | bytes 589832 | tf_op jit(solution)/shard_map/ppermute | solution.py:50
  48.5 0.9 %copy-start = (s32[64,4,256]{2,1,0:T(4,128)S(1)}, s32[64,4,256]{2,1,0:T(4,128)}, u32[]{:S(2)}) copy-start(s32[64,4,256]{2,1,0:T(4,128)} %refs_5_.1) | copy-start | bytes 786436
  49.4 0.7 %copy-start.1 = (s32[32,1,128]{2,1,0:T(1,128)S(1)}, s32[32,1,128]{2,1,0:T(1,128)}, u32[]{:S(2)}) copy-start(s32[32,1,128]{2,1,0:T(1,128)} %constant.2.clone.refs_4_) | copy-start | bytes 49156
  50.1 0.7 %copy-start.2 = (s32[4]{0:T(128)S(1)}, s32[4]{0:T(128)}, u32[]{:S(2)}) copy-start(s32[4]{0:T(128)} %refs_0_.1) | copy-start | bytes 52

commit v2 on v1

--- a/solution.py
+++ b/solution.py
@@ -22,8 +22,8 @@
         return (self.rep, self.slab, self.pix) == (2, 8, 2)
 
     def target(self, port, rep, slab, pix):
-        if port == "x|y":
-            port = "y" if pix else "x"
+        if "|" in port:
+            port = port.split("|")[pix]
         if port in ("x", "xy"):
             rep = 1 - rep
         if port in ("y", "xy"):
@@ -50,6 +50,24 @@
         value = lax.ppermute(value, ("rep", "slab", "pix"), self.pairs(port))
         return value, [self.move(owner, port) for owner in owners]
 
+    def distances(self, owners):
+        found = []
+        for piece in range(owners.shape[-1]):
+            per_core = []
+            for pix in range(self.pix):
+                rep, slab, core = np.unravel_index(owners[0, 0, pix, piece], self.ids.shape)
+                per_core.append((int(rep), int(slab // 2), int(slab % 2), int(core) ^ pix))
+            for at in np.ndindex(self.ids.shape):
+                rep, slab, core = self.owner(per_core[at[2]], *at)
+                assert self.ids[rep, slab, core] == owners[at][piece]
+            found.append(per_core)
+        return found
+
+    def owner(self, distance, rep, slab, pix):
+        far_x, far_z, far_y, far_core = distance
+        upper = (slab // 2 + far_z) & (self.slab // 2 - 1)
+        return rep ^ far_x, upper * 2 + ((slab & 1) ^ far_y), pix ^ far_core
+
     def both(self, held):
         other = self.send(held, "core")
         return other, (jnp.concatenate([held[0], other[0]], axis=0), held[1] + other[1])
@@ -64,7 +82,8 @@
     across = ports.send(own, "xy")
     orients = [(orient, [ports.ids])]
     orients.append(ports.send(orients[0], "core"))
-    orients += [ports.send(orients[0], "x"), ports.send(orients[1], "x")]
+    orients += [ports.send(orients[0], "x")]
+    orients.append(ports.send(orients[2], "core"))
     core_up1, chip_up1 = ports.both(up1)
     up2 = ports.send(up1, "z")
     side1 = ports.send(chip_up1, "x|y")
@@ -74,7 +93,7 @@
     across3 = ports.send(across, "back")
     core_up2, chip_up2 = ports.both(up2)
     side2 = ports.send(chip_up2, "x|y")
-    across2 = ports.send(across1, "z")
+    across2 = ports.send(up2, "xy")
     pieces = [own, core_own, up1, core_up1, up2, core_up2, down, core_down]
     late = (across, side0, side1, across1, side3, across3, side2, across2)
     for held in late:
@@ -99,9 +118,9 @@
     return size.bit_length() - 1
 
 
-def make_plan(orients, place, table, pieces_n, sizes):
+def make_plan(ports, orients, orders, table, distances, sizes):
     batch, planes, columns, count_x, row_block, batches = sizes
-    parts = len(orients)
+    parts, pieces_n = len(orients), len(distances)
     items = batch * planes // GROUP
     segments = pieces_n * items
     steps, lane_groups = count_x // row_block, LANES // GROUP
@@ -111,14 +130,21 @@
 
     def kernel(*refs):
         orient_refs = refs[:parts]
-        place_all, table_ref, info_ref, where_ref, place_ref, raw, geometry, found, found_s, listed, sems = refs[parts:]
-        me = (lax.axis_index("rep") * lax.axis_size("slab") + lax.axis_index("slab")) * lax.axis_size("pix")
-        me += lax.axis_index("pix")
-        rep, pix = lax.axis_index("rep"), lax.axis_index("pix")
-        first_x = (rep * lax.axis_size("pix") + pix) * count_x
-        first_z = lax.axis_index("slab") * planes
-        placing = pltpu.make_async_copy(place_all.at[me, 0], place_ref, sems.at[total_n])
-        placing.start()
+        table_ref, info_ref, where_ref, raw, geometry, found, found_s, listed, sems = refs[parts:]
+        rep, slab, pix = (lax.axis_index(axis) for axis in ("rep", "slab", "pix"))
+        first_x = (rep * ports.pix + pix) * count_x
+        first_z = slab * planes
+        known = {}
+
+        def place(per_core):
+            for distance in per_core:
+                if distance not in known:
+                    at_rep, at_slab, at_pix = ports.owner(distance, rep, slab, pix)
+                    known[distance] = (at_rep * ports.pix + at_pix) * batch, at_slab * (planes // GROUP)
+            if len(set(per_core)) == 1:
+                return known[per_core[0]]
+            return [jnp.where(pix == 0, first, second) for first, second in zip(*(known[d] for d in per_core))]
+
         copies = [
             pltpu.make_async_copy(
                 table_ref.at[orient_refs[n // batch][n % batch]], raw.at[n], sems.at[n]
@@ -127,13 +153,12 @@
         ]
         for copy in copies:
             copy.start()
-        placing.wait()
         for copy in copies:
             copy.wait()
         unit = lax.broadcasted_iota(jnp.int32, (1, 4, columns), 1) & 1
         unit = jnp.where(unit[0] == 1, 1.0 / 256.0, 1.0)
         for n in range(total_n):
-            geometry[place_ref[n], 0:4, :] = raw[n].astype(jnp.float32) * unit
+            geometry[place(orders[n // batch])[0] + n % batch, 0:4, :] = raw[n].astype(jnp.float32) * unit
         near_x = geometry[:, 0, :] - first_x.astype(jnp.float32)
         near_z = geometry[:, 2, :] - first_z.astype(jnp.float32)
         hit_z = (near_z >= -1.0) & (near_z < planes)
@@ -170,8 +195,7 @@
 
         count = jnp.int32(0)
         for piece in range(pieces_n):
-            first_n = place_ref[total_n + 2 * piece]
-            first_g = place_ref[total_n + 2 * piece + 1]
+            first_n, first_g = place(distances[piece])
             for item in range(items):
                 n, g = first_n + item // (items // batch), first_g + item % (items // batch)
                 code = found_s[n, g]
@@ -210,20 +234,19 @@
             jax.ShapeDtypeStruct((info_size,), jnp.int32),
             jax.ShapeDtypeStruct((8, segments * GROUP), jnp.float32),
         ],
-        in_specs=[smem] * parts + [pl.BlockSpec(memory_space=pltpu.HBM)] * 2,
+        in_specs=[smem] * parts + [pl.BlockSpec(memory_space=pl.ANY)],
         out_specs=[smem, vmem],
         scratch_shapes=[
-            pltpu.SMEM(place.shape[2:], jnp.int32),
             pltpu.VMEM((total_n, 4, columns), jnp.int32),
             pltpu.VMEM((total_n, 8, columns), jnp.float32),
             pltpu.VMEM((total_n, LANES), jnp.int32),
             pltpu.SMEM((total_n, LANES), jnp.int32),
             pltpu.SMEM((segments + 1,), jnp.int32),
-            pltpu.SemaphoreType.DMA((total_n + 1,)),
+            pltpu.SemaphoreType.DMA((total_n,)),
         ],
         compiler_params=pltpu.CompilerParams(vmem_limit_bytes=4 << 20),
         name="plan",
-    )(*orients, place, table)
+    )(*orients, table)
 
 
 def spread(pieces, info, where, sizes):
@@ -345,16 +368,9 @@
         sizes = (batch, planes, columns, count_x, row_block, ports.rep * ports.pix)
         samples = jnp.concatenate([projections, ctf_weight], axis=2).reshape(batch * planes, 3 * columns)
         pieces, owners, orients, orient_owners = gather_pieces(samples, orient, ports)
-        place = []
-        for owner in (orient_owners, owners):
-            rep, slab, pix = np.unravel_index(owner, ports.ids.shape)
-            place.append(((rep * ports.pix + pix) * batch, slab * (planes // GROUP)))
-        (order, _), (first_n, first_g) = place
-        order = order[..., None] + np.arange(batch)
-        place = [order.reshape(ports.ids.size, -1), np.stack([first_n, first_g], -1).reshape(ports.ids.size, -1)]
-        place = np.concatenate(place, axis=1)
-        place = np.pad(place, ((0, 0), (0, -place.shape[1] % LANES)))[:, None]
-        info, where = make_plan(orients, jnp.asarray(place, jnp.int32), angle_table, owners.shape[-1], sizes)
+        info, where = make_plan(
+            ports, orients, ports.distances(orient_owners), angle_table, ports.distances(owners), sizes
+        )
         return spread(pieces, info, where, sizes)
 
     return body

time: 63.6 us -> 63.1 us (level)
  waiting for transfers between devices: 30.3 us -> 33.3 us
  starting transfers between devices: 17.1 us -> 14.9 us
  local copies, waits for them, and re-layouts: 2.32 us -> 1.61 us
    ppermute x26, waiting for transfers between devices: 30.3 us -> 33.3 us  [send(): value = lax.ppermute(value, ('rep', 'slab', 'pix'), self.pairs(port))]
    ppermute x26, starting transfers between devices: 17.1 us -> 14.9 us  [send(): value = lax.ppermute(value, ('rep', 'slab', 'pix'), self.pairs(port))]
    unnamed x6 -> x4, local copies, waits for them, and re-layouts: 2.32 us -> 1.61 us
  transfers between devices with their start and end apart: 26 -> 26, of which waited for: 8 -> 10; matrix products, arithmetic and copies ran while one was open for 0% -> 0% of each run, Pallas kernels for 8% -> 7%
where the time goes in v2:
time: 63.1 us; the launch traced here: 62.9 us
  waiting for transfers between devices  33.3 us (53%)
  starting transfers between devices  14.9 us (24%)
  Pallas kernels  12 us (19%)
  local copies, waits for them, and re-layouts  1.61 us (3%)
  other arithmetic  1.06 us (2%)
    ppermute x26, waiting for transfers between devices, send(): value = lax.ppermute(value, ('rep', 'slab', 'pix'), self.pairs(port))  33.3 us
    ppermute x26, starting transfers between devices, send(): value = lax.ppermute(value, ('rep', 'slab', 'pix'), self.pairs(port))  14.9 us
    pallas_call x1, Pallas kernels, spread(): pl.pallas_call(kernel, out_shape=jax.ShapeDtypeStruct((count_x, planes, 2...  7.43 us
    pallas_call x1, Pallas kernels, make_plan(): pl.pallas_call(kernel, out_shape=[jax.ShapeDtypeStruct((info_size,), jnp....  4.58 us
    unnamed x4, local copies, waits for them, and re-layouts  1.61 us
  transfers between devices with their start and end apart: 26, of which 10 were waited for; matrix products, arithmetic and copies ran while one was open for 0% of the time, Pallas kernels for 7%

profile of v2, /device:TPU:18, one launch (start us, length us, event | category | flops | bytes accessed | tf_op | source)
XLA Modules:
  0.0 62.9 jit_solution(8198126063972465673)
XLA Ops:
  0.0 1.0 %pad_maximum_fusion.4 = bf16[4,32,768]{2,1,0:T(8,128)(2,1)S(1)} fusion(bf16[4,32,256]{2,1,0:T(8,128)(2,1)} %param.5, bf16[4,32,512]{2,1,0:T(8,128)(2,1)} %param.4), kind=kLoop, calls=%fused_computation.4 | loop fusion | flops 393216 | bytes 393216 | tf_op jit(solution)/shard_map/concatenate | solution.py:369
  1.0 1.6 %collective-permute-start.4 = (bf16[128,768]{1,0:T(8,128)(2,1)S(1)}, bf16[128,768]{1,0:T(8,128)(2,1)S(1)}, u32[]{:S(2)}, u32[]{:S(2)}) collective-permute-start(bf16[128,768]{1,0:T(8,128)(2,1)S(1)} %bitcast.1), channel_id=1, source_target_pairs={{0,4},{1,5},{2,6},{3,7},{4,8},{5,9},{6,10},{7,11},{8,12},{9,13},{1... | collective-permute-start | bytes 589832 | tf_op jit(solution)/shard_map/ppermute | solution.py:50
  2.6 1.5 %collective-permute-start.10 = (bf16[128,768]{1,0:T(8,128)(2,1)S(1)}, bf16[128,768]{1,0:T(8,128)(2,1)S(1)}, u32[]{:S(2)}, u32[]{:S(2)}) collective-permute-start(bf16[128,768]{1,0:T(8,128)(2,1)S(1)} %bitcast.2), channel_id=1, source_target_pairs={{0,18},{1,19},{2,16},{3,17},{4,22},{5,23},{6,20},{7,21},{8,26},{9,... | collective-permute-start | bytes 589832 | tf_op jit(solution)/shard_map/ppermute | solution.py:50
  4.1 0.4 collective-permute-start.8
  4.5 0.0 collective-permute-start.3
  4.5 6.5 %collective-permute-done.4.refs_4_ = bf16[128,768]{1,0:T(8,128)(2,1)S(1)} collective-permute-done((bf16[128,768]{1,0:T(8,128)(2,1)S(1)}, bf16[128,768]{1,0:T(8,128)(2,1)S(1)}, u32[]{:S(2)}, u32[]{:S(2)}) %collective-permute-start.4) | collective-permute-done | bytes 196640 | tf_op jit(solution)/shard_map/ppermute | solution.py:50
  11.1 1.9 %collective-permute-start.6 = (bf16[128,768]{1,0:T(8,128)(2,1)S(1)}, bf16[128,768]{1,0:T(8,128)(2,1)S(1)}, u32[]{:S(2)}, u32[]{:S(2)}) collective-permute-start(bf16[128,768]{1,0:T(8,128)(2,1)S(1)} %collective-permute-done.4.refs_4_), channel_id=1, source_target_pairs={{0,4},{1,5},{2,6},{3,7},{4,8},{5,9},{6,10},{7,11},{8,12},{9,13},{1... | collective-permute-start | bytes 589832 | tf_op jit(solution)/shard_map/ppermute | solution.py:50
  13.0 0.0 collective-permute-start.1
  13.0 1.0 %collective-permute-start.20 = (bf16[128,768]{1,0:T(8,128)(2,1)S(1)}, bf16[128,768]{1,0:T(8,128)(2,1)S(1)}, u32[]{:S(2)}, u32[]{:S(2)}) collective-permute-start(bf16[128,768]{1,0:T(8,128)(2,1)S(1)} %collective-permute-done.10.refs_10_), channel_id=1, source_target_pairs={{0,12},{1,13},{2,14},{3,15},{4,0},{5,1},{6,2},{7,3},{8,4},{9,5},{1... | collective-permute-start | bytes 589832 | tf_op jit(solution)/shard_map/ppermute | solution.py:50
  14.0 6.2 %collective-permute-done.6.refs_6_ = bf16[128,768]{1,0:T(8,128)(2,1)S(1)} collective-permute-done((bf16[128,768]{1,0:T(8,128)(2,1)S(1)}, bf16[128,768]{1,0:T(8,128)(2,1)S(1)}, u32[]{:S(2)}, u32[]{:S(2)}) %collective-permute-start.6) | collective-permute-done | bytes 196640 | tf_op jit(solution)/shard_map/ppermute | solution.py:50
  20.2 3.0 %collective-permute-start.16 = (bf16[128,768]{1,0:T(8,128)(2,1)S(1)}, bf16[128,768]{1,0:T(8,128)(2,1)S(1)}, u32[]{:S(2)}, u32[]{:S(2)}) collective-permute-start(bf16[128,768]{1,0:T(8,128)(2,1)S(1)} %collective-permute-done.10.refs_10_), channel_id=1, source_target_pairs={{0,4},{1,5},{2,6},{3,7},{4,8},{5,9},{6,10},{7,11},{8,12},{9,13},{1... | collective-permute-start | bytes 589832 | tf_op jit(solution)/shard_map/ppermute | solution.py:50
  23.2 0.6 collective-permute-start.11
  23.8 0.1 collective-permute-start
  23.9 0.5 collective-permute-start.2
  24.4 0.2 collective-permute-done.7.refs_7_
  24.6 0.1 collective-permute-start.21
  24.7 0.4 collective-permute-done.refs_1_
  25.2 0.0 collective-permute-done.2.refs_3_
  25.2 2.0 %collective-permute-start.18 = (bf16[256,768]{1,0:T(8,128)(2,1)S(1)}, bf16[256,768]{1,0:T(8,128)(2,1)S(1)}, u32[]{:S(2)}, u32[]{:S(2)}) collective-permute-start(bf16[256,768]{1,0:T(8,128)(2,1)S(1)} %pad_maximum_fusion.2), channel_id=1, source_target_pairs={{0,16},{1,3},{2,18},{3,1},{4,20},{5,7},{6,22},{7,5},{8,24},{9,11},... | collective-permute-start | bytes 1179656 | tf_op jit(solution)/shard_map/ppermute | solution.py:50
  27.2 0.1 collective-permute-start.14
  27.3 2.0 %collective-permute-start.22 = (bf16[256,768]{1,0:T(8,128)(2,1)S(1)}, bf16[256,768]{1,0:T(8,128)(2,1)S(1)}, u32[]{:S(2)}, u32[]{:S(2)}) collective-permute-start(bf16[256,768]{1,0:T(8,128)(2,1)S(1)} %pad_maximum_fusion.3), channel_id=1, source_target_pairs={{0,16},{1,3},{2,18},{3,1},{4,20},{5,7},{6,22},{7,5},{8,24},{9,11},... | collective-permute-start | bytes 1179656 | tf_op jit(solution)/shard_map/ppermute | solution.py:50
  29.2 1.4 %collective-permute-done.17.refs_17_ = bf16[128,768]{1,0:T(8,128)(2,1)S(1)} collective-permute-done((bf16[128,768]{1,0:T(8,128)(2,1)S(1)}, bf16[128,768]{1,0:T(8,128)(2,1)S(1)}, u32[]{:S(2)}, u32[]{:S(2)}) %collective-permute-start.17) | collective-permute-done | bytes 196640 | tf_op jit(solution)/shard_map/ppermute | solution.py:50
  30.7 0.1 collective-permute-start.24
  30.8 2.2 %collective-permute-done.12.refs_12_ = bf16[256,768]{1,0:T(8,128)(2,1)S(1)} collective-permute-done((bf16[256,768]{1,0:T(8,128)(2,1)S(1)}, bf16[256,768]{1,0:T(8,128)(2,1)S(1)}, u32[]{:S(2)}, u32[]{:S(2)}) %collective-permute-start.12) | collective-permute-done | bytes 393248 | tf_op jit(solution)/shard_map/ppermute | solution.py:50
  33.0 6.3 %collective-permute-done.18.refs_18_ = bf16[256,768]{1,0:T(8,128)(2,1)S(1)} collective-permute-done((bf16[256,768]{1,0:T(8,128)(2,1)S(1)}, bf16[256,768]{1,0:T(8,128)(2,1)S(1)}, u32[]{:S(2)}, u32[]{:S(2)}) %collective-permute-start.18) | collective-permute-done | bytes 393248 | tf_op jit(solution)/shard_map/ppermute | solution.py:50
  39.3 4.2 %collective-permute-done.14.refs_14_ = bf16[256,768]{1,0:T(8,128)(2,1)S(1)} collective-permute-done((bf16[256,768]{1,0:T(8,128)(2,1)S(1)}, bf16[256,768]{1,0:T(8,128)(2,1)S(1)}, u32[]{:S(2)}, u32[]{:S(2)}) %collective-permute-start.14) | collective-permute-done | bytes 393248 | tf_op jit(solution)/shard_map/ppermute | solution.py:50
  43.5 4.2 %collective-permute-done.22.refs_22_ = bf16[256,768]{1,0:T(8,128)(2,1)S(1)} collective-permute-done((bf16[256,768]{1,0:T(8,128)(2,1)S(1)}, bf16[256,768]{1,0:T(8,128)(2,1)S(1)}, u32[]{:S(2)}, u32[]{:S(2)}) %collective-permute-start.22) | collective-permute-done | bytes 393248 | tf_op jit(solution)/shard_map/ppermute | solution.py:50
  47.7 1.6 %collective-permute-done.24.refs_24_ = bf16[128,768]{1,0:T(8,128)(2,1)S(1)} collective-permute-done((bf16[128,768]{1,0:T(8,128)(2,1)S(1)}, bf16[128,768]{1,0:T(8,128)(2,1)S(1)}, u32[]{:S(2)}, u32[]{:S(2)}) %collective-permute-start.24) | collective-permute-done | bytes 196640 | tf_op jit(solution)/shard_map/ppermute | solution.py:50
  49.3 0.9 %copy-done = s32[64,4,256]{2,1,0:T(4,128)S(1)} copy-done((s32[64,4,256]{2,1,0:T(4,128)S(1)}, s32[64,4,256]{2,1,0:T(4,128)}, u32[]{:S(2)}) %copy-start) | copy-done | bytes 262168
  50.2 0.7 %copy-done.1 = s32[4]{0:T(128)S(1)} copy-done((s32[4]{0:T(128)S(1)}, s32[4]{0:T(128)}, u32[]{:S(2)}) %copy-start.1) | copy-done | bytes 40
  50.9 4.6 %plan.1 = (s32[273]{0:T(512)S(1)}, f32[8,4096]{1,0:T(8,128)S(1)}) custom-call(s32[4]{0:T(128)S(1)} %copy-done.1, s32[4]{0:T(128)S(1)} %collective-permute-done.refs_1_, s32[4]{0:T(128)S(1)} %collective-permute-done.1.refs_2_, s32[4]{0:T(128)S(1)} %collective-permute-done.2.refs_3_, s32[64,4,256]{2,1,0:T(4,128)S(1)} %copy-done), custom_call_target="tpu_custom_call" | custom-call | tf_op jit(solution)/shard_map/plan/pallas_call | solution.py:231
  55.5 7.4 %spread.1 = f32[64,32,512]{2,1,0:T(8,128)} custom-call(s32[273]{0:T(512)S(1)} %get-tuple-element.7.refs_0_, f32[8,4096]{1,0:T(8,128)S(1)} %get-tuple-element.8.refs_1_, bf16[128,768]{1,0:T(8,128)(2,1)S(1)} %bitcast.6, bf16[128,768]{1,0:T(8,128)(2,1)S(1)} %collective-permute-done.3.refs_3_, bf16[128,768]{1,0:T(8,128)(2,1)S(1)} %collective-permute-done.4.refs_4_, ...), custom_call_target="tpu_custom_call" | custom-call | tf_op jit(solution)/shard_map/spread/pallas_call | solution.py:346
  (31 shorter events, 0.2 us)
Async XLA Ops:
  1.0 10.1 %collective-permute-start.4 = (bf16[128,768]{1,0:T(8,128)(2,1)S(1)}, bf16[128,768]{1,0:T(8,128)(2,1)S(1)}, u32[]{:S(2)}, u32[]{:S(2)}) collective-permute-start(bf16[128,768]{1,0:T(8,128)(2,1)S(1)} %bitcast.1), channel_id=1, source_target_pairs={{0,4},{1,5},{2,6},{3,7},{4,8},{5,9},{6,10},{7,11},{8,12},{9,13},{1... | collective-permute-start | bytes 589832 | tf_op jit(solution)/shard_map/ppermute | solution.py:50
  2.6 10.4 %collective-permute-start.10 = (bf16[128,768]{1,0:T(8,128)(2,1)S(1)}, bf16[128,768]{1,0:T(8,128)(2,1)S(1)}, u32[]{:S(2)}, u32[]{:S(2)}) collective-permute-start(bf16[128,768]{1,0:T(8,128)(2,1)S(1)} %bitcast.2), channel_id=1, source_target_pairs={{0,18},{1,19},{2,16},{3,17},{4,22},{5,23},{6,20},{7,21},{8,26},{9,... | collective-permute-start | bytes 589832 | tf_op jit(solution)/shard_map/ppermute | solution.py:50
  4.1 8.9 %collective-permute-start.8 = (bf16[128,768]{1,0:T(8,128)(2,1)S(1)}, bf16[128,768]{1,0:T(8,128)(2,1)S(1)}, u32[]{:S(2)}, u32[]{:S(2)}) collective-permute-start(bf16[128,768]{1,0:T(8,128)(2,1)S(1)} %bitcast.3), channel_id=1, source_target_pairs={{0,12},{1,13},{2,14},{3,15},{4,0},{5,1},{6,2},{7,3},{8,4},{9,5},{1... | collective-permute-start | bytes 589832 | tf_op jit(solution)/shard_map/ppermute | solution.py:50
  4.5 9.4 %collective-permute-start.3 = (bf16[128,768]{1,0:T(8,128)(2,1)S(1)}, bf16[128,768]{1,0:T(8,128)(2,1)S(1)}, u32[]{:S(2)}, u32[]{:S(2)}) collective-permute-start(bf16[128,768]{1,0:T(8,128)(2,1)S(1)} %bitcast.4), channel_id=1, source_target_pairs={{0,1},{1,0},{2,3},{3,2},{4,5},{5,4},{6,7},{7,6},{8,9},{9,8},{10,11... | collective-permute-start | bytes 589832 | tf_op jit(solution)/shard_map/ppermute | solution.py:50
  11.1 9.1 %collective-permute-start.6 = (bf16[128,768]{1,0:T(8,128)(2,1)S(1)}, bf16[128,768]{1,0:T(8,128)(2,1)S(1)}, u32[]{:S(2)}, u32[]{:S(2)}) collective-permute-start(bf16[128,768]{1,0:T(8,128)(2,1)S(1)} %collective-permute-done.4.refs_4_), channel_id=1, source_target_pairs={{0,4},{1,5},{2,6},{3,7},{4,8},{5,9},{6,10},{7,11},{8,12},{9,13},{1... | collective-permute-start | bytes 589832 | tf_op jit(solution)/shard_map/ppermute | solution.py:50
  13.0 10.2 %collective-permute-start.5 = (bf16[128,768]{1,0:T(8,128)(2,1)S(1)}, bf16[128,768]{1,0:T(8,128)(2,1)S(1)}, u32[]{:S(2)}, u32[]{:S(2)}) collective-permute-start(bf16[128,768]{1,0:T(8,128)(2,1)S(1)} %collective-permute-done.4.refs_4_), channel_id=1, source_target_pairs={{0,1},{1,0},{2,3},{3,2},{4,5},{5,4},{6,7},{7,6},{8,9},{9,8},{10,11... | collective-permute-start | bytes 589832 | tf_op jit(solution)/shard_map/ppermute | solution.py:50
  13.0 10.8 %collective-permute-start.1 = (s32[4]{0:T(128)}, s32[4]{0:T(128)S(1)}, u32[]{:S(2)}, u32[]{:S(2)}) collective-permute-start(s32[4]{0:T(128)} %refs_0_.1), channel_id=1, source_target_pairs={{0,16},{1,17},{2,18},{3,19},{4,20},{5,21},{6,22},{7,23},{8,24},{9,... | collective-permute-start | bytes 56 | tf_op jit(solution)/shard_map/ppermute | solution.py:50
  13.0 10.9 %collective-permute-start.20 = (bf16[128,768]{1,0:T(8,128)(2,1)S(1)}, bf16[128,768]{1,0:T(8,128)(2,1)S(1)}, u32[]{:S(2)}, u32[]{:S(2)}) collective-permute-start(bf16[128,768]{1,0:T(8,128)(2,1)S(1)} %collective-permute-done.10.refs_10_), channel_id=1, source_target_pairs={{0,12},{1,13},{2,14},{3,15},{4,0},{5,1},{6,2},{7,3},{8,4},{9,5},{1... | collective-permute-start | bytes 589832 | tf_op jit(solution)/shard_map/ppermute | solution.py:50
  13.9 9.2 %collective-permute-start.9 = (bf16[128,768]{1,0:T(8,128)(2,1)S(1)}, bf16[128,768]{1,0:T(8,128)(2,1)S(1)}, u32[]{:S(2)}, u32[]{:S(2)}) collective-permute-start(bf16[128,768]{1,0:T(8,128)(2,1)S(1)} %collective-permute-done.8.refs_8_), channel_id=1, source_target_pairs={{0,1},{1,0},{2,3},{3,2},{4,5},{5,4},{6,7},{7,6},{8,9},{9,8},{10,11... | collective-permute-start | bytes 589832 | tf_op jit(solution)/shard_map/ppermute | solution.py:50
  20.2 7.0 %collective-permute-start.16 = (bf16[128,768]{1,0:T(8,128)(2,1)S(1)}, bf16[128,768]{1,0:T(8,128)(2,1)S(1)}, u32[]{:S(2)}, u32[]{:S(2)}) collective-permute-start(bf16[128,768]{1,0:T(8,128)(2,1)S(1)} %collective-permute-done.10.refs_10_), channel_id=1, source_target_pairs={{0,4},{1,5},{2,6},{3,7},{4,8},{5,9},{6,10},{7,11},{8,12},{9,13},{1... | collective-permute-start | bytes 589832 | tf_op jit(solution)/shard_map/ppermute | solution.py:50
  23.1 1.4 %collective-permute-start.7 = (bf16[128,768]{1,0:T(8,128)(2,1)S(1)}, bf16[128,768]{1,0:T(8,128)(2,1)S(1)}, u32[]{:S(2)}, u32[]{:S(2)}) collective-permute-start(bf16[128,768]{1,0:T(8,128)(2,1)S(1)} %collective-permute-done.6.refs_6_), channel_id=1, source_target_pairs={{0,1},{1,0},{2,3},{3,2},{4,5},{5,4},{6,7},{7,6},{8,9},{9,8},{10,11... | collective-permute-start | bytes 589832 | tf_op jit(solution)/shard_map/ppermute | solution.py:50
  23.2 4.1 %collective-permute-start.11 = (bf16[128,768]{1,0:T(8,128)(2,1)S(1)}, bf16[128,768]{1,0:T(8,128)(2,1)S(1)}, u32[]{:S(2)}, u32[]{:S(2)}) collective-permute-start(bf16[128,768]{1,0:T(8,128)(2,1)S(1)} %collective-permute-done.10.refs_10_), channel_id=1, source_target_pairs={{0,1},{1,0},{2,3},{3,2},{4,5},{5,4},{6,7},{7,6},{8,9},{9,8},{10,11... | collective-permute-start | bytes 589832 | tf_op jit(solution)/shard_map/ppermute | solution.py:50
  23.8 1.4 %collective-permute-start = (s32[4]{0:T(128)}, s32[4]{0:T(128)S(1)}, u32[]{:S(2)}, u32[]{:S(2)}) collective-permute-start(s32[4]{0:T(128)} %refs_0_.1), channel_id=1, source_target_pairs={{0,1},{1,0},{2,3},{3,2},{4,5},{5,4},{6,7},{7,6},{8,9},{9,8},{10,11... | collective-permute-start | bytes 56 | tf_op jit(solution)/shard_map/ppermute | solution.py:50
  23.9 1.3 %collective-permute-start.2 = (s32[4]{0:T(128)S(1)}, s32[4]{0:T(128)S(1)}, u32[]{:S(2)}, u32[]{:S(2)}) collective-permute-start(s32[4]{0:T(128)S(1)} %collective-permute-done.1.refs_2_), channel_id=1, source_target_pairs={{0,1},{1,0},{2,3},{3,2},{4,5},{5,4},{6,7},{7,6},{8,9},{9,8},{10,11... | collective-permute-start | bytes 56 | tf_op jit(solution)/shard_map/ppermute | solution.py:50
  24.6 4.6 %collective-permute-start.21 = (bf16[128,768]{1,0:T(8,128)(2,1)S(1)}, bf16[128,768]{1,0:T(8,128)(2,1)S(1)}, u32[]{:S(2)}, u32[]{:S(2)}) collective-permute-start(bf16[128,768]{1,0:T(8,128)(2,1)S(1)} %collective-permute-done.20.refs_20_), channel_id=1, source_target_pairs={{0,1},{1,0},{2,3},{3,2},{4,5},{5,4},{6,7},{7,6},{8,9},{9,8},{10,11... | collective-permute-start | bytes 589832 | tf_op jit(solution)/shard_map/ppermute | solution.py:50
  25.2 7.8 %collective-permute-start.12 = (bf16[256,768]{1,0:T(8,128)(2,1)S(1)}, bf16[256,768]{1,0:T(8,128)(2,1)S(1)}, u32[]{:S(2)}, u32[]{:S(2)}) collective-permute-start(bf16[256,768]{1,0:T(8,128)(2,1)S(1)} %pad_maximum_fusion), channel_id=1, source_target_pairs={{0,16},{1,3},{2,18},{3,1},{4,20},{5,7},{6,22},{7,5},{8,24},{9,11},... | collective-permute-start | bytes 1179656 | tf_op jit(solution)/shard_map/ppermute | solution.py:50
  25.2 14.1 %collective-permute-start.18 = (bf16[256,768]{1,0:T(8,128)(2,1)S(1)}, bf16[256,768]{1,0:T(8,128)(2,1)S(1)}, u32[]{:S(2)}, u32[]{:S(2)}) collective-permute-start(bf16[256,768]{1,0:T(8,128)(2,1)S(1)} %pad_maximum_fusion.2), channel_id=1, source_target_pairs={{0,16},{1,3},{2,18},{3,1},{4,20},{5,7},{6,22},{7,5},{8,24},{9,11},... | collective-permute-start | bytes 1179656 | tf_op jit(solution)/shard_map/ppermute | solution.py:50
  27.2 16.3 %collective-permute-start.14 = (bf16[256,768]{1,0:T(8,128)(2,1)S(1)}, bf16[256,768]{1,0:T(8,128)(2,1)S(1)}, u32[]{:S(2)}, u32[]{:S(2)}) collective-permute-start(bf16[256,768]{1,0:T(8,128)(2,1)S(1)} %pad_maximum_fusion.1), channel_id=1, source_target_pairs={{0,16},{1,3},{2,18},{3,1},{4,20},{5,7},{6,22},{7,5},{8,24},{9,11},... | collective-permute-start | bytes 1179656 | tf_op jit(solution)/shard_map/ppermute | solution.py:50
  27.3 20.4 %collective-permute-start.22 = (bf16[256,768]{1,0:T(8,128)(2,1)S(1)}, bf16[256,768]{1,0:T(8,128)(2,1)S(1)}, u32[]{:S(2)}, u32[]{:S(2)}) collective-permute-start(bf16[256,768]{1,0:T(8,128)(2,1)S(1)} %pad_maximum_fusion.3), channel_id=1, source_target_pairs={{0,16},{1,3},{2,18},{3,1},{4,20},{5,7},{6,22},{7,5},{8,24},{9,11},... | collective-permute-start | bytes 1179656 | tf_op jit(solution)/shard_map/ppermute | solution.py:50
  29.2 1.4 %collective-permute-start.17 = (bf16[128,768]{1,0:T(8,128)(2,1)S(1)}, bf16[128,768]{1,0:T(8,128)(2,1)S(1)}, u32[]{:S(2)}, u32[]{:S(2)}) collective-permute-start(bf16[128,768]{1,0:T(8,128)(2,1)S(1)} %collective-permute-done.16.refs_16_), channel_id=1, source_target_pairs={{0,1},{1,0},{2,3},{3,2},{4,5},{5,4},{6,7},{7,6},{8,9},{9,8},{10,11... | collective-permute-start | bytes 589832 | tf_op jit(solution)/shard_map/ppermute | solution.py:50
  30.7 18.6 %collective-permute-start.24 = (bf16[128,768]{1,0:T(8,128)(2,1)S(1)}, bf16[128,768]{1,0:T(8,128)(2,1)S(1)}, u32[]{:S(2)}, u32[]{:S(2)}) collective-permute-start(bf16[128,768]{1,0:T(8,128)(2,1)S(1)} %collective-permute-done.6.refs_6_), channel_id=1, source_target_pairs={{0,18},{1,19},{2,16},{3,17},{4,22},{5,23},{6,20},{7,21},{8,26},{9,... | collective-permute-start | bytes 589832 | tf_op jit(solution)/shard_map/ppermute | solution.py:50
  33.0 22.5 %collective-permute-start.13 = (bf16[256,768]{1,0:T(8,128)(2,1)S(1)}, bf16[256,768]{1,0:T(8,128)(2,1)S(1)}, u32[]{:S(2)}, u32[]{:S(2)}) collective-permute-start(bf16[256,768]{1,0:T(8,128)(2,1)S(1)} %collective-permute-done.12.refs_12_), channel_id=1, source_target_pairs={{0,1},{1,0},{2,3},{3,2},{4,5},{5,4},{6,7},{7,6},{8,9},{9,8},{10,11... | collective-permute-start | bytes 1179656 | tf_op jit(solution)/shard_map/ppermute | solution.py:50
  39.3 16.2 %collective-permute-start.19 = (bf16[256,768]{1,0:T(8,128)(2,1)S(1)}, bf16[256,768]{1,0:T(8,128)(2,1)S(1)}, u32[]{:S(2)}, u32[]{:S(2)}) collective-permute-start(bf16[256,768]{1,0:T(8,128)(2,1)S(1)} %collective-permute-done.18.refs_18_), channel_id=1, source_target_pairs={{0,1},{1,0},{2,3},{3,2},{4,5},{5,4},{6,7},{7,6},{8,9},{9,8},{10,11... | collective-permute-start | bytes 1179656 | tf_op jit(solution)/shard_map/ppermute | solution.py:50
  43.5 12.0 %collective-permute-start.15 = (bf16[256,768]{1,0:T(8,128)(2,1)S(1)}, bf16[256,768]{1,0:T(8,128)(2,1)S(1)}, u32[]{:S(2)}, u32[]{:S(2)}) collective-permute-start(bf16[256,768]{1,0:T(8,128)(2,1)S(1)} %collective-permute-done.14.refs_14_), channel_id=1, source_target_pairs={{0,1},{1,0},{2,3},{3,2},{4,5},{5,4},{6,7},{7,6},{8,9},{9,8},{10,11... | collective-permute-start | bytes 1179656 | tf_op jit(solution)/shard_map/ppermute | solution.py:50
  47.7 7.8 %collective-permute-start.23 = (bf16[256,768]{1,0:T(8,128)(2,1)S(1)}, bf16[256,768]{1,0:T(8,128)(2,1)S(1)}, u32[]{:S(2)}, u32[]{:S(2)}) collective-permute-start(bf16[256,768]{1,0:T(8,128)(2,1)S(1)} %collective-permute-done.22.refs_22_), channel_id=1, source_target_pairs={{0,1},{1,0},{2,3},{3,2},{4,5},{5,4},{6,7},{7,6},{8,9},{9,8},{10,11... | collective-permute-start | bytes 1179656 | tf_op jit(solution)/shard_map/ppermute | solution.py:50
  49.3 6.2 %collective-permute-start.25 = (bf16[128,768]{1,0:T(8,128)(2,1)S(1)}, bf16[128,768]{1,0:T(8,128)(2,1)S(1)}, u32[]{:S(2)}, u32[]{:S(2)}) collective-permute-start(bf16[128,768]{1,0:T(8,128)(2,1)S(1)} %collective-permute-done.24.refs_24_), channel_id=1, source_target_pairs={{0,1},{1,0},{2,3},{3,2},{4,5},{5,4},{6,7},{7,6},{8,9},{9,8},{10,11... | collective-permute-start | bytes 589832 | tf_op jit(solution)/shard_map/ppermute | solution.py:50
  49.3 1.0 %copy-start = (s32[64,4,256]{2,1,0:T(4,128)S(1)}, s32[64,4,256]{2,1,0:T(4,128)}, u32[]{:S(2)}) copy-start(s32[64,4,256]{2,1,0:T(4,128)} %refs_4_.1) | copy-start | bytes 786436
  50.2 0.7 %copy-start.1 = (s32[4]{0:T(128)S(1)}, s32[4]{0:T(128)}, u32[]{:S(2)}) copy-start(s32[4]{0:T(128)} %refs_0_.1) | copy-start | bytes 52

commit v3 on v2

--- a/solution.py
+++ b/solution.py
@@ -125,12 +125,14 @@
     segments = pieces_n * items
     steps, lane_groups = count_x // row_block, LANES // GROUP
     bits_at = 2 * segments
-    info_size = segments + segments * GROUP // TILE + 1
+    tiles_max = segments * GROUP // TILE
+    counts_at = segments + steps * tiles_max
+    info_size = counts_at + steps + 1
     total_n = batch * batches
 
     def kernel(*refs):
         orient_refs = refs[:parts]
-        table_ref, info_ref, where_ref, raw, geometry, found, found_s, listed, sems = refs[parts:]
+        table_ref, info_ref, where_ref, raw, geometry, found, found_s, listed, touched, sems = refs[parts:]
         rep, slab, pix = (lax.axis_index(axis) for axis in ("rep", "slab", "pix"))
         first_x = (rep * ports.pix + pix) * count_x
         first_z = slab * planes
@@ -190,8 +192,8 @@
         to_scalar.start()
         to_scalar.wait()
 
-        for tile in range(segments, info_size):
-            info_ref[tile] = 0
+        for tile in range(tiles_max):
+            touched[tile] = 0
 
         count = jnp.int32(0)
         for piece in range(pieces_n):
@@ -221,11 +223,21 @@
                 rolled = pltpu.roll(geometry[n, :, lanes], shift, 1)
                 gathered = jnp.where((lane_group == slot) & valid, rolled, gathered)
             where_ref[:, pl.ds(pl.multiple_of(block * LANES, LANES), LANES)] = gathered
-            tile = segments + (block >> shift_of(TILE // LANES))
-            info_ref[tile] = info_ref[tile] | tile_bits
+            tile = block >> shift_of(TILE // LANES)
+            touched[tile] = touched[tile] | tile_bits
             return carry
 
         lax.fori_loop(0, tiles * (TILE // LANES), order, 0)
+
+        def to_steps(tile, counts):
+            tile_bits = touched[tile]
+            for s in range(steps):
+                info_ref[segments + s * tiles_max + counts[s]] = tile
+            return tuple(counts[s] + ((tile_bits >> s) & 1) for s in range(steps))
+
+        counts = lax.fori_loop(0, tiles, to_steps, (jnp.int32(0),) * steps)
+        for s in range(steps):
+            info_ref[counts_at + s] = counts[s]
 
     smem, vmem = pl.BlockSpec(memory_space=pltpu.SMEM), pl.BlockSpec(memory_space=pltpu.VMEM)
     return pl.pallas_call(
@@ -242,6 +254,7 @@
             pltpu.VMEM((total_n, LANES), jnp.int32),
             pltpu.SMEM((total_n, LANES), jnp.int32),
             pltpu.SMEM((segments + 1,), jnp.int32),
+            pltpu.SMEM((tiles_max,), jnp.int32),
             pltpu.SemaphoreType.DMA((total_n,)),
         ],
         compiler_params=pltpu.CompilerParams(vmem_limit_bytes=4 << 20),
@@ -263,7 +276,9 @@
         compact, total, staged, sems = refs[3 + pieces_n :]
         first_x = (lax.axis_index("rep") * lax.axis_size("pix") + lax.axis_index("pix")) * count_x
         first_z = lax.axis_index("slab") * planes
-        count = info_ref[segments + segments * GROUP // TILE]
+        tiles_max = segments * GROUP // TILE
+        counts_at = segments + steps * tiles_max
+        count = info_ref[counts_at + steps]
         tiles = (count + TILE // GROUP - 1) >> shift_of(TILE // GROUP)
 
         first = 0
@@ -295,10 +310,12 @@
             rows = pl.ds(step * row_block, row_block)
             return pltpu.make_async_copy(staged.at[slot], out_ref.at[rows], sems.at[slot])
 
-        for step in range(steps):
-            slot = step % 2
-
-            def product(tile, step=step):
+        shape = (row_block, planes, columns)
+
+        def one_step(step, carry):
+            slot = step & 1
+
+            def product(tile):
                 lanes = pl.ds(pl.multiple_of(tile * TILE, TILE), TILE)
                 lower_x, part_x = where_ref[0:1, lanes], where_ref[1:2, lanes]
                 lower_z, part_z = where_ref[2:3, lanes], where_ref[3:4, lanes]
@@ -310,35 +327,41 @@
                 matrix = matrix.reshape(row_block * planes, TILE)
                 return jnp.dot(matrix, compact[lanes, :], preferred_element_type=jnp.float32)
 
-            def add(tile, seen, step=step, product=product):
-                hit = (info_ref[segments + tile] >> step) & 1
-
-                @pl.when((hit > 0) & (seen == 0))
-                def _():
-                    total[...] = product(tile)
-
-                @pl.when((hit > 0) & (seen > 0))
-                def _():
-                    total[...] += product(tile)
-
-                return seen + hit
-
-            seen = lax.fori_loop(0, tiles, add, jnp.int32(0))
-            if step >= 2:
+            touched = info_ref[counts_at + step]
+            list_at = segments + step * tiles_max
+
+            @pl.when(touched == 1)
+            def _():
+                total[...] = product(info_ref[list_at])
+
+            @pl.when(touched >= 2)
+            def _():
+                total[...] = product(info_ref[list_at]) + product(info_ref[list_at + 1])
+
+            def add(index, carry):
+                total[...] += product(info_ref[list_at + index])
+                return carry
+
+            lax.fori_loop(2, touched, add, 0)
+
+            @pl.when(step >= 2)
+            def _():
                 out_copy(step - 2, slot).wait()
-            shape = (row_block, planes, columns)
-
-            @pl.when(seen > 0)
-            def _(slot=slot):
+
+            @pl.when(touched > 0)
+            def _():
                 scale = 1.0 / (total[:, 2 * columns :] + 1.0)
                 staged[slot, :, :, :columns] = (total[:, :columns] * scale).reshape(shape)
                 staged[slot, :, :, columns:] = (total[:, columns : 2 * columns] * scale).reshape(shape)
 
-            @pl.when(seen == 0)
-            def _(slot=slot):
+            @pl.when(touched == 0)
+            def _():
                 staged[slot] = jnp.zeros((row_block, planes, 2 * columns), jnp.float32)
 
             out_copy(step, slot).start()
+            return carry
+
+        lax.fori_loop(0, steps, one_step, 0)
         for step in range(max(steps - 2, 0), steps):
             out_copy(step, step % 2).wait()
 

time: 63.1 us -> 61.9 us (0.981)
  Pallas kernels: 12 us -> 10.8 us
    pallas_call x1, Pallas kernels: 7.43 us -> 6.12 us  [spread(): pl.pallas_call(kernel, out_shape=jax.ShapeDtypeStruct((count_x, planes, 2...]
  transfers between devices with their start and end apart: 26 -> 26, of which waited for: 10 -> 10; matrix products, arithmetic and copies ran while one was open for 0% -> 0% of each run, Pallas kernels for 7% -> 8%
where the time goes in v3:
time: 61.9 us; the launch traced here: 61.7 us
  waiting for transfers between devices  33.3 us (54%)
  starting transfers between devices  14.9 us (24%)
  Pallas kernels  10.8 us (17%)
  local copies, waits for them, and re-layouts  1.61 us (3%)
  other arithmetic  1.06 us (2%)
    ppermute x26, waiting for transfers between devices, send(): value = lax.ppermute(value, ('rep', 'slab', 'pix'), self.pairs(port))  33.3 us
    ppermute x26, starting transfers between devices, send(): value = lax.ppermute(value, ('rep', 'slab', 'pix'), self.pairs(port))  14.9 us
    pallas_call x1, Pallas kernels, spread(): pl.pallas_call(kernel, out_shape=jax.ShapeDtypeStruct((count_x, planes, 2...  6.12 us
    pallas_call x1, Pallas kernels, make_plan(): pl.pallas_call(kernel, out_shape=[jax.ShapeDtypeStruct((info_size,), jnp....  4.66 us
    unnamed x4, local copies, waits for them, and re-layouts  1.61 us
  transfers between devices with their start and end apart: 26, of which 10 were waited for; matrix products, arithmetic and copies ran while one was open for 0% of the time, Pallas kernels for 8%

profile of v3, /device:TPU:18, one launch (start us, length us, event | category | flops | bytes accessed | tf_op | source)
XLA Modules:
  0.0 61.7 jit_solution(17323076898016676959)
XLA Ops:
  0.0 1.0 %pad_maximum_fusion.4 = bf16[4,32,768]{2,1,0:T(8,128)(2,1)S(1)} fusion(bf16[4,32,256]{2,1,0:T(8,128)(2,1)} %param.5, bf16[4,32,512]{2,1,0:T(8,128)(2,1)} %param.4), kind=kLoop, calls=%fused_computation.4 | loop fusion | flops 393216 | bytes 393216 | tf_op jit(solution)/shard_map/concatenate | solution.py:392
  1.0 1.6 %collective-permute-start.4 = (bf16[128,768]{1,0:T(8,128)(2,1)S(1)}, bf16[128,768]{1,0:T(8,128)(2,1)S(1)}, u32[]{:S(2)}, u32[]{:S(2)}) collective-permute-start(bf16[128,768]{1,0:T(8,128)(2,1)S(1)} %bitcast.1), channel_id=1, source_target_pairs={{0,4},{1,5},{2,6},{3,7},{4,8},{5,9},{6,10},{7,11},{8,12},{9,13},{1... | collective-permute-start | bytes 589832 | tf_op jit(solution)/shard_map/ppermute | solution.py:50
  2.6 1.5 %collective-permute-start.10 = (bf16[128,768]{1,0:T(8,128)(2,1)S(1)}, bf16[128,768]{1,0:T(8,128)(2,1)S(1)}, u32[]{:S(2)}, u32[]{:S(2)}) collective-permute-start(bf16[128,768]{1,0:T(8,128)(2,1)S(1)} %bitcast.2), channel_id=1, source_target_pairs={{0,18},{1,19},{2,16},{3,17},{4,22},{5,23},{6,20},{7,21},{8,26},{9,... | collective-permute-start | bytes 589832 | tf_op jit(solution)/shard_map/ppermute | solution.py:50
  4.1 0.4 collective-permute-start.8
  4.5 0.0 collective-permute-start.3
  4.5 6.5 %collective-permute-done.4.refs_4_ = bf16[128,768]{1,0:T(8,128)(2,1)S(1)} collective-permute-done((bf16[128,768]{1,0:T(8,128)(2,1)S(1)}, bf16[128,768]{1,0:T(8,128)(2,1)S(1)}, u32[]{:S(2)}, u32[]{:S(2)}) %collective-permute-start.4) | collective-permute-done | bytes 196640 | tf_op jit(solution)/shard_map/ppermute | solution.py:50
  11.1 1.9 %collective-permute-start.6 = (bf16[128,768]{1,0:T(8,128)(2,1)S(1)}, bf16[128,768]{1,0:T(8,128)(2,1)S(1)}, u32[]{:S(2)}, u32[]{:S(2)}) collective-permute-start(bf16[128,768]{1,0:T(8,128)(2,1)S(1)} %collective-permute-done.4.refs_4_), channel_id=1, source_target_pairs={{0,4},{1,5},{2,6},{3,7},{4,8},{5,9},{6,10},{7,11},{8,12},{9,13},{1... | collective-permute-start | bytes 589832 | tf_op jit(solution)/shard_map/ppermute | solution.py:50
  13.0 0.0 collective-permute-start.1
  13.0 1.0 %collective-permute-start.20 = (bf16[128,768]{1,0:T(8,128)(2,1)S(1)}, bf16[128,768]{1,0:T(8,128)(2,1)S(1)}, u32[]{:S(2)}, u32[]{:S(2)}) collective-permute-start(bf16[128,768]{1,0:T(8,128)(2,1)S(1)} %collective-permute-done.10.refs_10_), channel_id=1, source_target_pairs={{0,12},{1,13},{2,14},{3,15},{4,0},{5,1},{6,2},{7,3},{8,4},{9,5},{1... | collective-permute-start | bytes 589832 | tf_op jit(solution)/shard_map/ppermute | solution.py:50
  14.0 6.2 %collective-permute-done.6.refs_6_ = bf16[128,768]{1,0:T(8,128)(2,1)S(1)} collective-permute-done((bf16[128,768]{1,0:T(8,128)(2,1)S(1)}, bf16[128,768]{1,0:T(8,128)(2,1)S(1)}, u32[]{:S(2)}, u32[]{:S(2)}) %collective-permute-start.6) | collective-permute-done | bytes 196640 | tf_op jit(solution)/shard_map/ppermute | solution.py:50
  20.2 3.0 %collective-permute-start.16 = (bf16[128,768]{1,0:T(8,128)(2,1)S(1)}, bf16[128,768]{1,0:T(8,128)(2,1)S(1)}, u32[]{:S(2)}, u32[]{:S(2)}) collective-permute-start(bf16[128,768]{1,0:T(8,128)(2,1)S(1)} %collective-permute-done.10.refs_10_), channel_id=1, source_target_pairs={{0,4},{1,5},{2,6},{3,7},{4,8},{5,9},{6,10},{7,11},{8,12},{9,13},{1... | collective-permute-start | bytes 589832 | tf_op jit(solution)/shard_map/ppermute | solution.py:50
  23.2 0.6 collective-permute-start.11
  23.8 0.1 collective-permute-start
  23.9 0.5 collective-permute-start.2
  24.4 0.2 collective-permute-done.7.refs_7_
  24.6 0.1 collective-permute-start.21
  24.7 0.4 collective-permute-done.refs_1_
  25.2 0.0 collective-permute-done.2.refs_3_
  25.2 2.0 %collective-permute-start.18 = (bf16[256,768]{1,0:T(8,128)(2,1)S(1)}, bf16[256,768]{1,0:T(8,128)(2,1)S(1)}, u32[]{:S(2)}, u32[]{:S(2)}) collective-permute-start(bf16[256,768]{1,0:T(8,128)(2,1)S(1)} %pad_maximum_fusion.2), channel_id=1, source_target_pairs={{0,16},{1,3},{2,18},{3,1},{4,20},{5,7},{6,22},{7,5},{8,24},{9,11},... | collective-permute-start | bytes 1179656 | tf_op jit(solution)/shard_map/ppermute | solution.py:50
  27.2 0.1 collective-permute-start.14
  27.3 2.0 %collective-permute-start.22 = (bf16[256,768]{1,0:T(8,128)(2,1)S(1)}, bf16[256,768]{1,0:T(8,128)(2,1)S(1)}, u32[]{:S(2)}, u32[]{:S(2)}) collective-permute-start(bf16[256,768]{1,0:T(8,128)(2,1)S(1)} %pad_maximum_fusion.3), channel_id=1, source_target_pairs={{0,16},{1,3},{2,18},{3,1},{4,20},{5,7},{6,22},{7,5},{8,24},{9,11},... | collective-permute-start | bytes 1179656 | tf_op jit(solution)/shard_map/ppermute | solution.py:50
  29.2 1.4 %collective-permute-done.17.refs_17_ = bf16[128,768]{1,0:T(8,128)(2,1)S(1)} collective-permute-done((bf16[128,768]{1,0:T(8,128)(2,1)S(1)}, bf16[128,768]{1,0:T(8,128)(2,1)S(1)}, u32[]{:S(2)}, u32[]{:S(2)}) %collective-permute-start.17) | collective-permute-done | bytes 196640 | tf_op jit(solution)/shard_map/ppermute | solution.py:50
  30.7 0.1 collective-permute-start.24
  30.8 2.2 %collective-permute-done.12.refs_12_ = bf16[256,768]{1,0:T(8,128)(2,1)S(1)} collective-permute-done((bf16[256,768]{1,0:T(8,128)(2,1)S(1)}, bf16[256,768]{1,0:T(8,128)(2,1)S(1)}, u32[]{:S(2)}, u32[]{:S(2)}) %collective-permute-start.12) | collective-permute-done | bytes 393248 | tf_op jit(solution)/shard_map/ppermute | solution.py:50
  33.0 6.3 %collective-permute-done.18.refs_18_ = bf16[256,768]{1,0:T(8,128)(2,1)S(1)} collective-permute-done((bf16[256,768]{1,0:T(8,128)(2,1)S(1)}, bf16[256,768]{1,0:T(8,128)(2,1)S(1)}, u32[]{:S(2)}, u32[]{:S(2)}) %collective-permute-start.18) | collective-permute-done | bytes 393248 | tf_op jit(solution)/shard_map/ppermute | solution.py:50
  39.3 4.2 %collective-permute-done.14.refs_14_ = bf16[256,768]{1,0:T(8,128)(2,1)S(1)} collective-permute-done((bf16[256,768]{1,0:T(8,128)(2,1)S(1)}, bf16[256,768]{1,0:T(8,128)(2,1)S(1)}, u32[]{:S(2)}, u32[]{:S(2)}) %collective-permute-start.14) | collective-permute-done | bytes 393248 | tf_op jit(solution)/shard_map/ppermute | solution.py:50
  43.5 4.2 %collective-permute-done.22.refs_22_ = bf16[256,768]{1,0:T(8,128)(2,1)S(1)} collective-permute-done((bf16[256,768]{1,0:T(8,128)(2,1)S(1)}, bf16[256,768]{1,0:T(8,128)(2,1)S(1)}, u32[]{:S(2)}, u32[]{:S(2)}) %collective-permute-start.22) | collective-permute-done | bytes 393248 | tf_op jit(solution)/shard_map/ppermute | solution.py:50
  47.7 1.6 %collective-permute-done.24.refs_24_ = bf16[128,768]{1,0:T(8,128)(2,1)S(1)} collective-permute-done((bf16[128,768]{1,0:T(8,128)(2,1)S(1)}, bf16[128,768]{1,0:T(8,128)(2,1)S(1)}, u32[]{:S(2)}, u32[]{:S(2)}) %collective-permute-start.24) | collective-permute-done | bytes 196640 | tf_op jit(solution)/shard_map/ppermute | solution.py:50
  49.3 0.9 %copy-done = s32[64,4,256]{2,1,0:T(4,128)S(1)} copy-done((s32[64,4,256]{2,1,0:T(4,128)S(1)}, s32[64,4,256]{2,1,0:T(4,128)}, u32[]{:S(2)}) %copy-start) | copy-done | bytes 262168
  50.2 0.7 %copy-done.1 = s32[4]{0:T(128)S(1)} copy-done((s32[4]{0:T(128)S(1)}, s32[4]{0:T(128)}, u32[]{:S(2)}) %copy-start.1) | copy-done | bytes 40
  50.9 4.7 %plan.1 = (s32[393]{0:T(512)S(1)}, f32[8,4096]{1,0:T(8,128)S(1)}) custom-call(s32[4]{0:T(128)S(1)} %copy-done.1, s32[4]{0:T(128)S(1)} %collective-permute-done.refs_1_, s32[4]{0:T(128)S(1)} %collective-permute-done.1.refs_2_, s32[4]{0:T(128)S(1)} %collective-permute-done.2.refs_3_, s32[64,4,256]{2,1,0:T(4,128)S(1)} %copy-done), custom_call_target="tpu_custom_call" | custom-call | tf_op jit(solution)/shard_map/plan/pallas_call | solution.py:243
  55.6 6.1 %spread.1 = f32[64,32,512]{2,1,0:T(8,128)} custom-call(s32[393]{0:T(512)S(1)} %get-tuple-element.7.refs_0_, f32[8,4096]{1,0:T(8,128)S(1)} %get-tuple-element.8.refs_1_, bf16[128,768]{1,0:T(8,128)(2,1)S(1)} %bitcast.6, bf16[128,768]{1,0:T(8,128)(2,1)S(1)} %collective-permute-done.3.refs_3_, bf16[128,768]{1,0:T(8,128)(2,1)S(1)} %collective-permute-done.4.refs_4_, ...), custom_call_target="tpu_custom_call" | custom-call | tf_op jit(solution)/shard_map/spread/pallas_call | solution.py:369
  (31 shorter events, 0.2 us)
Async XLA Ops:
  1.0 10.1 %collective-permute-start.4 = (bf16[128,768]{1,0:T(8,128)(2,1)S(1)}, bf16[128,768]{1,0:T(8,128)(2,1)S(1)}, u32[]{:S(2)}, u32[]{:S(2)}) collective-permute-start(bf16[128,768]{1,0:T(8,128)(2,1)S(1)} %bitcast.1), channel_id=1, source_target_pairs={{0,4},{1,5},{2,6},{3,7},{4,8},{5,9},{6,10},{7,11},{8,12},{9,13},{1... | collective-permute-start | bytes 589832 | tf_op jit(solution)/shard_map/ppermute | solution.py:50
  2.6 10.4 %collective-permute-start.10 = (bf16[128,768]{1,0:T(8,128)(2,1)S(1)}, bf16[128,768]{1,0:T(8,128)(2,1)S(1)}, u32[]{:S(2)}, u32[]{:S(2)}) collective-permute-start(bf16[128,768]{1,0:T(8,128)(2,1)S(1)} %bitcast.2), channel_id=1, source_target_pairs={{0,18},{1,19},{2,16},{3,17},{4,22},{5,23},{6,20},{7,21},{8,26},{9,... | collective-permute-start | bytes 589832 | tf_op jit(solution)/shard_map/ppermute | solution.py:50
  4.1 8.9 %collective-permute-start.8 = (bf16[128,768]{1,0:T(8,128)(2,1)S(1)}, bf16[128,768]{1,0:T(8,128)(2,1)S(1)}, u32[]{:S(2)}, u32[]{:S(2)}) collective-permute-start(bf16[128,768]{1,0:T(8,128)(2,1)S(1)} %bitcast.3), channel_id=1, source_target_pairs={{0,12},{1,13},{2,14},{3,15},{4,0},{5,1},{6,2},{7,3},{8,4},{9,5},{1... | collective-permute-start | bytes 589832 | tf_op jit(solution)/shard_map/ppermute | solution.py:50
  4.5 9.4 %collective-permute-start.3 = (bf16[128,768]{1,0:T(8,128)(2,1)S(1)}, bf16[128,768]{1,0:T(8,128)(2,1)S(1)}, u32[]{:S(2)}, u32[]{:S(2)}) collective-permute-start(bf16[128,768]{1,0:T(8,128)(2,1)S(1)} %bitcast.4), channel_id=1, source_target_pairs={{0,1},{1,0},{2,3},{3,2},{4,5},{5,4},{6,7},{7,6},{8,9},{9,8},{10,11... | collective-permute-start | bytes 589832 | tf_op jit(solution)/shard_map/ppermute | solution.py:50
  11.1 9.1 %collective-permute-start.6 = (bf16[128,768]{1,0:T(8,128)(2,1)S(1)}, bf16[128,768]{1,0:T(8,128)(2,1)S(1)}, u32[]{:S(2)}, u32[]{:S(2)}) collective-permute-start(bf16[128,768]{1,0:T(8,128)(2,1)S(1)} %collective-permute-done.4.refs_4_), channel_id=1, source_target_pairs={{0,4},{1,5},{2,6},{3,7},{4,8},{5,9},{6,10},{7,11},{8,12},{9,13},{1... | collective-permute-start | bytes 589832 | tf_op jit(solution)/shard_map/ppermute | solution.py:50
  13.0 10.2 %collective-permute-start.5 = (bf16[128,768]{1,0:T(8,128)(2,1)S(1)}, bf16[128,768]{1,0:T(8,128)(2,1)S(1)}, u32[]{:S(2)}, u32[]{:S(2)}) collective-permute-start(bf16[128,768]{1,0:T(8,128)(2,1)S(1)} %collective-permute-done.4.refs_4_), channel_id=1, source_target_pairs={{0,1},{1,0},{2,3},{3,2},{4,5},{5,4},{6,7},{7,6},{8,9},{9,8},{10,11... | collective-permute-start | bytes 589832 | tf_op jit(solution)/shard_map/ppermute | solution.py:50
  13.0 10.8 %collective-permute-start.1 = (s32[4]{0:T(128)}, s32[4]{0:T(128)S(1)}, u32[]{:S(2)}, u32[]{:S(2)}) collective-permute-start(s32[4]{0:T(128)} %refs_0_.1), channel_id=1, source_target_pairs={{0,16},{1,17},{2,18},{3,19},{4,20},{5,21},{6,22},{7,23},{8,24},{9,... | collective-permute-start | bytes 56 | tf_op jit(solution)/shard_map/ppermute | solution.py:50
  13.0 10.9 %collective-permute-start.20 = (bf16[128,768]{1,0:T(8,128)(2,1)S(1)}, bf16[128,768]{1,0:T(8,128)(2,1)S(1)}, u32[]{:S(2)}, u32[]{:S(2)}) collective-permute-start(bf16[128,768]{1,0:T(8,128)(2,1)S(1)} %collective-permute-done.10.refs_10_), channel_id=1, source_target_pairs={{0,12},{1,13},{2,14},{3,15},{4,0},{5,1},{6,2},{7,3},{8,4},{9,5},{1... | collective-permute-start | bytes 589832 | tf_op jit(solution)/shard_map/ppermute | solution.py:50
  13.9 9.2 %collective-permute-start.9 = (bf16[128,768]{1,0:T(8,128)(2,1)S(1)}, bf16[128,768]{1,0:T(8,128)(2,1)S(1)}, u32[]{:S(2)}, u32[]{:S(2)}) collective-permute-start(bf16[128,768]{1,0:T(8,128)(2,1)S(1)} %collective-permute-done.8.refs_8_), channel_id=1, source_target_pairs={{0,1},{1,0},{2,3},{3,2},{4,5},{5,4},{6,7},{7,6},{8,9},{9,8},{10,11... | collective-permute-start | bytes 589832 | tf_op jit(solution)/shard_map/ppermute | solution.py:50
  20.2 7.0 %collective-permute-start.16 = (bf16[128,768]{1,0:T(8,128)(2,1)S(1)}, bf16[128,768]{1,0:T(8,128)(2,1)S(1)}, u32[]{:S(2)}, u32[]{:S(2)}) collective-permute-start(bf16[128,768]{1,0:T(8,128)(2,1)S(1)} %collective-permute-done.10.refs_10_), channel_id=1, source_target_pairs={{0,4},{1,5},{2,6},{3,7},{4,8},{5,9},{6,10},{7,11},{8,12},{9,13},{1... | collective-permute-start | bytes 589832 | tf_op jit(solution)/shard_map/ppermute | solution.py:50
  23.1 1.4 %collective-permute-start.7 = (bf16[128,768]{1,0:T(8,128)(2,1)S(1)}, bf16[128,768]{1,0:T(8,128)(2,1)S(1)}, u32[]{:S(2)}, u32[]{:S(2)}) collective-permute-start(bf16[128,768]{1,0:T(8,128)(2,1)S(1)} %collective-permute-done.6.refs_6_), channel_id=1, source_target_pairs={{0,1},{1,0},{2,3},{3,2},{4,5},{5,4},{6,7},{7,6},{8,9},{9,8},{10,11... | collective-permute-start | bytes 589832 | tf_op jit(solution)/shard_map/ppermute | solution.py:50
  23.2 4.1 %collective-permute-start.11 = (bf16[128,768]{1,0:T(8,128)(2,1)S(1)}, bf16[128,768]{1,0:T(8,128)(2,1)S(1)}, u32[]{:S(2)}, u32[]{:S(2)}) collective-permute-start(bf16[128,768]{1,0:T(8,128)(2,1)S(1)} %collective-permute-done.10.refs_10_), channel_id=1, source_target_pairs={{0,1},{1,0},{2,3},{3,2},{4,5},{5,4},{6,7},{7,6},{8,9},{9,8},{10,11... | collective-permute-start | bytes 589832 | tf_op jit(solution)/shard_map/ppermute | solution.py:50
  23.8 1.4 %collective-permute-start = (s32[4]{0:T(128)}, s32[4]{0:T(128)S(1)}, u32[]{:S(2)}, u32[]{:S(2)}) collective-permute-start(s32[4]{0:T(128)} %refs_0_.1), channel_id=1, source_target_pairs={{0,1},{1,0},{2,3},{3,2},{4,5},{5,4},{6,7},{7,6},{8,9},{9,8},{10,11... | collective-permute-start | bytes 56 | tf_op jit(solution)/shard_map/ppermute | solution.py:50
  23.9 1.3 %collective-permute-start.2 = (s32[4]{0:T(128)S(1)}, s32[4]{0:T(128)S(1)}, u32[]{:S(2)}, u32[]{:S(2)}) collective-permute-start(s32[4]{0:T(128)S(1)} %collective-permute-done.1.refs_2_), channel_id=1, source_target_pairs={{0,1},{1,0},{2,3},{3,2},{4,5},{5,4},{6,7},{7,6},{8,9},{9,8},{10,11... | collective-permute-start | bytes 56 | tf_op jit(solution)/shard_map/ppermute | solution.py:50
  24.6 4.6 %collective-permute-start.21 = (bf16[128,768]{1,0:T(8,128)(2,1)S(1)}, bf16[128,768]{1,0:T(8,128)(2,1)S(1)}, u32[]{:S(2)}, u32[]{:S(2)}) collective-permute-start(bf16[128,768]{1,0:T(8,128)(2,1)S(1)} %collective-permute-done.20.refs_20_), channel_id=1, source_target_pairs={{0,1},{1,0},{2,3},{3,2},{4,5},{5,4},{6,7},{7,6},{8,9},{9,8},{10,11... | collective-permute-start | bytes 589832 | tf_op jit(solution)/shard_map/ppermute | solution.py:50
  25.2 7.8 %collective-permute-start.12 = (bf16[256,768]{1,0:T(8,128)(2,1)S(1)}, bf16[256,768]{1,0:T(8,128)(2,1)S(1)}, u32[]{:S(2)}, u32[]{:S(2)}) collective-permute-start(bf16[256,768]{1,0:T(8,128)(2,1)S(1)} %pad_maximum_fusion), channel_id=1, source_target_pairs={{0,16},{1,3},{2,18},{3,1},{4,20},{5,7},{6,22},{7,5},{8,24},{9,11},... | collective-permute-start | bytes 1179656 | tf_op jit(solution)/shard_map/ppermute | solution.py:50
  25.2 14.1 %collective-permute-start.18 = (bf16[256,768]{1,0:T(8,128)(2,1)S(1)}, bf16[256,768]{1,0:T(8,128)(2,1)S(1)}, u32[]{:S(2)}, u32[]{:S(2)}) collective-permute-start(bf16[256,768]{1,0:T(8,128)(2,1)S(1)} %pad_maximum_fusion.2), channel_id=1, source_target_pairs={{0,16},{1,3},{2,18},{3,1},{4,20},{5,7},{6,22},{7,5},{8,24},{9,11},... | collective-permute-start | bytes 1179656 | tf_op jit(solution)/shard_map/ppermute | solution.py:50
  27.2 16.3 %collective-permute-start.14 = (bf16[256,768]{1,0:T(8,128)(2,1)S(1)}, bf16[256,768]{1,0:T(8,128)(2,1)S(1)}, u32[]{:S(2)}, u32[]{:S(2)}) collective-permute-start(bf16[256,768]{1,0:T(8,128)(2,1)S(1)} %pad_maximum_fusion.1), channel_id=1, source_target_pairs={{0,16},{1,3},{2,18},{3,1},{4,20},{5,7},{6,22},{7,5},{8,24},{9,11},... | collective-permute-start | bytes 1179656 | tf_op jit(solution)/shard_map/ppermute | solution.py:50
  27.3 20.4 %collective-permute-start.22 = (bf16[256,768]{1,0:T(8,128)(2,1)S(1)}, bf16[256,768]{1,0:T(8,128)(2,1)S(1)}, u32[]{:S(2)}, u32[]{:S(2)}) collective-permute-start(bf16[256,768]{1,0:T(8,128)(2,1)S(1)} %pad_maximum_fusion.3), channel_id=1, source_target_pairs={{0,16},{1,3},{2,18},{3,1},{4,20},{5,7},{6,22},{7,5},{8,24},{9,11},... | collective-permute-start | bytes 1179656 | tf_op jit(solution)/shard_map/ppermute | solution.py:50
  29.2 1.4 %collective-permute-start.17 = (bf16[128,768]{1,0:T(8,128)(2,1)S(1)}, bf16[128,768]{1,0:T(8,128)(2,1)S(1)}, u32[]{:S(2)}, u32[]{:S(2)}) collective-permute-start(bf16[128,768]{1,0:T(8,128)(2,1)S(1)} %collective-permute-done.16.refs_16_), channel_id=1, source_target_pairs={{0,1},{1,0},{2,3},{3,2},{4,5},{5,4},{6,7},{7,6},{8,9},{9,8},{10,11... | collective-permute-start | bytes 589832 | tf_op jit(solution)/shard_map/ppermute | solution.py:50
  30.7 18.6 %collective-permute-start.24 = (bf16[128,768]{1,0:T(8,128)(2,1)S(1)}, bf16[128,768]{1,0:T(8,128)(2,1)S(1)}, u32[]{:S(2)}, u32[]{:S(2)}) collective-permute-start(bf16[128,768]{1,0:T(8,128)(2,1)S(1)} %collective-permute-done.6.refs_6_), channel_id=1, source_target_pairs={{0,18},{1,19},{2,16},{3,17},{4,22},{5,23},{6,20},{7,21},{8,26},{9,... | collective-permute-start | bytes 589832 | tf_op jit(solution)/shard_map/ppermute | solution.py:50
  33.0 22.6 %collective-permute-start.13 = (bf16[256,768]{1,0:T(8,128)(2,1)S(1)}, bf16[256,768]{1,0:T(8,128)(2,1)S(1)}, u32[]{:S(2)}, u32[]{:S(2)}) collective-permute-start(bf16[256,768]{1,0:T(8,128)(2,1)S(1)} %collective-permute-done.12.refs_12_), channel_id=1, source_target_pairs={{0,1},{1,0},{2,3},{3,2},{4,5},{5,4},{6,7},{7,6},{8,9},{9,8},{10,11... | collective-permute-start | bytes 1179656 | tf_op jit(solution)/shard_map/ppermute | solution.py:50
  39.3 16.3 %collective-permute-start.19 = (bf16[256,768]{1,0:T(8,128)(2,1)S(1)}, bf16[256,768]{1,0:T(8,128)(2,1)S(1)}, u32[]{:S(2)}, u32[]{:S(2)}) collective-permute-start(bf16[256,768]{1,0:T(8,128)(2,1)S(1)} %collective-permute-done.18.refs_18_), channel_id=1, source_target_pairs={{0,1},{1,0},{2,3},{3,2},{4,5},{5,4},{6,7},{7,6},{8,9},{9,8},{10,11... | collective-permute-start | bytes 1179656 | tf_op jit(solution)/shard_map/ppermute | solution.py:50
  43.5 12.1 %collective-permute-start.15 = (bf16[256,768]{1,0:T(8,128)(2,1)S(1)}, bf16[256,768]{1,0:T(8,128)(2,1)S(1)}, u32[]{:S(2)}, u32[]{:S(2)}) collective-permute-start(bf16[256,768]{1,0:T(8,128)(2,1)S(1)} %collective-permute-done.14.refs_14_), channel_id=1, source_target_pairs={{0,1},{1,0},{2,3},{3,2},{4,5},{5,4},{6,7},{7,6},{8,9},{9,8},{10,11... | collective-permute-start | bytes 1179656 | tf_op jit(solution)/shard_map/ppermute | solution.py:50
  47.7 7.9 %collective-permute-start.23 = (bf16[256,768]{1,0:T(8,128)(2,1)S(1)}, bf16[256,768]{1,0:T(8,128)(2,1)S(1)}, u32[]{:S(2)}, u32[]{:S(2)}) collective-permute-start(bf16[256,768]{1,0:T(8,128)(2,1)S(1)} %collective-permute-done.22.refs_22_), channel_id=1, source_target_pairs={{0,1},{1,0},{2,3},{3,2},{4,5},{5,4},{6,7},{7,6},{8,9},{9,8},{10,11... | collective-permute-start | bytes 1179656 | tf_op jit(solution)/shard_map/ppermute | solution.py:50
  49.3 6.3 %collective-permute-start.25 = (bf16[128,768]{1,0:T(8,128)(2,1)S(1)}, bf16[128,768]{1,0:T(8,128)(2,1)S(1)}, u32[]{:S(2)}, u32[]{:S(2)}) collective-permute-start(bf16[128,768]{1,0:T(8,128)(2,1)S(1)} %collective-permute-done.24.refs_24_), channel_id=1, source_target_pairs={{0,1},{1,0},{2,3},{3,2},{4,5},{5,4},{6,7},{7,6},{8,9},{9,8},{10,11... | collective-permute-start | bytes 589832 | tf_op jit(solution)/shard_map/ppermute | solution.py:50
  49.3 1.0 %copy-start = (s32[64,4,256]{2,1,0:T(4,128)S(1)}, s32[64,4,256]{2,1,0:T(4,128)}, u32[]{:S(2)}) copy-start(s32[64,4,256]{2,1,0:T(4,128)} %refs_4_.1) | copy-start | bytes 786436
  50.2 0.7 %copy-start.1 = (s32[4]{0:T(128)S(1)}, s32[4]{0:T(128)}, u32[]{:S(2)}) copy-start(s32[4]{0:T(128)} %refs_0_.1) | copy-start | bytes 52

commit v4 on v3

--- a/solution.py
+++ b/solution.py
@@ -313,7 +313,7 @@
         shape = (row_block, planes, columns)
 
         def one_step(step, carry):
-            slot = step & 1
+            slot = step & 3
 
             def product(tile):
                 lanes = pl.ds(pl.multiple_of(tile * TILE, TILE), TILE)
@@ -344,9 +344,9 @@
 
             lax.fori_loop(2, touched, add, 0)
 
-            @pl.when(step >= 2)
+            @pl.when(step >= 4)
             def _():
-                out_copy(step - 2, slot).wait()
+                out_copy(step - 4, slot).wait()
 
             @pl.when(touched > 0)
             def _():
@@ -362,8 +362,8 @@
             return carry
 
         lax.fori_loop(0, steps, one_step, 0)
-        for step in range(max(steps - 2, 0), steps):
-            out_copy(step, step % 2).wait()
+        for step in range(max(steps - 4, 0), steps):
+            out_copy(step, step % 4).wait()
 
     smem, vmem = pl.BlockSpec(memory_space=pltpu.SMEM), pl.BlockSpec(memory_space=pltpu.VMEM)
     return pl.pallas_call(
@@ -374,8 +374,8 @@
         scratch_shapes=[
             pltpu.VMEM((segments * GROUP + GROUP, channels), jnp.bfloat16),
             pltpu.VMEM((row_block * planes, channels), jnp.float32),
-            pltpu.VMEM((2, row_block, planes, 2 * columns), jnp.float32),
-            pltpu.SemaphoreType.DMA((2,)),
+            pltpu.VMEM((4, row_block, planes, 2 * columns), jnp.float32),
+            pltpu.SemaphoreType.DMA((4,)),
         ],
         compiler_params=pltpu.CompilerParams(vmem_limit_bytes=14 << 20),
         name="spread",

time: 61.9 us -> 61.7 us (level)
  no operation moved by 1% of the time
where the time goes in v4:
time: 61.7 us; the launch traced here: 61.6 us
  waiting for transfers between devices  33.3 us (54%)
  starting transfers between devices  14.9 us (24%)
  Pallas kernels  10.6 us (17%)
  local copies, waits for them, and re-layouts  1.61 us (3%)
  other arithmetic  1.06 us (2%)
    ppermute x26, waiting for transfers between devices, send(): value = lax.ppermute(value, ('rep', 'slab', 'pix'), self.pairs(port))  33.3 us
    ppermute x26, starting transfers between devices, send(): value = lax.ppermute(value, ('rep', 'slab', 'pix'), self.pairs(port))  14.9 us
    pallas_call x1, Pallas kernels, spread(): pl.pallas_call(kernel, out_shape=jax.ShapeDtypeStruct((count_x, planes, 2...  5.98 us
    pallas_call x1, Pallas kernels, make_plan(): pl.pallas_call(kernel, out_shape=[jax.ShapeDtypeStruct((info_size,), jnp....  4.66 us
    unnamed x4, local copies, waits for them, and re-layouts  1.61 us
  transfers between devices with their start and end apart: 26, of which 10 were waited for; matrix products, arithmetic and copies ran while one was open for 0% of the time, Pallas kernels for 8%

profile of v4, /device:TPU:18, one launch (start us, length us, event | category | flops | bytes accessed | tf_op | source)
XLA Modules:
  0.0 61.6 jit_solution(4456319391521371216)
XLA Ops:
  0.0 1.0 %pad_maximum_fusion.4 = bf16[4,32,768]{2,1,0:T(8,128)(2,1)S(1)} fusion(bf16[4,32,256]{2,1,0:T(8,128)(2,1)} %param.5, bf16[4,32,512]{2,1,0:T(8,128)(2,1)} %param.4), kind=kLoop, calls=%fused_computation.4 | loop fusion | flops 393216 | bytes 393216 | tf_op jit(solution)/shard_map/concatenate | solution.py:392
  1.0 1.6 %collective-permute-start.4 = (bf16[128,768]{1,0:T(8,128)(2,1)S(1)}, bf16[128,768]{1,0:T(8,128)(2,1)S(1)}, u32[]{:S(2)}, u32[]{:S(2)}) collective-permute-start(bf16[128,768]{1,0:T(8,128)(2,1)S(1)} %bitcast.1), channel_id=1, source_target_pairs={{0,4},{1,5},{2,6},{3,7},{4,8},{5,9},{6,10},{7,11},{8,12},{9,13},{1... | collective-permute-start | bytes 589832 | tf_op jit(solution)/shard_map/ppermute | solution.py:50
  2.6 1.5 %collective-permute-start.10 = (bf16[128,768]{1,0:T(8,128)(2,1)S(1)}, bf16[128,768]{1,0:T(8,128)(2,1)S(1)}, u32[]{:S(2)}, u32[]{:S(2)}) collective-permute-start(bf16[128,768]{1,0:T(8,128)(2,1)S(1)} %bitcast.2), channel_id=1, source_target_pairs={{0,18},{1,19},{2,16},{3,17},{4,22},{5,23},{6,20},{7,21},{8,26},{9,... | collective-permute-start | bytes 589832 | tf_op jit(solution)/shard_map/ppermute | solution.py:50
  4.1 0.4 collective-permute-start.8
  4.5 0.0 collective-permute-start.3
  4.5 6.5 %collective-permute-done.4.refs_4_ = bf16[128,768]{1,0:T(8,128)(2,1)S(1)} collective-permute-done((bf16[128,768]{1,0:T(8,128)(2,1)S(1)}, bf16[128,768]{1,0:T(8,128)(2,1)S(1)}, u32[]{:S(2)}, u32[]{:S(2)}) %collective-permute-start.4) | collective-permute-done | bytes 196640 | tf_op jit(solution)/shard_map/ppermute | solution.py:50
  11.1 1.9 %collective-permute-start.6 = (bf16[128,768]{1,0:T(8,128)(2,1)S(1)}, bf16[128,768]{1,0:T(8,128)(2,1)S(1)}, u32[]{:S(2)}, u32[]{:S(2)}) collective-permute-start(bf16[128,768]{1,0:T(8,128)(2,1)S(1)} %collective-permute-done.4.refs_4_), channel_id=1, source_target_pairs={{0,4},{1,5},{2,6},{3,7},{4,8},{5,9},{6,10},{7,11},{8,12},{9,13},{1... | collective-permute-start | bytes 589832 | tf_op jit(solution)/shard_map/ppermute | solution.py:50
  13.0 0.0 collective-permute-start.1
  13.0 1.0 %collective-permute-start.20 = (bf16[128,768]{1,0:T(8,128)(2,1)S(1)}, bf16[128,768]{1,0:T(8,128)(2,1)S(1)}, u32[]{:S(2)}, u32[]{:S(2)}) collective-permute-start(bf16[128,768]{1,0:T(8,128)(2,1)S(1)} %collective-permute-done.10.refs_10_), channel_id=1, source_target_pairs={{0,12},{1,13},{2,14},{3,15},{4,0},{5,1},{6,2},{7,3},{8,4},{9,5},{1... | collective-permute-start | bytes 589832 | tf_op jit(solution)/shard_map/ppermute | solution.py:50
  14.0 6.2 %collective-permute-done.6.refs_6_ = bf16[128,768]{1,0:T(8,128)(2,1)S(1)} collective-permute-done((bf16[128,768]{1,0:T(8,128)(2,1)S(1)}, bf16[128,768]{1,0:T(8,128)(2,1)S(1)}, u32[]{:S(2)}, u32[]{:S(2)}) %collective-permute-start.6) | collective-permute-done | bytes 196640 | tf_op jit(solution)/shard_map/ppermute | solution.py:50
  20.2 3.0 %collective-permute-start.16 = (bf16[128,768]{1,0:T(8,128)(2,1)S(1)}, bf16[128,768]{1,0:T(8,128)(2,1)S(1)}, u32[]{:S(2)}, u32[]{:S(2)}) collective-permute-start(bf16[128,768]{1,0:T(8,128)(2,1)S(1)} %collective-permute-done.10.refs_10_), channel_id=1, source_target_pairs={{0,4},{1,5},{2,6},{3,7},{4,8},{5,9},{6,10},{7,11},{8,12},{9,13},{1... | collective-permute-start | bytes 589832 | tf_op jit(solution)/shard_map/ppermute | solution.py:50
  23.2 0.6 collective-permute-start.11
  23.8 0.1 collective-permute-start
  23.9 0.5 collective-permute-start.2
  24.4 0.2 collective-permute-done.7.refs_7_
  24.6 0.1 collective-permute-start.21
  24.7 0.4 collective-permute-done.refs_1_
  25.2 0.0 collective-permute-done.2.refs_3_
  25.2 2.0 %collective-permute-start.18 = (bf16[256,768]{1,0:T(8,128)(2,1)S(1)}, bf16[256,768]{1,0:T(8,128)(2,1)S(1)}, u32[]{:S(2)}, u32[]{:S(2)}) collective-permute-start(bf16[256,768]{1,0:T(8,128)(2,1)S(1)} %pad_maximum_fusion.2), channel_id=1, source_target_pairs={{0,16},{1,3},{2,18},{3,1},{4,20},{5,7},{6,22},{7,5},{8,24},{9,11},... | collective-permute-start | bytes 1179656 | tf_op jit(solution)/shard_map/ppermute | solution.py:50
  27.2 0.1 collective-permute-start.14
  27.3 2.0 %collective-permute-start.22 = (bf16[256,768]{1,0:T(8,128)(2,1)S(1)}, bf16[256,768]{1,0:T(8,128)(2,1)S(1)}, u32[]{:S(2)}, u32[]{:S(2)}) collective-permute-start(bf16[256,768]{1,0:T(8,128)(2,1)S(1)} %pad_maximum_fusion.3), channel_id=1, source_target_pairs={{0,16},{1,3},{2,18},{3,1},{4,20},{5,7},{6,22},{7,5},{8,24},{9,11},... | collective-permute-start | bytes 1179656 | tf_op jit(solution)/shard_map/ppermute | solution.py:50
  29.2 1.4 %collective-permute-done.17.refs_17_ = bf16[128,768]{1,0:T(8,128)(2,1)S(1)} collective-permute-done((bf16[128,768]{1,0:T(8,128)(2,1)S(1)}, bf16[128,768]{1,0:T(8,128)(2,1)S(1)}, u32[]{:S(2)}, u32[]{:S(2)}) %collective-permute-start.17) | collective-permute-done | bytes 196640 | tf_op jit(solution)/shard_map/ppermute | solution.py:50
  30.7 0.1 collective-permute-start.24
  30.8 2.2 %collective-permute-done.12.refs_12_ = bf16[256,768]{1,0:T(8,128)(2,1)S(1)} collective-permute-done((bf16[256,768]{1,0:T(8,128)(2,1)S(1)}, bf16[256,768]{1,0:T(8,128)(2,1)S(1)}, u32[]{:S(2)}, u32[]{:S(2)}) %collective-permute-start.12) | collective-permute-done | bytes 393248 | tf_op jit(solution)/shard_map/ppermute | solution.py:50
  33.0 6.3 %collective-permute-done.18.refs_18_ = bf16[256,768]{1,0:T(8,128)(2,1)S(1)} collective-permute-done((bf16[256,768]{1,0:T(8,128)(2,1)S(1)}, bf16[256,768]{1,0:T(8,128)(2,1)S(1)}, u32[]{:S(2)}, u32[]{:S(2)}) %collective-permute-start.18) | collective-permute-done | bytes 393248 | tf_op jit(solution)/shard_map/ppermute | solution.py:50
  39.3 4.2 %collective-permute-done.14.refs_14_ = bf16[256,768]{1,0:T(8,128)(2,1)S(1)} collective-permute-done((bf16[256,768]{1,0:T(8,128)(2,1)S(1)}, bf16[256,768]{1,0:T(8,128)(2,1)S(1)}, u32[]{:S(2)}, u32[]{:S(2)}) %collective-permute-start.14) | collective-permute-done | bytes 393248 | tf_op jit(solution)/shard_map/ppermute | solution.py:50
  43.5 4.2 %collective-permute-done.22.refs_22_ = bf16[256,768]{1,0:T(8,128)(2,1)S(1)} collective-permute-done((bf16[256,768]{1,0:T(8,128)(2,1)S(1)}, bf16[256,768]{1,0:T(8,128)(2,1)S(1)}, u32[]{:S(2)}, u32[]{:S(2)}) %collective-permute-start.22) | collective-permute-done | bytes 393248 | tf_op jit(solution)/shard_map/ppermute | solution.py:50
  47.7 1.6 %collective-permute-done.24.refs_24_ = bf16[128,768]{1,0:T(8,128)(2,1)S(1)} collective-permute-done((bf16[128,768]{1,0:T(8,128)(2,1)S(1)}, bf16[128,768]{1,0:T(8,128)(2,1)S(1)}, u32[]{:S(2)}, u32[]{:S(2)}) %collective-permute-start.24) | collective-permute-done | bytes 196640 | tf_op jit(solution)/shard_map/ppermute | solution.py:50
  49.3 0.9 %copy-done = s32[64,4,256]{2,1,0:T(4,128)S(1)} copy-done((s32[64,4,256]{2,1,0:T(4,128)S(1)}, s32[64,4,256]{2,1,0:T(4,128)}, u32[]{:S(2)}) %copy-start) | copy-done | bytes 262168
  50.2 0.7 %copy-done.1 = s32[4]{0:T(128)S(1)} copy-done((s32[4]{0:T(128)S(1)}, s32[4]{0:T(128)}, u32[]{:S(2)}) %copy-start.1) | copy-done | bytes 40
  50.9 4.7 %plan.1 = (s32[393]{0:T(512)S(1)}, f32[8,4096]{1,0:T(8,128)S(1)}) custom-call(s32[4]{0:T(128)S(1)} %copy-done.1, s32[4]{0:T(128)S(1)} %collective-permute-done.refs_1_, s32[4]{0:T(128)S(1)} %collective-permute-done.1.refs_2_, s32[4]{0:T(128)S(1)} %collective-permute-done.2.refs_3_, s32[64,4,256]{2,1,0:T(4,128)S(1)} %copy-done), custom_call_target="tpu_custom_call" | custom-call | tf_op jit(solution)/shard_map/plan/pallas_call | solution.py:243
  55.6 6.0 %spread.1 = f32[64,32,512]{2,1,0:T(8,128)} custom-call(s32[393]{0:T(512)S(1)} %get-tuple-element.7.refs_0_, f32[8,4096]{1,0:T(8,128)S(1)} %get-tuple-element.8.refs_1_, bf16[128,768]{1,0:T(8,128)(2,1)S(1)} %bitcast.6, bf16[128,768]{1,0:T(8,128)(2,1)S(1)} %collective-permute-done.3.refs_3_, bf16[128,768]{1,0:T(8,128)(2,1)S(1)} %collective-permute-done.4.refs_4_, ...), custom_call_target="tpu_custom_call" | custom-call | tf_op jit(solution)/shard_map/spread/pallas_call | solution.py:369
  (31 shorter events, 0.2 us)
Async XLA Ops:
  1.0 10.1 %collective-permute-start.4 = (bf16[128,768]{1,0:T(8,128)(2,1)S(1)}, bf16[128,768]{1,0:T(8,128)(2,1)S(1)}, u32[]{:S(2)}, u32[]{:S(2)}) collective-permute-start(bf16[128,768]{1,0:T(8,128)(2,1)S(1)} %bitcast.1), channel_id=1, source_target_pairs={{0,4},{1,5},{2,6},{3,7},{4,8},{5,9},{6,10},{7,11},{8,12},{9,13},{1... | collective-permute-start | bytes 589832 | tf_op jit(solution)/shard_map/ppermute | solution.py:50
  2.6 10.4 %collective-permute-start.10 = (bf16[128,768]{1,0:T(8,128)(2,1)S(1)}, bf16[128,768]{1,0:T(8,128)(2,1)S(1)}, u32[]{:S(2)}, u32[]{:S(2)}) collective-permute-start(bf16[128,768]{1,0:T(8,128)(2,1)S(1)} %bitcast.2), channel_id=1, source_target_pairs={{0,18},{1,19},{2,16},{3,17},{4,22},{5,23},{6,20},{7,21},{8,26},{9,... | collective-permute-start | bytes 589832 | tf_op jit(solution)/shard_map/ppermute | solution.py:50
  4.1 8.9 %collective-permute-start.8 = (bf16[128,768]{1,0:T(8,128)(2,1)S(1)}, bf16[128,768]{1,0:T(8,128)(2,1)S(1)}, u32[]{:S(2)}, u32[]{:S(2)}) collective-permute-start(bf16[128,768]{1,0:T(8,128)(2,1)S(1)} %bitcast.3), channel_id=1, source_target_pairs={{0,12},{1,13},{2,14},{3,15},{4,0},{5,1},{6,2},{7,3},{8,4},{9,5},{1... | collective-permute-start | bytes 589832 | tf_op jit(solution)/shard_map/ppermute | solution.py:50
  4.5 9.4 %collective-permute-start.3 = (bf16[128,768]{1,0:T(8,128)(2,1)S(1)}, bf16[128,768]{1,0:T(8,128)(2,1)S(1)}, u32[]{:S(2)}, u32[]{:S(2)}) collective-permute-start(bf16[128,768]{1,0:T(8,128)(2,1)S(1)} %bitcast.4), channel_id=1, source_target_pairs={{0,1},{1,0},{2,3},{3,2},{4,5},{5,4},{6,7},{7,6},{8,9},{9,8},{10,11... | collective-permute-start | bytes 589832 | tf_op jit(solution)/shard_map/ppermute | solution.py:50
  11.1 9.1 %collective-permute-start.6 = (bf16[128,768]{1,0:T(8,128)(2,1)S(1)}, bf16[128,768]{1,0:T(8,128)(2,1)S(1)}, u32[]{:S(2)}, u32[]{:S(2)}) collective-permute-start(bf16[128,768]{1,0:T(8,128)(2,1)S(1)} %collective-permute-done.4.refs_4_), channel_id=1, source_target_pairs={{0,4},{1,5},{2,6},{3,7},{4,8},{5,9},{6,10},{7,11},{8,12},{9,13},{1... | collective-permute-start | bytes 589832 | tf_op jit(solution)/shard_map/ppermute | solution.py:50
  13.0 10.2 %collective-permute-start.5 = (bf16[128,768]{1,0:T(8,128)(2,1)S(1)}, bf16[128,768]{1,0:T(8,128)(2,1)S(1)}, u32[]{:S(2)}, u32[]{:S(2)}) collective-permute-start(bf16[128,768]{1,0:T(8,128)(2,1)S(1)} %collective-permute-done.4.refs_4_), channel_id=1, source_target_pairs={{0,1},{1,0},{2,3},{3,2},{4,5},{5,4},{6,7},{7,6},{8,9},{9,8},{10,11... | collective-permute-start | bytes 589832 | tf_op jit(solution)/shard_map/ppermute | solution.py:50
  13.0 10.8 %collective-permute-start.1 = (s32[4]{0:T(128)}, s32[4]{0:T(128)S(1)}, u32[]{:S(2)}, u32[]{:S(2)}) collective-permute-start(s32[4]{0:T(128)} %refs_0_.1), channel_id=1, source_target_pairs={{0,16},{1,17},{2,18},{3,19},{4,20},{5,21},{6,22},{7,23},{8,24},{9,... | collective-permute-start | bytes 56 | tf_op jit(solution)/shard_map/ppermute | solution.py:50
  13.0 10.9 %collective-permute-start.20 = (bf16[128,768]{1,0:T(8,128)(2,1)S(1)}, bf16[128,768]{1,0:T(8,128)(2,1)S(1)}, u32[]{:S(2)}, u32[]{:S(2)}) collective-permute-start(bf16[128,768]{1,0:T(8,128)(2,1)S(1)} %collective-permute-done.10.refs_10_), channel_id=1, source_target_pairs={{0,12},{1,13},{2,14},{3,15},{4,0},{5,1},{6,2},{7,3},{8,4},{9,5},{1... | collective-permute-start | bytes 589832 | tf_op jit(solution)/shard_map/ppermute | solution.py:50
  13.9 9.2 %collective-permute-start.9 = (bf16[128,768]{1,0:T(8,128)(2,1)S(1)}, bf16[128,768]{1,0:T(8,128)(2,1)S(1)}, u32[]{:S(2)}, u32[]{:S(2)}) collective-permute-start(bf16[128,768]{1,0:T(8,128)(2,1)S(1)} %collective-permute-done.8.refs_8_), channel_id=1, source_target_pairs={{0,1},{1,0},{2,3},{3,2},{4,5},{5,4},{6,7},{7,6},{8,9},{9,8},{10,11... | collective-permute-start | bytes 589832 | tf_op jit(solution)/shard_map/ppermute | solution.py:50
  20.2 7.0 %collective-permute-start.16 = (bf16[128,768]{1,0:T(8,128)(2,1)S(1)}, bf16[128,768]{1,0:T(8,128)(2,1)S(1)}, u32[]{:S(2)}, u32[]{:S(2)}) collective-permute-start(bf16[128,768]{1,0:T(8,128)(2,1)S(1)} %collective-permute-done.10.refs_10_), channel_id=1, source_target_pairs={{0,4},{1,5},{2,6},{3,7},{4,8},{5,9},{6,10},{7,11},{8,12},{9,13},{1... | collective-permute-start | bytes 589832 | tf_op jit(solution)/shard_map/ppermute | solution.py:50
  23.1 1.4 %collective-permute-start.7 = (bf16[128,768]{1,0:T(8,128)(2,1)S(1)}, bf16[128,768]{1,0:T(8,128)(2,1)S(1)}, u32[]{:S(2)}, u32[]{:S(2)}) collective-permute-start(bf16[128,768]{1,0:T(8,128)(2,1)S(1)} %collective-permute-done.6.refs_6_), channel_id=1, source_target_pairs={{0,1},{1,0},{2,3},{3,2},{4,5},{5,4},{6,7},{7,6},{8,9},{9,8},{10,11... | collective-permute-start | bytes 589832 | tf_op jit(solution)/shard_map/ppermute | solution.py:50
  23.2 4.1 %collective-permute-start.11 = (bf16[128,768]{1,0:T(8,128)(2,1)S(1)}, bf16[128,768]{1,0:T(8,128)(2,1)S(1)}, u32[]{:S(2)}, u32[]{:S(2)}) collective-permute-start(bf16[128,768]{1,0:T(8,128)(2,1)S(1)} %collective-permute-done.10.refs_10_), channel_id=1, source_target_pairs={{0,1},{1,0},{2,3},{3,2},{4,5},{5,4},{6,7},{7,6},{8,9},{9,8},{10,11... | collective-permute-start | bytes 589832 | tf_op jit(solution)/shard_map/ppermute | solution.py:50
  23.8 1.4 %collective-permute-start = (s32[4]{0:T(128)}, s32[4]{0:T(128)S(1)}, u32[]{:S(2)}, u32[]{:S(2)}) collective-permute-start(s32[4]{0:T(128)} %refs_0_.1), channel_id=1, source_target_pairs={{0,1},{1,0},{2,3},{3,2},{4,5},{5,4},{6,7},{7,6},{8,9},{9,8},{10,11... | collective-permute-start | bytes 56 | tf_op jit(solution)/shard_map/ppermute | solution.py:50
  23.9 1.3 %collective-permute-start.2 = (s32[4]{0:T(128)S(1)}, s32[4]{0:T(128)S(1)}, u32[]{:S(2)}, u32[]{:S(2)}) collective-permute-start(s32[4]{0:T(128)S(1)} %collective-permute-done.1.refs_2_), channel_id=1, source_target_pairs={{0,1},{1,0},{2,3},{3,2},{4,5},{5,4},{6,7},{7,6},{8,9},{9,8},{10,11... | collective-permute-start | bytes 56 | tf_op jit(solution)/shard_map/ppermute | solution.py:50
  24.6 4.6 %collective-permute-start.21 = (bf16[128,768]{1,0:T(8,128)(2,1)S(1)}, bf16[128,768]{1,0:T(8,128)(2,1)S(1)}, u32[]{:S(2)}, u32[]{:S(2)}) collective-permute-start(bf16[128,768]{1,0:T(8,128)(2,1)S(1)} %collective-permute-done.20.refs_20_), channel_id=1, source_target_pairs={{0,1},{1,0},{2,3},{3,2},{4,5},{5,4},{6,7},{7,6},{8,9},{9,8},{10,11... | collective-permute-start | bytes 589832 | tf_op jit(solution)/shard_map/ppermute | solution.py:50
  25.2 7.8 %collective-permute-start.12 = (bf16[256,768]{1,0:T(8,128)(2,1)S(1)}, bf16[256,768]{1,0:T(8,128)(2,1)S(1)}, u32[]{:S(2)}, u32[]{:S(2)}) collective-permute-start(bf16[256,768]{1,0:T(8,128)(2,1)S(1)} %pad_maximum_fusion), channel_id=1, source_target_pairs={{0,16},{1,3},{2,18},{3,1},{4,20},{5,7},{6,22},{7,5},{8,24},{9,11},... | collective-permute-start | bytes 1179656 | tf_op jit(solution)/shard_map/ppermute | solution.py:50
  25.2 14.1 %collective-permute-start.18 = (bf16[256,768]{1,0:T(8,128)(2,1)S(1)}, bf16[256,768]{1,0:T(8,128)(2,1)S(1)}, u32[]{:S(2)}, u32[]{:S(2)}) collective-permute-start(bf16[256,768]{1,0:T(8,128)(2,1)S(1)} %pad_maximum_fusion.2), channel_id=1, source_target_pairs={{0,16},{1,3},{2,18},{3,1},{4,20},{5,7},{6,22},{7,5},{8,24},{9,11},... | collective-permute-start | bytes 1179656 | tf_op jit(solution)/shard_map/ppermute | solution.py:50
  27.2 16.3 %collective-permute-start.14 = (bf16[256,768]{1,0:T(8,128)(2,1)S(1)}, bf16[256,768]{1,0:T(8,128)(2,1)S(1)}, u32[]{:S(2)}, u32[]{:S(2)}) collective-permute-start(bf16[256,768]{1,0:T(8,128)(2,1)S(1)} %pad_maximum_fusion.1), channel_id=1, source_target_pairs={{0,16},{1,3},{2,18},{3,1},{4,20},{5,7},{6,22},{7,5},{8,24},{9,11},... | collective-permute-start | bytes 1179656 | tf_op jit(solution)/shard_map/ppermute | solution.py:50
  27.3 20.4 %collective-permute-start.22 = (bf16[256,768]{1,0:T(8,128)(2,1)S(1)}, bf16[256,768]{1,0:T(8,128)(2,1)S(1)}, u32[]{:S(2)}, u32[]{:S(2)}) collective-permute-start(bf16[256,768]{1,0:T(8,128)(2,1)S(1)} %pad_maximum_fusion.3), channel_id=1, source_target_pairs={{0,16},{1,3},{2,18},{3,1},{4,20},{5,7},{6,22},{7,5},{8,24},{9,11},... | collective-permute-start | bytes 1179656 | tf_op jit(solution)/shard_map/ppermute | solution.py:50
  29.2 1.4 %collective-permute-start.17 = (bf16[128,768]{1,0:T(8,128)(2,1)S(1)}, bf16[128,768]{1,0:T(8,128)(2,1)S(1)}, u32[]{:S(2)}, u32[]{:S(2)}) collective-permute-start(bf16[128,768]{1,0:T(8,128)(2,1)S(1)} %collective-permute-done.16.refs_16_), channel_id=1, source_target_pairs={{0,1},{1,0},{2,3},{3,2},{4,5},{5,4},{6,7},{7,6},{8,9},{9,8},{10,11... | collective-permute-start | bytes 589832 | tf_op jit(solution)/shard_map/ppermute | solution.py:50
  30.7 18.6 %collective-permute-start.24 = (bf16[128,768]{1,0:T(8,128)(2,1)S(1)}, bf16[128,768]{1,0:T(8,128)(2,1)S(1)}, u32[]{:S(2)}, u32[]{:S(2)}) collective-permute-start(bf16[128,768]{1,0:T(8,128)(2,1)S(1)} %collective-permute-done.6.refs_6_), channel_id=1, source_target_pairs={{0,18},{1,19},{2,16},{3,17},{4,22},{5,23},{6,20},{7,21},{8,26},{9,... | collective-permute-start | bytes 589832 | tf_op jit(solution)/shard_map/ppermute | solution.py:50
  33.0 22.6 %collective-permute-start.13 = (bf16[256,768]{1,0:T(8,128)(2,1)S(1)}, bf16[256,768]{1,0:T(8,128)(2,1)S(1)}, u32[]{:S(2)}, u32[]{:S(2)}) collective-permute-start(bf16[256,768]{1,0:T(8,128)(2,1)S(1)} %collective-permute-done.12.refs_12_), channel_id=1, source_target_pairs={{0,1},{1,0},{2,3},{3,2},{4,5},{5,4},{6,7},{7,6},{8,9},{9,8},{10,11... | collective-permute-start | bytes 1179656 | tf_op jit(solution)/shard_map/ppermute | solution.py:50
  39.3 16.3 %collective-permute-start.19 = (bf16[256,768]{1,0:T(8,128)(2,1)S(1)}, bf16[256,768]{1,0:T(8,128)(2,1)S(1)}, u32[]{:S(2)}, u32[]{:S(2)}) collective-permute-start(bf16[256,768]{1,0:T(8,128)(2,1)S(1)} %collective-permute-done.18.refs_18_), channel_id=1, source_target_pairs={{0,1},{1,0},{2,3},{3,2},{4,5},{5,4},{6,7},{7,6},{8,9},{9,8},{10,11... | collective-permute-start | bytes 1179656 | tf_op jit(solution)/shard_map/ppermute | solution.py:50
  43.5 12.1 %collective-permute-start.15 = (bf16[256,768]{1,0:T(8,128)(2,1)S(1)}, bf16[256,768]{1,0:T(8,128)(2,1)S(1)}, u32[]{:S(2)}, u32[]{:S(2)}) collective-permute-start(bf16[256,768]{1,0:T(8,128)(2,1)S(1)} %collective-permute-done.14.refs_14_), channel_id=1, source_target_pairs={{0,1},{1,0},{2,3},{3,2},{4,5},{5,4},{6,7},{7,6},{8,9},{9,8},{10,11... | collective-permute-start | bytes 1179656 | tf_op jit(solution)/shard_map/ppermute | solution.py:50
  47.7 7.9 %collective-permute-start.23 = (bf16[256,768]{1,0:T(8,128)(2,1)S(1)}, bf16[256,768]{1,0:T(8,128)(2,1)S(1)}, u32[]{:S(2)}, u32[]{:S(2)}) collective-permute-start(bf16[256,768]{1,0:T(8,128)(2,1)S(1)} %collective-permute-done.22.refs_22_), channel_id=1, source_target_pairs={{0,1},{1,0},{2,3},{3,2},{4,5},{5,4},{6,7},{7,6},{8,9},{9,8},{10,11... | collective-permute-start | bytes 1179656 | tf_op jit(solution)/shard_map/ppermute | solution.py:50
  49.3 6.3 %collective-permute-start.25 = (bf16[128,768]{1,0:T(8,128)(2,1)S(1)}, bf16[128,768]{1,0:T(8,128)(2,1)S(1)}, u32[]{:S(2)}, u32[]{:S(2)}) collective-permute-start(bf16[128,768]{1,0:T(8,128)(2,1)S(1)} %collective-permute-done.24.refs_24_), channel_id=1, source_target_pairs={{0,1},{1,0},{2,3},{3,2},{4,5},{5,4},{6,7},{7,6},{8,9},{9,8},{10,11... | collective-permute-start | bytes 589832 | tf_op jit(solution)/shard_map/ppermute | solution.py:50
  49.3 1.0 %copy-start = (s32[64,4,256]{2,1,0:T(4,128)S(1)}, s32[64,4,256]{2,1,0:T(4,128)}, u32[]{:S(2)}) copy-start(s32[64,4,256]{2,1,0:T(4,128)} %refs_4_.1) | copy-start | bytes 786436
  50.2 0.7 %copy-start.1 = (s32[4]{0:T(128)S(1)}, s32[4]{0:T(128)}, u32[]{:S(2)}) copy-start(s32[4]{0:T(128)} %refs_0_.1) | copy-start | bytes 52

commit v5 on v4

--- a/solution.py
+++ b/solution.py
@@ -95,7 +95,7 @@
     side2 = ports.send(chip_up2, "x|y")
     across2 = ports.send(up2, "xy")
     pieces = [own, core_own, up1, core_up1, up2, core_up2, down, core_down]
-    late = (across, side0, side1, across1, side3, across3, side2, across2)
+    late = (across, side0, side1, across1, side3, across3, across2, side2)
     for held in late:
         pieces += [held, ports.send(held, "core")]
     owners = np.stack([owner for _, owned in pieces for owner in owned], axis=-1)
@@ -262,49 +262,68 @@
     )(*orients, table)
 
 
-def spread(pieces, info, where, sizes):
+def copy_groups(info_ref, compact, piece_refs, first, segments, items):
+    for piece in piece_refs:
+        for start in range(0, piece.shape[0] // GROUP, items):
+            targets = [info_ref[first + item] for item in range(items)]
+            least = targets[0]
+            for target in targets[1:]:
+                least = jnp.minimum(least, target)
+
+            @pl.when(least < segments)
+            def _(targets=targets, piece=piece, start=start):
+                for item, target in enumerate(targets):
+                    rows = pl.ds(pl.multiple_of(target * GROUP, GROUP), GROUP)
+                    source = (start + item) * GROUP
+                    compact[rows, :] = piece[source : source + GROUP, :]
+
+            first += items
+
+
+def collect(pieces, info, segments, sizes):
+    batch, planes, columns = sizes[:3]
+    channels = 3 * columns
+
+    def kernel(*refs):
+        info_ref, piece_refs, compact = refs[0], refs[1:-1], refs[-1]
+        count = info_ref[info.shape[0] - 1]
+        tiles = (count + TILE // GROUP - 1) >> shift_of(TILE // GROUP)
+
+        def clear(item, carry):
+            target = pl.ds(pl.multiple_of(item * GROUP, GROUP), GROUP)
+            compact[target, :] = jnp.zeros((GROUP, channels), jnp.bfloat16)
+            return carry
+
+        lax.fori_loop(count, tiles * (TILE // GROUP), clear, 0)
+        copy_groups(info_ref, compact, piece_refs, 0, segments, batch * planes // GROUP)
+
+    smem, vmem = pl.BlockSpec(memory_space=pltpu.SMEM), pl.BlockSpec(memory_space=pltpu.VMEM)
+    return pl.pallas_call(
+        kernel,
+        out_shape=jax.ShapeDtypeStruct((segments * GROUP + GROUP, channels), jnp.bfloat16),
+        in_specs=[smem] + [vmem] * len(pieces),
+        out_specs=vmem,
+        compiler_params=pltpu.CompilerParams(vmem_limit_bytes=8 << 20),
+        name="collect",
+    )(info, *pieces)
+
+
+def spread(compact, pieces, info, where, segments, sizes):
     batch, planes, columns, count_x, row_block, _ = sizes
     pieces_n = len(pieces)
-    segments = sum(piece.shape[0] for piece in pieces) // GROUP
+    first_segment = segments - sum(piece.shape[0] for piece in pieces) // GROUP
     steps = count_x // row_block
     channels = 3 * columns
 
     def kernel(*refs):
         info_ref, where_ref = refs[:2]
-        piece_refs = refs[2 : 2 + pieces_n]
-        out_ref = refs[2 + pieces_n]
-        compact, total, staged, sems = refs[3 + pieces_n :]
+        piece_refs = refs[3 : 3 + pieces_n]
+        out_ref, compact, total, staged, sems = refs[3 + pieces_n :]
         first_x = (lax.axis_index("rep") * lax.axis_size("pix") + lax.axis_index("pix")) * count_x
         first_z = lax.axis_index("slab") * planes
         tiles_max = segments * GROUP // TILE
         counts_at = segments + steps * tiles_max
-        count = info_ref[counts_at + steps]
-        tiles = (count + TILE // GROUP - 1) >> shift_of(TILE // GROUP)
-
-        first = 0
-        for piece in piece_refs:
-            items = batch * planes // GROUP
-            for start in range(0, piece.shape[0] // GROUP, items):
-                targets = [info_ref[first + item] for item in range(items)]
-                least = targets[0]
-                for target in targets[1:]:
-                    least = jnp.minimum(least, target)
-
-                @pl.when(least < segments)
-                def _(targets=targets, piece=piece, start=start):
-                    for item, target in enumerate(targets):
-                        rows = pl.ds(pl.multiple_of(target * GROUP, GROUP), GROUP)
-                        source = (start + item) * GROUP
-                        compact[rows, :] = piece[source : source + GROUP, :]
-
-                first += items
-
-        def clear(item, carry):
-            target = pl.ds(pl.multiple_of(item * GROUP, GROUP), GROUP)
-            compact[target, :] = jnp.zeros((GROUP, channels), jnp.bfloat16)
-            return carry
-
-        lax.fori_loop(count, tiles * (TILE // GROUP), clear, 0)
+        copy_groups(info_ref, compact, piece_refs, first_segment, segments, batch * planes // GROUP)
 
         def out_copy(step, slot):
             rows = pl.ds(step * row_block, row_block)
@@ -368,18 +387,21 @@
     smem, vmem = pl.BlockSpec(memory_space=pltpu.SMEM), pl.BlockSpec(memory_space=pltpu.VMEM)
     return pl.pallas_call(
         kernel,
-        out_shape=jax.ShapeDtypeStruct((count_x, planes, 2 * columns), jnp.float32),
-        in_specs=[smem, vmem] + [vmem] * pieces_n,
-        out_specs=pl.BlockSpec(memory_space=pl.ANY),
+        out_shape=[
+            jax.ShapeDtypeStruct((count_x, planes, 2 * columns), jnp.float32),
+            jax.ShapeDtypeStruct(compact.shape, compact.dtype),
+        ],
+        in_specs=[smem, vmem, vmem] + [vmem] * pieces_n,
+        out_specs=[pl.BlockSpec(memory_space=pl.ANY), vmem],
+        input_output_aliases={2: 1},
         scratch_shapes=[
-            pltpu.VMEM((segments * GROUP + GROUP, channels), jnp.bfloat16),
             pltpu.VMEM((row_block * planes, channels), jnp.float32),
             pltpu.VMEM((4, row_block, planes, 2 * columns), jnp.float32),
             pltpu.SemaphoreType.DMA((4,)),
         ],
         compiler_params=pltpu.CompilerParams(vmem_limit_bytes=14 << 20),
         name="spread",
-    )(info, where, *pieces)
+    )(info, where, compact, *pieces)[0]
 
 
 def make_body(ports):
@@ -394,7 +416,9 @@
         info, where = make_plan(
             ports, orients, ports.distances(orient_owners), angle_table, ports.distances(owners), sizes
         )
-        return spread(pieces, info, where, sizes)
+        segments = owners.shape[-1] * (batch * planes // GROUP)
+        compact = collect(pieces[:-1], info, segments, sizes)
+        return spread(compact, pieces[-1:], info, where, segments, sizes)
 
     return body
 

time: 61.7 us -> 67.3 us (1.091); the launches traced: 61.6 us -> 66.4 us
  waiting for transfers between devices: 33.3 us -> 36.6 us
  starting transfers between devices: 14.9 us -> 15.9 us
    ppermute x26, waiting for transfers between devices: 33.3 us -> 36.6 us  [send(): value = lax.ppermute(value, ('rep', 'slab', 'pix'), self.pairs(port))]
    ppermute x26, starting transfers between devices: 14.9 us -> 15.9 us  [send(): value = lax.ppermute(value, ('rep', 'slab', 'pix'), self.pairs(port))]
    pallas_call x1 -> x2, Pallas kernels: 5.98 us -> 6.49 us  [the longest x1 5.11 us: spread(): pl.pallas_call(kernel, out_shape=[jax.ShapeDtypeStruct((count_x, planes,...]
  transfers between devices with their start and end apart: 26 -> 26, of which waited for: 10 -> 10; matrix products, arithmetic and copies ran while one was open for 0% -> 0% of each run, Pallas kernels for 8% -> 9%
where the time goes in v5:
time: 67.3 us; the launch traced here: 66.4 us
  waiting for transfers between devices  36.6 us (54%)
  starting transfers between devices  15.9 us (24%)
  Pallas kernels  11.2 us (17%)
  local copies, waits for them, and re-layouts  1.61 us (2%)
  other arithmetic  1.06 us (2%)
    ppermute x26, waiting for transfers between devices, send(): value = lax.ppermute(value, ('rep', 'slab', 'pix'), self.pairs(port))  36.6 us
    ppermute x26, starting transfers between devices, send(): value = lax.ppermute(value, ('rep', 'slab', 'pix'), self.pairs(port))  15.9 us
    pallas_call x1, Pallas kernels, spread(): pl.pallas_call(kernel, out_shape=[jax.ShapeDtypeStruct((count_x, planes,...  5.11 us
    pallas_call x1, Pallas kernels, make_plan(): pl.pallas_call(kernel, out_shape=[jax.ShapeDtypeStruct((info_size,), jnp....  4.66 us
    unnamed x4, local copies, waits for them, and re-layouts  1.61 us
    pallas_call x1, Pallas kernels, collect(): pl.pallas_call(kernel, out_shape=jax.ShapeDtypeStruct((segments * GROUP +...  1.38 us
  transfers between devices with their start and end apart: 26, of which 10 were waited for; matrix products, arithmetic and copies ran while one was open for 0% of the time, Pallas kernels for 9%

profile of v5, /device:TPU:18, one launch (start us, length us, event | category | flops | bytes accessed | tf_op | source)
XLA Modules:
  0.0 66.4 jit_solution(15545842480739271815)
XLA Ops:
  0.0 1.0 %pad_maximum_fusion.4 = bf16[4,32,768]{2,1,0:T(8,128)(2,1)S(1)} fusion(bf16[4,32,256]{2,1,0:T(8,128)(2,1)} %param.5, bf16[4,32,512]{2,1,0:T(8,128)(2,1)} %param.4), kind=kLoop, calls=%fused_computation.4 | loop fusion | flops 393216 | bytes 393216 | tf_op jit(solution)/shard_map/concatenate | solution.py:414
  1.0 1.6 %collective-permute-start.4 = (bf16[128,768]{1,0:T(8,128)(2,1)S(1)}, bf16[128,768]{1,0:T(8,128)(2,1)S(1)}, u32[]{:S(2)}, u32[]{:S(2)}) collective-permute-start(bf16[128,768]{1,0:T(8,128)(2,1)S(1)} %bitcast.1), channel_id=1, source_target_pairs={{0,4},{1,5},{2,6},{3,7},{4,8},{5,9},{6,10},{7,11},{8,12},{9,13},{1... | collective-permute-start | bytes 589832 | tf_op jit(solution)/shard_map/ppermute | solution.py:50
  2.6 1.5 %collective-permute-start.10 = (bf16[128,768]{1,0:T(8,128)(2,1)S(1)}, bf16[128,768]{1,0:T(8,128)(2,1)S(1)}, u32[]{:S(2)}, u32[]{:S(2)}) collective-permute-start(bf16[128,768]{1,0:T(8,128)(2,1)S(1)} %bitcast.2), channel_id=1, source_target_pairs={{0,18},{1,19},{2,16},{3,17},{4,22},{5,23},{6,20},{7,21},{8,26},{9,... | collective-permute-start | bytes 589832 | tf_op jit(solution)/shard_map/ppermute | solution.py:50
  4.1 0.4 collective-permute-start.8
  4.5 6.5 %collective-permute-done.4.refs_3_ = bf16[128,768]{1,0:T(8,128)(2,1)S(1)} collective-permute-done((bf16[128,768]{1,0:T(8,128)(2,1)S(1)}, bf16[128,768]{1,0:T(8,128)(2,1)S(1)}, u32[]{:S(2)}, u32[]{:S(2)}) %collective-permute-start.4) | collective-permute-done | bytes 196640 | tf_op jit(solution)/shard_map/ppermute | solution.py:50
  11.1 1.9 %collective-permute-start.6 = (bf16[128,768]{1,0:T(8,128)(2,1)S(1)}, bf16[128,768]{1,0:T(8,128)(2,1)S(1)}, u32[]{:S(2)}, u32[]{:S(2)}) collective-permute-start(bf16[128,768]{1,0:T(8,128)(2,1)S(1)} %collective-permute-done.4.refs_3_), channel_id=1, source_target_pairs={{0,4},{1,5},{2,6},{3,7},{4,8},{5,9},{6,10},{7,11},{8,12},{9,13},{1... | collective-permute-start | bytes 589832 | tf_op jit(solution)/shard_map/ppermute | solution.py:50
  13.0 0.5 collective-permute-start
  13.5 0.5 collective-permute-start.20
  14.0 6.2 %collective-permute-done.6.refs_5_ = bf16[128,768]{1,0:T(8,128)(2,1)S(1)} collective-permute-done((bf16[128,768]{1,0:T(8,128)(2,1)S(1)}, bf16[128,768]{1,0:T(8,128)(2,1)S(1)}, u32[]{:S(2)}, u32[]{:S(2)}) %collective-permute-start.6) | collective-permute-done | bytes 196640 | tf_op jit(solution)/shard_map/ppermute | solution.py:50
  20.1 3.0 %collective-permute-start.16 = (bf16[128,768]{1,0:T(8,128)(2,1)S(1)}, bf16[128,768]{1,0:T(8,128)(2,1)S(1)}, u32[]{:S(2)}, u32[]{:S(2)}) collective-permute-start(bf16[128,768]{1,0:T(8,128)(2,1)S(1)} %collective-permute-done.10.refs_9_), channel_id=1, source_target_pairs={{0,4},{1,5},{2,6},{3,7},{4,8},{5,9},{6,10},{7,11},{8,12},{9,13},{1... | collective-permute-start | bytes 589832 | tf_op jit(solution)/shard_map/ppermute | solution.py:50
  23.2 0.6 collective-permute-start.11
  23.8 0.1 collective-permute-start.1
  23.9 3.7 %collective-permute-done.1.refs_2_ = s32[4]{0:T(128)S(1)} collective-permute-done((s32[4]{0:T(128)}, s32[4]{0:T(128)S(1)}, u32[]{:S(2)}, u32[]{:S(2)}) %collective-permute-start.1) | collective-permute-done | bytes 48 | tf_op jit(solution)/shard_map/ppermute | solution.py:50
  27.5 1.2 %collective-permute-done.2.refs_3_ = s32[4]{0:T(128)S(1)} collective-permute-done((s32[4]{0:T(128)S(1)}, s32[4]{0:T(128)S(1)}, u32[]{:S(2)}, u32[]{:S(2)}) %collective-permute-start.2) | collective-permute-done | bytes 48 | tf_op jit(solution)/shard_map/ppermute | solution.py:50
  28.7 0.0 collective-permute-start.12
  28.7 2.0 %collective-permute-start.18 = (bf16[256,768]{1,0:T(8,128)(2,1)S(1)}, bf16[256,768]{1,0:T(8,128)(2,1)S(1)}, u32[]{:S(2)}, u32[]{:S(2)}) collective-permute-start(bf16[256,768]{1,0:T(8,128)(2,1)S(1)} %pad_maximum_fusion.2), channel_id=1, source_target_pairs={{0,16},{1,3},{2,18},{3,1},{4,20},{5,7},{6,22},{7,5},{8,24},{9,11},... | collective-permute-start | bytes 1179656 | tf_op jit(solution)/shard_map/ppermute | solution.py:50
  30.7 0.1 collective-permute-start.14
  30.8 0.1 collective-permute-start.21
  30.9 2.0 %collective-permute-start.24 = (bf16[256,768]{1,0:T(8,128)(2,1)S(1)}, bf16[256,768]{1,0:T(8,128)(2,1)S(1)}, u32[]{:S(2)}, u32[]{:S(2)}) collective-permute-start(bf16[256,768]{1,0:T(8,128)(2,1)S(1)} %pad_maximum_fusion.3), channel_id=1, source_target_pairs={{0,16},{1,3},{2,18},{3,1},{4,20},{5,7},{6,22},{7,5},{8,24},{9,11},... | collective-permute-start | bytes 1179656 | tf_op jit(solution)/shard_map/ppermute | solution.py:50
  32.9 0.1 collective-permute-start.17
  33.0 1.4 %collective-permute-done.17.refs_16_ = bf16[128,768]{1,0:T(8,128)(2,1)S(1)} collective-permute-done((bf16[128,768]{1,0:T(8,128)(2,1)S(1)}, bf16[128,768]{1,0:T(8,128)(2,1)S(1)}, u32[]{:S(2)}, u32[]{:S(2)}) %collective-permute-start.17) | collective-permute-done | bytes 196640 | tf_op jit(solution)/shard_map/ppermute | solution.py:50
  34.3 1.6 %collective-permute-start.22 = (bf16[128,768]{1,0:T(8,128)(2,1)S(1)}, bf16[128,768]{1,0:T(8,128)(2,1)S(1)}, u32[]{:S(2)}, u32[]{:S(2)}) collective-permute-start(bf16[128,768]{1,0:T(8,128)(2,1)S(1)} %collective-permute-done.6.refs_5_), channel_id=1, source_target_pairs={{0,18},{1,19},{2,16},{3,17},{4,22},{5,23},{6,20},{7,21},{8,26},{9,... | collective-permute-start | bytes 589832 | tf_op jit(solution)/shard_map/ppermute | solution.py:50
  35.9 0.6 collective-permute-done.12.refs_11_
  36.5 6.3 %collective-permute-done.18.refs_17_ = bf16[256,768]{1,0:T(8,128)(2,1)S(1)} collective-permute-done((bf16[256,768]{1,0:T(8,128)(2,1)S(1)}, bf16[256,768]{1,0:T(8,128)(2,1)S(1)}, u32[]{:S(2)}, u32[]{:S(2)}) %collective-permute-start.18) | collective-permute-done | bytes 393248 | tf_op jit(solution)/shard_map/ppermute | solution.py:50
  42.8 4.2 %collective-permute-done.14.refs_13_ = bf16[256,768]{1,0:T(8,128)(2,1)S(1)} collective-permute-done((bf16[256,768]{1,0:T(8,128)(2,1)S(1)}, bf16[256,768]{1,0:T(8,128)(2,1)S(1)}, u32[]{:S(2)}, u32[]{:S(2)}) %collective-permute-start.14) | collective-permute-done | bytes 393248 | tf_op jit(solution)/shard_map/ppermute | solution.py:50
  47.0 4.2 %collective-permute-done.24.refs_23_ = bf16[256,768]{1,0:T(8,128)(2,1)S(1)} collective-permute-done((bf16[256,768]{1,0:T(8,128)(2,1)S(1)}, bf16[256,768]{1,0:T(8,128)(2,1)S(1)}, u32[]{:S(2)}, u32[]{:S(2)}) %collective-permute-start.24) | collective-permute-done | bytes 393248 | tf_op jit(solution)/shard_map/ppermute | solution.py:50
  51.2 2.4 %collective-permute-done.22.refs_21_ = bf16[128,768]{1,0:T(8,128)(2,1)S(1)} collective-permute-done((bf16[128,768]{1,0:T(8,128)(2,1)S(1)}, bf16[128,768]{1,0:T(8,128)(2,1)S(1)}, u32[]{:S(2)}, u32[]{:S(2)}) %collective-permute-start.22) | collective-permute-done | bytes 196640 | tf_op jit(solution)/shard_map/ppermute | solution.py:50
  53.6 0.9 %copy-done = s32[64,4,256]{2,1,0:T(4,128)S(1)} copy-done((s32[64,4,256]{2,1,0:T(4,128)S(1)}, s32[64,4,256]{2,1,0:T(4,128)}, u32[]{:S(2)}) %copy-start) | copy-done | bytes 262168
  54.5 0.7 copy-done.1
  55.2 4.7 %plan.1 = (s32[393]{0:T(512)S(1)}, f32[8,4096]{1,0:T(8,128)S(1)}) custom-call(s32[4]{0:T(128)S(1)} %copy-done.1, s32[4]{0:T(128)S(1)} %collective-permute-done.refs_1_, s32[4]{0:T(128)S(1)} %collective-permute-done.1.refs_2_, s32[4]{0:T(128)S(1)} %collective-permute-done.2.refs_3_, s32[64,4,256]{2,1,0:T(4,128)S(1)} %copy-done), custom_call_target="tpu_custom_call" | custom-call | tf_op jit(solution)/shard_map/plan/pallas_call | solution.py:243
  59.9 1.4 %collect.1.refs_2_ = bf16[4112,768]{1,0:T(8,128)(2,1)S(1)} custom-call(s32[393]{0:T(512)S(1)} %get-tuple-element.8.refs_0_, bf16[128,768]{1,0:T(8,128)(2,1)S(1)} %bitcast.6, bf16[128,768]{1,0:T(8,128)(2,1)S(1)} %collective-permute-done.3.refs_2_, bf16[128,768]{1,0:T(8,128)(2,1)S(1)} %collective-permute-done.4.refs_3_, ...), custom_call_target="tpu_custom_call" | custom-call | tf_op jit(solution)/shard_map/collect/pallas_call | solution.py:301
  61.3 5.1 %spread.1 = (f32[64,32,512]{2,1,0:T(8,128)}, bf16[4112,768]{1,0:T(8,128)(2,1)S(1)}) custom-call(s32[393]{0:T(512)S(1)} %get-tuple-element.8.refs_0_, f32[8,4096]{1,0:T(8,128)S(1)} %get-tuple-element.9.refs_1_, bf16[4112,768]{1,0:T(8,128)(2,1)S(1)} %collect.1.refs_2_, ...), custom_call_target="tpu_custom_call", output_to_operand_aliasing={{1}: (2, {})} | custom-call | tf_op jit(solution)/shard_map/spread/pallas_call | solution.py:388
  (32 shorter events, 0.2 us)
Async XLA Ops:
  1.0 10.1 %collective-permute-start.4 = (bf16[128,768]{1,0:T(8,128)(2,1)S(1)}, bf16[128,768]{1,0:T(8,128)(2,1)S(1)}, u32[]{:S(2)}, u32[]{:S(2)}) collective-permute-start(bf16[128,768]{1,0:T(8,128)(2,1)S(1)} %bitcast.1), channel_id=1, source_target_pairs={{0,4},{1,5},{2,6},{3,7},{4,8},{5,9},{6,10},{7,11},{8,12},{9,13},{1... | collective-permute-start | bytes 589832 | tf_op jit(solution)/shard_map/ppermute | solution.py:50
  2.6 10.4 %collective-permute-start.10 = (bf16[128,768]{1,0:T(8,128)(2,1)S(1)}, bf16[128,768]{1,0:T(8,128)(2,1)S(1)}, u32[]{:S(2)}, u32[]{:S(2)}) collective-permute-start(bf16[128,768]{1,0:T(8,128)(2,1)S(1)} %bitcast.2), channel_id=1, source_target_pairs={{0,18},{1,19},{2,16},{3,17},{4,22},{5,23},{6,20},{7,21},{8,26},{9,... | collective-permute-start | bytes 589832 | tf_op jit(solution)/shard_map/ppermute | solution.py:50
  4.1 9.4 %collective-permute-start.8 = (bf16[128,768]{1,0:T(8,128)(2,1)S(1)}, bf16[128,768]{1,0:T(8,128)(2,1)S(1)}, u32[]{:S(2)}, u32[]{:S(2)}) collective-permute-start(bf16[128,768]{1,0:T(8,128)(2,1)S(1)} %bitcast.3), channel_id=1, source_target_pairs={{0,12},{1,13},{2,14},{3,15},{4,0},{5,1},{6,2},{7,3},{8,4},{9,5},{1... | collective-permute-start | bytes 589832 | tf_op jit(solution)/shard_map/ppermute | solution.py:50
  4.5 9.4 %collective-permute-start.3 = (bf16[128,768]{1,0:T(8,128)(2,1)S(1)}, bf16[128,768]{1,0:T(8,128)(2,1)S(1)}, u32[]{:S(2)}, u32[]{:S(2)}) collective-permute-start(bf16[128,768]{1,0:T(8,128)(2,1)S(1)} %bitcast.4), channel_id=1, source_target_pairs={{0,1},{1,0},{2,3},{3,2},{4,5},{5,4},{6,7},{7,6},{8,9},{9,8},{10,11... | collective-permute-start | bytes 589832 | tf_op jit(solution)/shard_map/ppermute | solution.py:50
  11.1 9.1 %collective-permute-start.6 = (bf16[128,768]{1,0:T(8,128)(2,1)S(1)}, bf16[128,768]{1,0:T(8,128)(2,1)S(1)}, u32[]{:S(2)}, u32[]{:S(2)}) collective-permute-start(bf16[128,768]{1,0:T(8,128)(2,1)S(1)} %collective-permute-done.4.refs_3_), channel_id=1, source_target_pairs={{0,4},{1,5},{2,6},{3,7},{4,8},{5,9},{6,10},{7,11},{8,12},{9,13},{1... | collective-permute-start | bytes 589832 | tf_op jit(solution)/shard_map/ppermute | solution.py:50
  13.0 10.2 %collective-permute-start.5 = (bf16[128,768]{1,0:T(8,128)(2,1)S(1)}, bf16[128,768]{1,0:T(8,128)(2,1)S(1)}, u32[]{:S(2)}, u32[]{:S(2)}) collective-permute-start(bf16[128,768]{1,0:T(8,128)(2,1)S(1)} %collective-permute-done.4.refs_3_), channel_id=1, source_target_pairs={{0,1},{1,0},{2,3},{3,2},{4,5},{5,4},{6,7},{7,6},{8,9},{9,8},{10,11... | collective-permute-start | bytes 589832 | tf_op jit(solution)/shard_map/ppermute | solution.py:50
  13.0 10.8 %collective-permute-start = (s32[4]{0:T(128)}, s32[4]{0:T(128)S(1)}, u32[]{:S(2)}, u32[]{:S(2)}) collective-permute-start(s32[4]{0:T(128)} %refs_0_.1), channel_id=1, source_target_pairs={{0,1},{1,0},{2,3},{3,2},{4,5},{5,4},{6,7},{7,6},{8,9},{9,8},{10,11... | collective-permute-start | bytes 56 | tf_op jit(solution)/shard_map/ppermute | solution.py:50
  13.5 15.2 %collective-permute-start.20 = (bf16[128,768]{1,0:T(8,128)(2,1)S(1)}, bf16[128,768]{1,0:T(8,128)(2,1)S(1)}, u32[]{:S(2)}, u32[]{:S(2)}) collective-permute-start(bf16[128,768]{1,0:T(8,128)(2,1)S(1)} %collective-permute-done.10.refs_9_), channel_id=1, source_target_pairs={{0,12},{1,13},{2,14},{3,15},{4,0},{5,1},{6,2},{7,3},{8,4},{9,5},{1... | collective-permute-start | bytes 589832 | tf_op jit(solution)/shard_map/ppermute | solution.py:50
  13.9 9.2 %collective-permute-start.9 = (bf16[128,768]{1,0:T(8,128)(2,1)S(1)}, bf16[128,768]{1,0:T(8,128)(2,1)S(1)}, u32[]{:S(2)}, u32[]{:S(2)}) collective-permute-start(bf16[128,768]{1,0:T(8,128)(2,1)S(1)} %collective-permute-done.8.refs_7_), channel_id=1, source_target_pairs={{0,1},{1,0},{2,3},{3,2},{4,5},{5,4},{6,7},{7,6},{8,9},{9,8},{10,11... | collective-permute-start | bytes 589832 | tf_op jit(solution)/shard_map/ppermute | solution.py:50
  20.1 10.6 %collective-permute-start.16 = (bf16[128,768]{1,0:T(8,128)(2,1)S(1)}, bf16[128,768]{1,0:T(8,128)(2,1)S(1)}, u32[]{:S(2)}, u32[]{:S(2)}) collective-permute-start(bf16[128,768]{1,0:T(8,128)(2,1)S(1)} %collective-permute-done.10.refs_9_), channel_id=1, source_target_pairs={{0,4},{1,5},{2,6},{3,7},{4,8},{5,9},{6,10},{7,11},{8,12},{9,13},{1... | collective-permute-start | bytes 589832 | tf_op jit(solution)/shard_map/ppermute | solution.py:50
  23.1 7.7 %collective-permute-start.7 = (bf16[128,768]{1,0:T(8,128)(2,1)S(1)}, bf16[128,768]{1,0:T(8,128)(2,1)S(1)}, u32[]{:S(2)}, u32[]{:S(2)}) collective-permute-start(bf16[128,768]{1,0:T(8,128)(2,1)S(1)} %collective-permute-done.6.refs_5_), channel_id=1, source_target_pairs={{0,1},{1,0},{2,3},{3,2},{4,5},{5,4},{6,7},{7,6},{8,9},{9,8},{10,11... | collective-permute-start | bytes 589832 | tf_op jit(solution)/shard_map/ppermute | solution.py:50
  23.2 7.8 %collective-permute-start.11 = (bf16[128,768]{1,0:T(8,128)(2,1)S(1)}, bf16[128,768]{1,0:T(8,128)(2,1)S(1)}, u32[]{:S(2)}, u32[]{:S(2)}) collective-permute-start(bf16[128,768]{1,0:T(8,128)(2,1)S(1)} %collective-permute-done.10.refs_9_), channel_id=1, source_target_pairs={{0,1},{1,0},{2,3},{3,2},{4,5},{5,4},{6,7},{7,6},{8,9},{9,8},{10,11... | collective-permute-start | bytes 589832 | tf_op jit(solution)/shard_map/ppermute | solution.py:50
  23.8 3.8 %collective-permute-start.1 = (s32[4]{0:T(128)}, s32[4]{0:T(128)S(1)}, u32[]{:S(2)}, u32[]{:S(2)}) collective-permute-start(s32[4]{0:T(128)} %refs_0_.1), channel_id=1, source_target_pairs={{0,16},{1,17},{2,18},{3,19},{4,20},{5,21},{6,22},{7,23},{8,24},{9,... | collective-permute-start | bytes 56 | tf_op jit(solution)/shard_map/ppermute | solution.py:50
  27.5 1.2 %collective-permute-start.2 = (s32[4]{0:T(128)S(1)}, s32[4]{0:T(128)S(1)}, u32[]{:S(2)}, u32[]{:S(2)}) collective-permute-start(s32[4]{0:T(128)S(1)} %collective-permute-done.1.refs_2_), channel_id=1, source_target_pairs={{0,1},{1,0},{2,3},{3,2},{4,5},{5,4},{6,7},{7,6},{8,9},{9,8},{10,11... | collective-permute-start | bytes 56 | tf_op jit(solution)/shard_map/ppermute | solution.py:50
  28.7 7.8 %collective-permute-start.12 = (bf16[256,768]{1,0:T(8,128)(2,1)S(1)}, bf16[256,768]{1,0:T(8,128)(2,1)S(1)}, u32[]{:S(2)}, u32[]{:S(2)}) collective-permute-start(bf16[256,768]{1,0:T(8,128)(2,1)S(1)} %pad_maximum_fusion), channel_id=1, source_target_pairs={{0,16},{1,3},{2,18},{3,1},{4,20},{5,7},{6,22},{7,5},{8,24},{9,11},... | collective-permute-start | bytes 1179656 | tf_op jit(solution)/shard_map/ppermute | solution.py:50
  28.7 14.1 %collective-permute-start.18 = (bf16[256,768]{1,0:T(8,128)(2,1)S(1)}, bf16[256,768]{1,0:T(8,128)(2,1)S(1)}, u32[]{:S(2)}, u32[]{:S(2)}) collective-permute-start(bf16[256,768]{1,0:T(8,128)(2,1)S(1)} %pad_maximum_fusion.2), channel_id=1, source_target_pairs={{0,16},{1,3},{2,18},{3,1},{4,20},{5,7},{6,22},{7,5},{8,24},{9,11},... | collective-permute-start | bytes 1179656 | tf_op jit(solution)/shard_map/ppermute | solution.py:50
  30.7 16.3 %collective-permute-start.14 = (bf16[256,768]{1,0:T(8,128)(2,1)S(1)}, bf16[256,768]{1,0:T(8,128)(2,1)S(1)}, u32[]{:S(2)}, u32[]{:S(2)}) collective-permute-start(bf16[256,768]{1,0:T(8,128)(2,1)S(1)} %pad_maximum_fusion.1), channel_id=1, source_target_pairs={{0,16},{1,3},{2,18},{3,1},{4,20},{5,7},{6,22},{7,5},{8,24},{9,11},... | collective-permute-start | bytes 1179656 | tf_op jit(solution)/shard_map/ppermute | solution.py:50
  30.8 2.1 %collective-permute-start.21 = (bf16[128,768]{1,0:T(8,128)(2,1)S(1)}, bf16[128,768]{1,0:T(8,128)(2,1)S(1)}, u32[]{:S(2)}, u32[]{:S(2)}) collective-permute-start(bf16[128,768]{1,0:T(8,128)(2,1)S(1)} %collective-permute-done.20.refs_19_), channel_id=1, source_target_pairs={{0,1},{1,0},{2,3},{3,2},{4,5},{5,4},{6,7},{7,6},{8,9},{9,8},{10,11... | collective-permute-start | bytes 589832 | tf_op jit(solution)/shard_map/ppermute | solution.py:50
  30.9 20.3 %collective-permute-start.24 = (bf16[256,768]{1,0:T(8,128)(2,1)S(1)}, bf16[256,768]{1,0:T(8,128)(2,1)S(1)}, u32[]{:S(2)}, u32[]{:S(2)}) collective-permute-start(bf16[256,768]{1,0:T(8,128)(2,1)S(1)} %pad_maximum_fusion.3), channel_id=1, source_target_pairs={{0,16},{1,3},{2,18},{3,1},{4,20},{5,7},{6,22},{7,5},{8,24},{9,11},... | collective-permute-start | bytes 1179656 | tf_op jit(solution)/shard_map/ppermute | solution.py:50
  32.9 1.4 %collective-permute-start.17 = (bf16[128,768]{1,0:T(8,128)(2,1)S(1)}, bf16[128,768]{1,0:T(8,128)(2,1)S(1)}, u32[]{:S(2)}, u32[]{:S(2)}) collective-permute-start(bf16[128,768]{1,0:T(8,128)(2,1)S(1)} %collective-permute-done.16.refs_15_), channel_id=1, source_target_pairs={{0,1},{1,0},{2,3},{3,2},{4,5},{5,4},{6,7},{7,6},{8,9},{9,8},{10,11... | collective-permute-start | bytes 589832 | tf_op jit(solution)/shard_map/ppermute | solution.py:50
  34.3 19.3 %collective-permute-start.22 = (bf16[128,768]{1,0:T(8,128)(2,1)S(1)}, bf16[128,768]{1,0:T(8,128)(2,1)S(1)}, u32[]{:S(2)}, u32[]{:S(2)}) collective-permute-start(bf16[128,768]{1,0:T(8,128)(2,1)S(1)} %collective-permute-done.6.refs_5_), channel_id=1, source_target_pairs={{0,18},{1,19},{2,16},{3,17},{4,22},{5,23},{6,20},{7,21},{8,26},{9,... | collective-permute-start | bytes 589832 | tf_op jit(solution)/shard_map/ppermute | solution.py:50
  36.5 23.4 %collective-permute-start.13 = (bf16[256,768]{1,0:T(8,128)(2,1)S(1)}, bf16[256,768]{1,0:T(8,128)(2,1)S(1)}, u32[]{:S(2)}, u32[]{:S(2)}) collective-permute-start(bf16[256,768]{1,0:T(8,128)(2,1)S(1)} %collective-permute-done.12.refs_11_), channel_id=1, source_target_pairs={{0,1},{1,0},{2,3},{3,2},{4,5},{5,4},{6,7},{7,6},{8,9},{9,8},{10,11... | collective-permute-start | bytes 1179656 | tf_op jit(solution)/shard_map/ppermute | solution.py:50
  42.8 17.1 %collective-permute-start.19 = (bf16[256,768]{1,0:T(8,128)(2,1)S(1)}, bf16[256,768]{1,0:T(8,128)(2,1)S(1)}, u32[]{:S(2)}, u32[]{:S(2)}) collective-permute-start(bf16[256,768]{1,0:T(8,128)(2,1)S(1)} %collective-permute-done.18.refs_17_), channel_id=1, source_target_pairs={{0,1},{1,0},{2,3},{3,2},{4,5},{5,4},{6,7},{7,6},{8,9},{9,8},{10,11... | collective-permute-start | bytes 1179656 | tf_op jit(solution)/shard_map/ppermute | solution.py:50
  47.0 12.9 %collective-permute-start.15 = (bf16[256,768]{1,0:T(8,128)(2,1)S(1)}, bf16[256,768]{1,0:T(8,128)(2,1)S(1)}, u32[]{:S(2)}, u32[]{:S(2)}) collective-permute-start(bf16[256,768]{1,0:T(8,128)(2,1)S(1)} %collective-permute-done.14.refs_13_), channel_id=1, source_target_pairs={{0,1},{1,0},{2,3},{3,2},{4,5},{5,4},{6,7},{7,6},{8,9},{9,8},{10,11... | collective-permute-start | bytes 1179656 | tf_op jit(solution)/shard_map/ppermute | solution.py:50
  51.2 10.1 %collective-permute-start.25 = (bf16[256,768]{1,0:T(8,128)(2,1)S(1)}, bf16[256,768]{1,0:T(8,128)(2,1)S(1)}, u32[]{:S(2)}, u32[]{:S(2)}) collective-permute-start(bf16[256,768]{1,0:T(8,128)(2,1)S(1)} %collective-permute-done.24.refs_23_), channel_id=1, source_target_pairs={{0,1},{1,0},{2,3},{3,2},{4,5},{5,4},{6,7},{7,6},{8,9},{9,8},{10,11... | collective-permute-start | bytes 1179656 | tf_op jit(solution)/shard_map/ppermute | solution.py:50
  53.6 6.3 %collective-permute-start.23 = (bf16[128,768]{1,0:T(8,128)(2,1)S(1)}, bf16[128,768]{1,0:T(8,128)(2,1)S(1)}, u32[]{:S(2)}, u32[]{:S(2)}) collective-permute-start(bf16[128,768]{1,0:T(8,128)(2,1)S(1)} %collective-permute-done.22.refs_21_), channel_id=1, source_target_pairs={{0,1},{1,0},{2,3},{3,2},{4,5},{5,4},{6,7},{7,6},{8,9},{9,8},{10,11... | collective-permute-start | bytes 589832 | tf_op jit(solution)/shard_map/ppermute | solution.py:50
  53.6 1.0 %copy-start = (s32[64,4,256]{2,1,0:T(4,128)S(1)}, s32[64,4,256]{2,1,0:T(4,128)}, u32[]{:S(2)}) copy-start(s32[64,4,256]{2,1,0:T(4,128)} %refs_4_.1) | copy-start | bytes 786436
  54.5 0.7 copy-start.1
